TPU v7x, 32 devices: a 4x4x1 block of a 4x4x8 slice. The times are simulated.
32 devices in a mesh: dp: 1 (over z), tp: 32 (over y, x, core).
Axes of the slice: x: 4, y: 4, z: 1, core: 2. Of those that a mesh axis runs over, the one named last changes fastest.
The devices are a block of a 4x4x8 slice.
Arguments:
- x_in: bfloat16 [1, 2048, 2048], P('dp', 'tp')
- y_grad: bfloat16 [1, 2048, 2048], P('dp', 'tp')
- ln_par: float32 [2, 4, 2048], replicated
- bias_d: float32 [2, 2, 2048], replicated
- w_qkv: bfloat16 [2, 2048, 3, 32, 64], P(None, None, None, 'tp')
- w_out: bfloat16 [2, 32, 64, 2048], P(None, 'tp')
- w_up: bfloat16 [2, 2048, 8192], P(None, None, 'tp')
- b_up: float32 [2, 8192], P(None, 'tp')
- w_down: bfloat16 [2, 8192, 2048], P(None, 'tp')
Outputs:
- output 1: bfloat16 [1, 2048, 2048], P('dp', 'tp')
- output 2: bfloat16 [1, 2048, 2048], P('dp', 'tp')
- output 3: float32 [2, 4, 2048], P('dp')
- output 4: float32 [2, 2, 2048], P('dp')
- output 5: bfloat16 [2, 2048, 3, 32, 64], P('dp', None, None, 'tp')
- output 6: bfloat16 [2, 32, 64, 2048], P('dp', 'tp')
- output 7: bfloat16 [2, 2048, 8192], P('dp', None, 'tp')
- output 8: float32 [2, 8192], P('dp', 'tp')
- output 9: bfloat16 [2, 8192, 2048], P('dp', 'tp')
All inputs are finite; a program needn't handle non-finite values.
Results may differ from a plain program's by a relative error of at most 0.02.
Values are sent between devices in bfloat16 or wider.
A program may use at most 768 MiB of HBM per device.

v0:
```python
import jax
import jax.numpy as jnp
from jax import lax
from jax.sharding import PartitionSpec as P


def layer_norm(row_vals, ln_gain, ln_shift):
    mean_val = jnp.mean(row_vals, axis=-1, keepdims=True)
    centered = row_vals - mean_val
    var_val = jnp.mean(centered * centered, axis=-1, keepdims=True)
    return centered * lax.rsqrt(var_val + 1e-5) * ln_gain + ln_shift


def gelu_tanh(pre_act):
    return jax.nn.gelu(pre_act, approximate=True)


def gather_rows(local_vals):
    return lax.all_gather(local_vals, 'tp', axis=1, tiled=True)


def scatter_rows(partial_vals, group_size):
    n_batch, seq_len, width = partial_vals.shape
    sent = partial_vals.astype(jnp.bfloat16).reshape(n_batch, group_size, seq_len // group_size, width)
    received = lax.all_to_all(sent, 'tp', 1, 1, tiled=True)
    return jnp.sum(received, axis=1, dtype=jnp.float32)


def causal_attention(q_vals, k_vals, v_vals):
    seq_len = q_vals.shape[1]
    score_scale = q_vals.shape[-1] ** -0.5
    scores = jnp.einsum('bqhe,bkhe->bhqk', q_vals, k_vals, preferred_element_type=jnp.float32) * score_scale
    positions = jnp.arange(seq_len)
    causal = positions[:, None] >= positions[None, :]
    scores = jnp.where(causal, scores, -1e30)
    prob_bf = jax.nn.softmax(scores, axis=-1).astype(jnp.bfloat16)
    attn_vals = jnp.einsum('bhqk,bkhe->bqhe', prob_bf, v_vals, preferred_element_type=jnp.float32).astype(jnp.bfloat16)
    return attn_vals, prob_bf


def attention_backward(d_attn, q_vals, k_vals, v_vals, prob_bf):
    score_scale = q_vals.shape[-1] ** -0.5
    d_prob = jnp.einsum('bqhe,bkhe->bhqk', d_attn, v_vals, preferred_element_type=jnp.float32)
    d_v = jnp.einsum('bhqk,bqhe->bkhe', prob_bf, d_attn, preferred_element_type=jnp.float32)
    row_dot = jnp.sum(d_prob * prob_bf, axis=-1, keepdims=True)
    d_score = (prob_bf * (d_prob - row_dot) * score_scale).astype(jnp.bfloat16)
    d_q = jnp.einsum('bhqk,bkhe->bqhe', d_score, k_vals, preferred_element_type=jnp.float32)
    d_k = jnp.einsum('bhqk,bqhe->bkhe', d_score, q_vals, preferred_element_type=jnp.float32)
    return d_q, d_k, d_v


def solution(mesh):
    group_size = mesh.shape['tp']

    def device_step(x_loc, dy_loc, ln_par, bias_d, w_qkv, w_out, w_up, b_up, w_down):
        n_layers = ln_par.shape[0]
        residual = x_loc.astype(jnp.float32)
        saved = []
        for layer_idx in range(n_layers):
            ln_vals = ln_par[layer_idx]
            bias_vals = bias_d[layer_idx]
            w_proj = w_qkv[layer_idx]
            res_one = residual
            h_all = gather_rows(layer_norm(res_one, ln_vals[0], ln_vals[1]).astype(jnp.bfloat16))
            q_vals = jnp.einsum('bsd,dhe->bshe', h_all, w_proj[:, 0], preferred_element_type=jnp.float32).astype(jnp.bfloat16)
            k_vals = jnp.einsum('bsd,dhe->bshe', h_all, w_proj[:, 1], preferred_element_type=jnp.float32).astype(jnp.bfloat16)
            v_vals = jnp.einsum('bsd,dhe->bshe', h_all, w_proj[:, 2], preferred_element_type=jnp.float32).astype(jnp.bfloat16)
            attn_vals, prob_bf = causal_attention(q_vals, k_vals, v_vals)
            attn_part = jnp.einsum('bshe,hed->bsd', attn_vals, w_out[layer_idx], preferred_element_type=jnp.float32)
            res_two = res_one + scatter_rows(attn_part, group_size) + bias_vals[0]
            h2_all = gather_rows(layer_norm(res_two, ln_vals[2], ln_vals[3]).astype(jnp.bfloat16))
            pre_act = jnp.einsum('bsd,df->bsf', h2_all, w_up[layer_idx], preferred_element_type=jnp.float32) + b_up[layer_idx]
            act_f, gelu_pull = jax.vjp(gelu_tanh, pre_act)
            act_vals = act_f.astype(jnp.bfloat16)
            mlp_part = jnp.einsum('bsf,fd->bsd', act_vals, w_down[layer_idx], preferred_element_type=jnp.float32)
            residual = res_two + scatter_rows(mlp_part, group_size) + bias_vals[1]
            saved.append((res_one, h_all, q_vals, k_vals, v_vals, prob_bf, attn_vals, res_two, h2_all, gelu_pull, act_vals))
        y_loc = residual.astype(jnp.bfloat16)

        d_res = dy_loc.astype(jnp.float32)
        layer_grads = [None] * n_layers
        for layer_idx in reversed(range(n_layers)):
            res_one, h_all, q_vals, k_vals, v_vals, prob_bf, attn_vals, res_two, h2_all, gelu_pull, act_vals = saved[layer_idx]
            ln_vals = ln_par[layer_idx]
            w_proj = w_qkv[layer_idx]
            d_bias_two = jnp.sum(d_res, axis=(0, 1))
            d_mlp_all = gather_rows(d_res.astype(jnp.bfloat16))
            d_wdown = jnp.einsum('bsf,bsd->fd', act_vals, d_mlp_all, preferred_element_type=jnp.float32)
            d_act = jnp.einsum('bsd,fd->bsf', d_mlp_all, w_down[layer_idx], preferred_element_type=jnp.float32)
            d_pre = gelu_pull(d_act)[0]
            d_bup = jnp.sum(d_pre, axis=(0, 1))
            d_pre_bf = d_pre.astype(jnp.bfloat16)
            d_wup = jnp.einsum('bsd,bsf->df', h2_all, d_pre_bf, preferred_element_type=jnp.float32)
            d_h2 = scatter_rows(jnp.einsum('bsf,df->bsd', d_pre_bf, w_up[layer_idx], preferred_element_type=jnp.float32), group_size)
            ln_pull = jax.vjp(layer_norm, res_two, ln_vals[2], ln_vals[3])[1]
            d_mid, d_gain_two, d_shift_two = ln_pull(d_h2)
            d_res = d_res + d_mid
            d_bias_one = jnp.sum(d_res, axis=(0, 1))
            d_attn_all = gather_rows(d_res.astype(jnp.bfloat16))
            d_wout = jnp.einsum('bshe,bsd->hed', attn_vals, d_attn_all, preferred_element_type=jnp.float32)
            d_attn = jnp.einsum('bsd,hed->bshe', d_attn_all, w_out[layer_idx], preferred_element_type=jnp.float32).astype(jnp.bfloat16)
            d_q, d_k, d_v = attention_backward(d_attn, q_vals, k_vals, v_vals, prob_bf)
            d_proj = [d_q.astype(jnp.bfloat16), d_k.astype(jnp.bfloat16), d_v.astype(jnp.bfloat16)]
            d_wqkv = jnp.stack([jnp.einsum('bsd,bshe->dhe', h_all, d_part, preferred_element_type=jnp.float32) for d_part in d_proj], axis=1)
            d_h_part = (jnp.einsum('bshe,dhe->bsd', d_proj[0], w_proj[:, 0], preferred_element_type=jnp.float32)
                        + jnp.einsum('bshe,dhe->bsd', d_proj[1], w_proj[:, 1], preferred_element_type=jnp.float32)
                        + jnp.einsum('bshe,dhe->bsd', d_proj[2], w_proj[:, 2], preferred_element_type=jnp.float32))
            d_h = scatter_rows(d_h_part, group_size)
            ln_pull = jax.vjp(layer_norm, res_one, ln_vals[0], ln_vals[1])[1]
            d_in, d_gain_one, d_shift_one = ln_pull(d_h)
            d_res = d_res + d_in
            layer_grads[layer_idx] = (jnp.stack([d_gain_one, d_shift_one, d_gain_two, d_shift_two]), jnp.stack([d_bias_one, d_bias_two]), d_wqkv, d_wout, d_wup, d_bup, d_wdown)
        small_grads = lax.psum((jnp.stack([grad_set[0] for grad_set in layer_grads]), jnp.stack([grad_set[1] for grad_set in layer_grads])), 'tp')
        return (y_loc, d_res.astype(jnp.bfloat16), small_grads[0], small_grads[1],
                jnp.stack([grad_set[2] for grad_set in layer_grads]).astype(jnp.bfloat16),
                jnp.stack([grad_set[3] for grad_set in layer_grads]).astype(jnp.bfloat16),
                jnp.stack([grad_set[4] for grad_set in layer_grads]).astype(jnp.bfloat16),
                jnp.stack([grad_set[5] for grad_set in layer_grads]),
                jnp.stack([grad_set[6] for grad_set in layer_grads]).astype(jnp.bfloat16))

    in_specs = (P('dp', 'tp', None), P('dp', 'tp', None), P(None, None, None), P(None, None, None),
                P(None, None, None, 'tp', None), P(None, 'tp', None, None), P(None, None, 'tp'), P(None, 'tp'), P(None, 'tp', None))
    out_specs = (P('dp', 'tp', None), P('dp', 'tp', None), P('dp', None, None), P('dp', None, None),
                 P('dp', None, None, 'tp', None), P('dp', 'tp', None, None), P('dp', None, 'tp'), P('dp', 'tp'), P('dp', 'tp', None))
    return jax.shard_map(device_step, mesh=mesh, in_specs=in_specs, out_specs=out_specs, check_vma=False)
```

profile of v0, /device:TPU:97, one launch (start us, length us, event | category | flops | bytes accessed | tf_op | source)
XLA Modules:
  0.0 1723.9 jit_solution(3867162743553716909)
XLA Ops:
  15.1 50.3 %all-gather.9.cloned.1.call-done = bf16[1,2048,2048]{2,1,0:T(8,128)(2,1)} async-done(((bf16[1,64,2048]{2,1,0:T(8,128)(2,1)}), bf16[1,2048,2048]{2,1,0:T(8,128)(2,1)}) %all-gather.9.cloned.1.call-update) | async-done | bytes 8388624 | tf_op jit(solution)/shard_map/all_gather | solution.py:19
  65.4 6.2 fusion.94
  93.8 5.6 convolution_convert_fusion.5
  104.4 103.8 %all-to-all-done = bf16[1,32,64,2048]{3,2,0,1:T(8,128)(2,1)} async-done(((bf16[1,32,64,2048]{3,2,0,1:T(8,128)(2,1)}), bf16[1,32,64,2048]{3,2,0,1:T(8,128)(2,1)}, u32[]{:S(2)}, u32[]{:S(2)}) %all-to-all-start) | async-done | bytes 8388640 | tf_op jit(solution)/shard_map/all_to_all | solution.py:25
  208.1 5.6 convert_reduce_fusion.11
  215.2 54.7 %all-gather.11.cloned.1.call-done = bf16[1,2048,2048]{2,1,0:T(8,128)(2,1)} async-done(((bf16[1,64,2048]{2,1,0:T(8,128)(2,1)}), bf16[1,2048,2048]{2,1,0:T(8,128)(2,1)}) %all-gather.11.cloned.1.call-update) | async-done | bytes 8388624 | tf_op jit(solution)/shard_map/all_gather | solution.py:19
  269.9 6.1 fusion.58
  278.7 106.5 %all_to_all.40 = bf16[1,32,64,2048]{3,2,0,1:T(8,128)(2,1)S(1)} all-to-all(bf16[1,32,64,2048]{3,2,0,1:T(8,128)(2,1)S(1)} %bitcast.453), channel_id=1, replica_groups=mesh['dp'=1,'tp'=32] {'tp'}, dimensions={1} | all-to-all | bytes 16777216 | tf_op jit(solution)/shard_map/all_to_all | solution.py:25
  388.9 46.2 %all-gather.13.cloned.1.call-done = bf16[1,2048,2048]{2,1,0:T(8,128)(2,1)} async-done(((bf16[1,64,2048]{2,1,0:T(8,128)(2,1)}), bf16[1,2048,2048]{2,1,0:T(8,128)(2,1)}) %all-gather.13.cloned.1.call-update) | async-done | bytes 8388624 | tf_op jit(solution)/shard_map/all_gather | solution.py:19
  435.1 6.2 fusion.109
  465.0 108.2 %all_to_all.41 = bf16[1,32,64,2048]{3,2,0,1:T(8,128)(2,1)S(1)} all-to-all(bf16[1,32,64,2048]{3,2,0,1:T(8,128)(2,1)S(1)} %bitcast.447), channel_id=1, replica_groups=mesh['dp'=1,'tp'=32] {'tp'}, dimensions={1} | all-to-all | bytes 16777216 | tf_op jit(solution)/shard_map/all_to_all | solution.py:25
  577.4 45.9 %all-gather.15.cloned.1.call-done = bf16[1,2048,2048]{2,1,0:T(8,128)(2,1)} async-done(((bf16[1,64,2048]{2,1,0:T(8,128)(2,1)}), bf16[1,2048,2048]{2,1,0:T(8,128)(2,1)}) %all-gather.15.cloned.1.call-update) | async-done | bytes 8388624 | tf_op jit(solution)/shard_map/all_gather | solution.py:19
  623.3 7.3 fusion.61
  630.6 41.5 %all-gather.17.cloned.1.call-done = bf16[1,2048,2048]{2,1,0:T(8,128)(2,1)} async-done(((bf16[1,64,2048]{2,1,0:T(8,128)(2,1)}), bf16[1,2048,2048]{2,1,0:T(8,128)(2,1)}) %all-gather.17.cloned.1.call-update) | async-done | bytes 8388624 | tf_op jit(solution)/shard_map/all_gather | solution.py:19
  672.1 8.7 fusion.256
  680.8 5.6 convolution_convert_fusion.1
  691.6 7.7 convolution_convert_fusion.2
  699.3 96.7 %all-to-all-done.4 = bf16[1,32,64,2048]{3,2,0,1:T(8,128)(2,1)} async-done(((bf16[1,32,64,2048]{3,2,0,1:T(8,128)(2,1)}), bf16[1,32,64,2048]{3,2,0,1:T(8,128)(2,1)}, u32[]{:S(2)}, u32[]{:S(2)}) %all-to-all-start.4) | async-done | bytes 8388640 | tf_op jit(solution)/shard_map/all_to_all | solution.py:25
  796.1 12.1 all-to-all-start.3
  808.3 6.3 convert_reduce_fusion.6
  815.4 97.4 %all-to-all-done.3 = bf16[1,32,64,2048]{3,2,0,1:T(8,128)(2,1)} async-done(((bf16[1,32,64,2048]{3,2,0,1:T(8,128)(2,1)}), bf16[1,32,64,2048]{3,2,0,1:T(8,128)(2,1)}, u32[]{:S(2)}, u32[]{:S(2)}) %all-to-all-start.3) | async-done | bytes 8388640 | tf_op jit(solution)/shard_map/all_to_all | solution.py:25
  912.8 5.6 convert_reduce_fusion.8
  921.0 54.5 %all-gather.19.cloned.1.call-done = bf16[1,2048,2048]{2,1,0:T(8,128)(2,1)} async-done(((bf16[1,64,2048]{2,1,0:T(8,128)(2,1)}), bf16[1,2048,2048]{2,1,0:T(8,128)(2,1)}) %all-gather.19.cloned.1.call-update) | async-done | bytes 8388624 | tf_op jit(solution)/shard_map/all_gather | solution.py:19
  975.5 6.0 fusion.124
  981.5 6.2 fusion.164
  987.8 11.9 fusion
  1000.3 9.6 fusion.2
  1014.2 8.1 fusion.230
  1022.3 8.1 fusion.229
  1030.4 15.4 add_convert_fusion.1
  1045.7 109.6 %all_to_all.42 = bf16[1,32,64,2048]{3,2,0,1:T(8,128)(2,1)S(1)} all-to-all(bf16[1,32,64,2048]{3,2,0,1:T(8,128)(2,1)} %bitcast.451), channel_id=1, replica_groups=mesh['dp'=1,'tp'=32] {'tp'}, dimensions={1} | all-to-all | bytes 16777216 | tf_op jit(solution)/shard_map/all_to_all | solution.py:25
  1160.6 46.9 %all-gather.21.cloned.1.call-done = bf16[1,2048,2048]{2,1,0:T(8,128)(2,1)} async-done(((bf16[1,64,2048]{2,1,0:T(8,128)(2,1)}), bf16[1,2048,2048]{2,1,0:T(8,128)(2,1)}) %all-gather.21.cloned.1.call-update) | async-done | bytes 8388624 | tf_op jit(solution)/shard_map/all_gather | solution.py:19
  1207.5 8.0 fusion.257
  1219.5 108.4 %all_to_all.43 = bf16[1,32,64,2048]{3,2,0,1:T(8,128)(2,1)S(1)} all-to-all(bf16[1,32,64,2048]{3,2,0,1:T(8,128)(2,1)S(1)} %bitcast.449), channel_id=1, replica_groups=mesh['dp'=1,'tp'=32] {'tp'}, dimensions={1} | all-to-all | bytes 16777216 | tf_op jit(solution)/shard_map/all_to_all | solution.py:25
  1331.8 7.1 fusion.82
  1338.9 39.4 %all-gather.23.cloned.1.call-done = bf16[1,2048,2048]{2,1,0:T(8,128)(2,1)} async-done(((bf16[1,64,2048]{2,1,0:T(8,128)(2,1)}), bf16[1,2048,2048]{2,1,0:T(8,128)(2,1)}) %all-gather.23.cloned.1.call-update) | async-done | bytes 8388624 | tf_op jit(solution)/shard_map/all_gather | solution.py:19
  1378.3 6.0 fusion.130
  1384.4 6.2 fusion.167
  1390.6 11.9 fusion.3
  1403.5 9.7 fusion.5
  1417.5 8.1 fusion.228
  1425.6 8.1 fusion.227
  1433.7 15.4 add_convert_fusion
  1453.8 6.5 fusion.79
  1484.3 117.2 %psum.15 = f32[2,2,2048]{2,1,0:T(2,128)} all-reduce(f32[2,2,2048]{2,1,0:T(2,128)S(1)} %pad_maximum_fusion.4), channel_id=1, replica_groups=mesh['dp'=1,'tp'=32] {'tp'}, use_global_device_ids=true, to_apply=%region_43.44 | all-reduce | flops 8192 | bytes 65536 | tf_op jit(solution)/shard_map/psum | solution.py:113
  1607.5 5.5 fusion.157
  1617.7 5.7 convert_reduce_fusion
  1625.9 89.6 %all-reduce.2.cloned.1.call-done = f32[2,4,2048]{2,1,0:T(4,128)} async-done(((f32[2,4,2048]{2,1,0:T(4,128)}), f32[2,4,2048]{2,1,0:T(4,128)}) %all-reduce.2.cloned.1.call-update) | async-done | bytes 65552 | tf_op jit(solution)/shard_map/psum | solution.py:113
  (289 shorter events, 144.8 us)
Async XLA Ops:
  7.2 58.2 %all-gather.9.cloned.1.call-start = ((), (), s32[]{:S(2)}) async-start(), calls=%async_computation.8 | async-start | bytes 8650752 | tf_op jit(solution)/shard_map/all_gather | solution.py:19
  8.4 65.9 %copy-start.50 = (f32[64]{0:T(128)}, f32[64]{0:T(128)S(1)}, u32[]{:S(2)}) copy-start(f32[64]{0:T(128)S(1)} %broadcast_multiply_fusion.3) | copy-start | bytes 772
  10.2 64.1 %copy-start.56 = (f32[64]{0:T(128)}, f32[64]{0:T(128)S(1)}, u32[]{:S(2)}) copy-start(f32[64]{0:T(128)S(1)} %fusion.235) | copy-start | bytes 772
  11.2 203.0 %copy-start.37 = (f32[1,1,2048]{2,1,0:T(1,128)}, f32[1,1,2048]{2,1,0:T(1,128)S(1)}, u32[]{:S(2)}) copy-start(f32[1,1,2048]{2,1,0:T(1,128)S(1)} %get-tuple-element.69) | copy-start | bytes 24580
  15.1 74.4 %copy-start.10 = (bf16[2048,3,1,64]{0,3,1,2:T(8,128)(2,1)}, bf16[2048,3,1,64]{0,3,1,2:T(8,128)(2,1)S(1)}, u32[]{:S(2)}) copy-start(bf16[2048,3,1,64]{0,3,1,2:T(8,128)(2,1)S(1)} %get-tuple-element.62) | copy-start | bytes 2359300
  99.4 108.7 %all-to-all-start = ((bf16[1,32,64,2048]{3,2,0,1:T(8,128)(2,1)}), bf16[1,32,64,2048]{3,2,0,1:T(8,128)(2,1)}, u32[]{:S(2)}, u32[]{:S(2)}) async-start(bf16[1,32,64,2048]{3,2,0,1:T(8,128)(2,1)} %bitcast.446), calls=%async_computation | async-start | bytes 16777216 | tf_op jit(solution)/shard_map/all_to_all | solution.py:25
  103.8 109.9 %copy-start.8 = (bf16[1,64,2048]{2,1,0:T(8,128)(2,1)S(1)}, bf16[1,64,2048]{2,1,0:T(8,128)(2,1)}, u32[]{:S(2)}) copy-start(bf16[1,64,2048]{2,1,0:T(8,128)(2,1)} %param.9) | copy-start | bytes 786436
  103.8 111.4 %copy-start.58 = (f32[2,256]{1,0:T(2,128)S(1)}, f32[2,256]{1,0:T(2,128)}, u32[]{:S(2)}) copy-start(f32[2,256]{1,0:T(2,128)} %param.16) | copy-start | bytes 6148
  103.8 166.1 %all-gather.11.cloned.1.call-start = ((), (), s32[]{:S(2)}) async-start(), calls=%async_computation.9 | async-start | bytes 8650752 | tf_op jit(solution)/shard_map/all_gather | solution.py:19
  213.9 173.4 %copy-start.6 = (f32[1,64,2048]{2,1,0:T(8,128)}, f32[1,64,2048]{2,1,0:T(8,128)S(1)}, u32[]{:S(2)}) copy-start(f32[1,64,2048]{2,1,0:T(8,128)S(1)} %get-tuple-element.60) | copy-start | bytes 1572868
  214.0 62.1 %copy-start.52 = (f32[64]{0:T(128)}, f32[64]{0:T(128)S(1)}, u32[]{:S(2)}) copy-start(f32[64]{0:T(128)S(1)} %broadcast_multiply_fusion.2) | copy-start | bytes 772
  214.2 61.9 %copy-start.62 = (f32[64]{0:T(128)}, f32[64]{0:T(128)S(1)}, u32[]{:S(2)}) copy-start(f32[64]{0:T(128)S(1)} %multiply_reduce_fusion.5) | copy-start | bytes 772
  214.2 61.9 %copy-start.54 = (f32[64]{0:T(128)}, f32[64]{0:T(128)S(1)}, u32[]{:S(2)}) copy-start(f32[64]{0:T(128)S(1)} %fusion.236) | copy-start | bytes 772
  215.1 219.9 %all-gather.13.cloned.1.call-start = ((), (), s32[]{:S(2)}) async-start(), calls=%async_computation.10 | async-start | bytes 8650752 | tf_op jit(solution)/shard_map/all_gather | solution.py:19
  388.7 234.6 %all-gather.15.cloned.1.call-start = ((), (), s32[]{:S(2)}) async-start(), calls=%async_computation.11 | async-start | bytes 8650752 | tf_op jit(solution)/shard_map/all_gather | solution.py:19
  576.7 95.4 %all-gather.17.cloned.1.call-start = ((), (), s32[]{:S(2)}) async-start(), calls=%async_computation.12 | async-start | bytes 8650752 | tf_op jit(solution)/shard_map/all_gather | solution.py:19
  672.1 8.7 copy-start.26
  686.4 109.7 %all-to-all-start.4 = ((bf16[1,32,64,2048]{3,2,0,1:T(8,128)(2,1)}), bf16[1,32,64,2048]{3,2,0,1:T(8,128)(2,1)}, u32[]{:S(2)}, u32[]{:S(2)}) async-start(bf16[1,32,64,2048]{3,2,0,1:T(8,128)(2,1)} %bitcast.448), calls=%async_computation.4 | async-start | bytes 16777216 | tf_op jit(solution)/shard_map/all_to_all | solution.py:25
  796.1 116.7 %all-to-all-start.3 = ((bf16[1,32,64,2048]{3,2,0,1:T(8,128)(2,1)}), bf16[1,32,64,2048]{3,2,0,1:T(8,128)(2,1)}, u32[]{:S(2)}, u32[]{:S(2)}) async-start(bf16[1,32,64,2048]{3,2,0,1:T(8,128)(2,1)} %bitcast.452), calls=%async_computation.3 | async-start | bytes 16777216 | tf_op jit(solution)/shard_map/all_to_all | solution.py:25
  808.2 167.3 %all-gather.19.cloned.1.call-start = ((), (), s32[]{:S(2)}) async-start(), calls=%async_computation.13 | async-start | bytes 8650752 | tf_op jit(solution)/shard_map/all_gather | solution.py:19
  814.6 104.8 %copy-start.22 = (bf16[1,64,2048]{2,1,0:T(8,128)(2,1)S(1)}, bf16[1,64,2048]{2,1,0:T(8,128)(2,1)}, u32[]{:S(2)}) copy-start(bf16[1,64,2048]{2,1,0:T(8,128)(2,1)} %param.10) | copy-start | bytes 786436
  920.9 286.6 %all-gather.21.cloned.1.call-start = ((), (), s32[]{:S(2)}) async-start(), calls=%async_computation.14 | async-start | bytes 8650752 | tf_op jit(solution)/shard_map/all_gather | solution.py:19
  981.5 18.1 %slice-start.8 = ((s8[16777216]{0:T(1024)(128)(4,1)}), s8[4194304]{0:T(1024)(128)(4,1)S(1)}, s32[]{:S(2)}) async-start(s8[16777216]{0:T(1024)(128)(4,1)} %bitcast.442), calls=%async_computation.25 | async-start | bytes 8388608
  987.7 11.9 slice-start.9
  987.7 11.9 slice-start.10
  987.8 12.5 slice-start.11
  1000.3 9.6 copy-start.33
  1160.5 217.8 %all-gather.23.cloned.1.call-start = ((), (), s32[]{:S(2)}) async-start(), calls=%async_computation.15 | async-start | bytes 8650752 | tf_op jit(solution)/shard_map/all_gather | solution.py:19
  1215.5 112.4 %copy-start.28 = (bf16[2048,256]{1,0:T(8,128)(2,1)}, bf16[2048,256]{1,0:T(8,128)(2,1)S(1)}, u32[]{:S(2)}) copy-start(bf16[2048,256]{1,0:T(8,128)(2,1)S(1)} %get-tuple-element.90) | copy-start | bytes 3145732
  1331.8 46.6 %copy-start.25 = (bf16[2,1,64,2048]{3,2,1,0:T(8,128)(2,1)S(1)}, bf16[2,1,64,2048]{3,2,1,0:T(8,128)(2,1)}, u32[]{:S(2)}) copy-start(bf16[2,1,64,2048]{3,2,1,0:T(8,128)(2,1)} %param.14) | copy-start | bytes 1572868
  1338.9 51.6 %copy-start.17 = (bf16[2048,64]{0,1:T(8,128)(2,1)S(1)}, bf16[2048,64]{0,1:T(8,128)(2,1)}, u32[]{:S(2)}) copy-start(bf16[2048,64]{0,1:T(8,128)(2,1)} %copy-done.16) | copy-start | bytes 786436
  1384.4 18.1 %slice-start.4 = ((s8[16777216]{0:T(1024)(128)(4,1)}), s8[4194304]{0:T(1024)(128)(4,1)S(1)}, s32[]{:S(2)}) async-start(s8[16777216]{0:T(1024)(128)(4,1)} %bitcast.440), calls=%async_computation.21 | async-start | bytes 8388608
  1390.6 11.9 slice-start.5
  1390.6 11.9 slice-start.6
  1390.6 12.9 slice-start.7
  1390.6 12.9 copy-start.40
  1390.6 12.9 copy-start.42
  1403.5 9.7 copy-start.31
  1449.1 168.6 %all-to-all-start.7 = ((bf16[1,32,64,2048]{3,2,0,1:T(8,128)(2,1)}), bf16[1,32,64,2048]{3,2,0,1:T(8,128)(2,1)}, u32[]{:S(2)}, u32[]{:S(2)}) async-start(bf16[1,32,64,2048]{3,2,0,1:T(8,128)(2,1)} %bitcast.450), calls=%async_computation.7 | async-start | bytes 16777216 | tf_op jit(solution)/shard_map/all_to_all | solution.py:25
  1453.5 261.9 %all-reduce.2.cloned.1.call-start = ((), (), s32[]{:S(2)}) async-start(), calls=%async_computation.16 | async-start | bytes 131072 | tf_op jit(solution)/shard_map/psum | solution.py:113
  1460.3 10.2 slice-start.2
  1479.9 121.7 %copy-start.13 = (bf16[2048,64]{0,1:T(8,128)(2,1)S(1)}, bf16[2048,64]{0,1:T(8,128)(2,1)}, u32[]{:S(2)}) copy-start(bf16[2048,64]{0,1:T(8,128)(2,1)} %copy-done.12) | copy-start | bytes 786436
  1601.5 11.5 slice-start
  1616.3 7.4 copy-start.57
  1616.3 7.7 copy-start.43
  1616.3 7.7 copy-start.44
  1616.3 7.7 copy-start.45
  1616.4 7.7 copy-start.46
  (50 other events, 209.0 us)
Sparse Core Ops, SparseCore 0:
  13.8 51.5 all-gather.8
  215.3 54.6 all-gather.10
  388.8 46.2 all-gather.12
  576.8 46.3 all-gather.14
  625.2 46.8 all-gather.16
  921.0 54.4 all-gather.18
  1160.6 46.8 all-gather.20
  1331.9 46.3 all-gather.22
  1625.0 90.3 all-reduce.1
where the time goes:
time: 1730 us; the launch traced here: 1720 us
  waiting for transfers between devices  768 us (44%)
  blocking collectives  550 us (32%)
  matrix products  257 us (15%)
  other arithmetic  94.8 us (5%)
  starting transfers between devices  27.5 us (2%)
    all_to_all x4, blocking collectives, scatter_rows(): received = lax.all_to_all(sent, 'tp', 1, 1, tiled=True)  433 us
    all_gather x8, waiting for transfers between devices, gather_rows(): return lax.all_gather(local_vals, 'tp', axis=1, tiled=True)  379 us
    all_to_all x4, waiting for transfers between devices, scatter_rows(): received = lax.all_to_all(sent, 'tp', 1, 1, tiled=True)  298 us
    psum x1, blocking collectives, device_step(): lax.psum((jnp.stack([grad_set[0] for grad_set in layer_grads]), jnp.stack...  117 us
    psum x1, waiting for transfers between devices, device_step(): lax.psum((jnp.stack([grad_set[0] for grad_set in layer_grads]), jnp.stack...  89.6 us
  transfers between devices with their start and end apart: 13, of which 12 were waited for; matrix products, arithmetic and copies ran while one was open for 4% of the time, Pallas kernels for 0%

commit v1 on v0

v1 whole, which is shorter than its diff:
```python
import functools
import math

import jax
import jax.numpy as jnp
from jax import lax
from jax.experimental import pallas as pl
from jax.experimental.pallas import tpu as pltpu
from jax.sharding import PartitionSpec as P

MESH = pl.DeviceIdType.MESH
BF = jnp.bfloat16
F32 = jnp.float32
LN_EPS = 1e-5
OFFS = (0, -1, 1, 2)
RS_ORDER = (2, 1, -1, 0)
PAIR = (0, 1)
WAYS = (1, -1)
LATE = (2, 3)
NN = ((1,), (0,))
NT = ((1,), (1,))
TN = ((0,), (0,))
MIB = 1 << 20
COMM_VMEM = [size * MIB for size in (12, 26, 26, 26, 22, 8, 20, 26)]
Q_BLOCKS = 8
ROW_CHUNK = 64
BACK_CHUNK = 64
ROW_UNROLL = 4
BACK_UNROLL = 2
LOG2E = math.log2(math.e)


def matmul(lhs, rhs, dims):
    return lax.dot_general(lhs, rhs, (dims, ((), ())), preferred_element_type=F32)


class Net:
    def __init__(self, group_size):
        side = math.isqrt(group_size // 2)
        me = lax.axis_index('tp')
        self.side = side
        self.core = lax.rem(me, 2)
        self.col = lax.rem(me // 2, side)
        self.row = me // (2 * side)

    def shift(self, pos, off):
        return lax.rem(pos + (off + self.side), self.side)

    def block(self, half, first, second):
        if half == 0:
            return self.shift(self.row, second), self.shift(self.col, first)
        return self.shift(self.row, first), self.shift(self.col, second)

    def neighbour(self, half, axis, sgn):
        if (axis == 0) == (half == 0):
            row, col = self.row, self.shift(self.col, sgn)
        else:
            row, col = self.shift(self.row, sgn), self.col
        return {'tp': (row * self.side + col) * 2 + self.core}

    def partner(self):
        return {'tp': (self.row * self.side + self.col) * 2 + (1 - self.core)}

    def pair_copy(self, src, dst, send_sem, recv_sem, num):
        return pltpu.make_async_remote_copy(src_ref=src, dst_ref=dst, send_sem=send_sem.at[num], recv_sem=recv_sem.at[num],
                                            device_id=self.partner(), device_id_type=MESH)

    def pair_barrier(self):
        sem = pltpu.get_barrier_semaphore()
        pl.semaphore_signal(sem, inc=1, device_id=self.partner(), device_id_type=MESH)
        pl.semaphore_wait(sem, 1)

    def barrier(self):
        sem = pltpu.get_barrier_semaphore()
        for half in PAIR:
            for sgn in WAYS:
                pl.semaphore_signal(sem, inc=1, device_id=self.neighbour(half, 0, sgn), device_id_type=MESH)
        pl.semaphore_wait(sem, 4)


class Gather:
    def __init__(self, net, buf, send_sem, recv_sem):
        self.net, self.buf, self.send_sem, self.recv_sem = net, buf, send_sem, recv_sem
        self.rows = buf.shape[2]
        self.sent = []

    def ident(self, half, stage, first, kind):
        return half * 20 + (0 if stage == 0 else 4 + 4 * OFFS.index(first)) + kind

    def slot(self, half, first, second, kind):
        row, col = self.net.block(half, first, second)
        n_half = self.rows // 2
        start, size = half * n_half, n_half
        if kind >= 2:
            size = n_half // 2
            start += (kind - 2) * size
        return self.buf.at[row, col, pl.ds(start, size)]

    def copy(self, half, stage, first, kind, ref):
        ident = self.ident(half, stage, first, kind)
        sgn = 1 if kind % 2 == 0 else -1
        return pltpu.make_async_remote_copy(
            src_ref=ref, dst_ref=ref, send_sem=self.send_sem.at[ident], recv_sem=self.recv_sem.at[ident],
            device_id=self.net.neighbour(half, stage, sgn), device_id_type=MESH)

    def send(self, half, stage, first, kind):
        back = (0, 0, -1, 1)[kind]
        offs = (back, 0) if stage == 0 else (first, back)
        copy = self.copy(half, stage, first, kind, self.slot(half, offs[0], offs[1], kind))
        copy.start()
        self.sent.append(copy)

    def wait(self, half, stage, first, kind):
        back = (-1, 1, 2, 2)[kind]
        offs = (back, 0) if stage == 0 else (first, back)
        self.copy(half, stage, first, kind, self.slot(half, offs[0], offs[1], kind)).wait_recv()

    def each(self, call, stage, first, kinds):
        for kind in kinds:
            for half in PAIR:
                call(half, stage, first, kind)

    def onward(self, half, stage, first, kind):
        self.wait(half, stage, first, kind)
        self.send(half, stage, first, kind + 2)

    def run(self):
        self.each(self.send, 0, 0, PAIR)
        self.each(self.send, 1, 0, PAIR)
        for kind in PAIR:
            for half in PAIR:
                self.onward(half, 0, 0, kind)
                for way in PAIR:
                    self.send(half, 1, -WAYS[kind], way)
        self.each(self.onward, 1, 0, PAIR)
        self.each(self.wait, 0, 0, LATE)
        self.each(self.send, 1, 2, PAIR)
        for first in OFFS[1:]:
            self.each(self.onward, 1, first, PAIR)
        for first in OFFS:
            self.each(self.wait, 1, first, LATE)
        for copy in self.sent:
            copy.wait_send()


class Scatter:
    def __init__(self, net, part, recv, out, held, send_sem, recv_sem):
        self.net, self.part, self.recv, self.out, self.held = net, part, recv, out, held
        self.send_sem, self.recv_sem = send_sem, recv_sem
        self.quarter = part.shape[2] // 4
        self.sent = []

    def copy(self, half, stage, way, kind, ref):
        ident = ((half * 5 + stage) * 2 + way) * 3 + kind
        return pltpu.make_async_remote_copy(
            src_ref=ref, dst_ref=self.recv.at[half, stage, way, kind],
            send_sem=self.send_sem.at[ident], recv_sem=self.recv_sem.at[ident],
            device_id=self.net.neighbour(half, 0 if stage == 4 else 1, WAYS[way]), device_id_type=MESH)

    def send(self, half, stage, way, kind, ref):
        copy = self.copy(half, stage, way, kind, ref)
        copy.start()
        self.sent.append(copy)

    def wait(self, half, stage, way, kind):
        self.copy(half, stage, way, kind, self.recv.at[half, stage, way, kind]).wait_recv()

    def term(self, half, stage, off, sub):
        if stage == 4:
            return self.held.at[half, {2: 0, 1: 1, -1: 2}[off], pl.ds(sub * self.quarter, self.quarter)]
        row, col = self.net.block(half, RS_ORDER[stage], off)
        return self.part.at[row, col, pl.ds((2 * half + sub) * self.quarter, self.quarter)]

    def far(self, half, stage):
        for way in PAIR:
            self.send(half, stage, way, 0, self.term(half, stage, 2, way))

    def near_plain(self, half, stage, way):
        self.send(half, stage, way, 1, self.term(half, stage, WAYS[way], 1 - way))

    def near_summed(self, half, stage, way):
        self.wait(half, stage, way, 0)
        total = self.term(half, stage, WAYS[way], way)[...].astype(F32) + self.recv[half, stage, way, 0].astype(F32)
        self.out[half, stage, way] = total.astype(BF)
        self.send(half, stage, way, 2, self.out.at[half, stage, way])

    def arrived(self, half, stage, sub):
        first = self.recv[half, stage, 0, 2 if sub == 0 else 1].astype(F32)
        second = self.recv[half, stage, 1, 1 if sub == 0 else 2].astype(F32)
        return first + second

    def finish(self, half, stage):
        for way in PAIR:
            self.wait(half, stage, way, 1)
            self.wait(half, stage, way, 2)
        for sub in PAIR:
            total = self.term(half, stage, 0, sub)[...].astype(F32) + self.arrived(half, stage, sub)
            rows = pl.ds(sub * self.quarter, self.quarter)
            if stage < 3:
                self.held[half, stage, rows] = total.astype(BF)
            else:
                self.last[half, rows] = total

    def run(self, last):
        self.last = last
        for stage in range(4):
            for half in PAIR:
                self.far(half, stage)
        for stage in range(3):
            for half in PAIR:
                for way in PAIR:
                    self.near_summed(half, stage, way)
                    self.near_plain(half, stage, way)
        for half in PAIR:
            self.finish(half, 0)
            self.far(half, 4)
        for half in PAIR:
            for way in PAIR:
                self.near_summed(half, 3, way)
                self.near_plain(half, 3, way)
        for stage in (1, 2):
            for half in PAIR:
                self.finish(half, stage)
                self.near_plain(half, 4, stage - 1)
        for half in PAIR:
            for way in PAIR:
                self.near_summed(half, 4, way)
        for half in PAIR:
            self.finish(half, 3)
        for half in PAIR:
            for way in PAIR:
                self.wait(half, 4, way, 1)
                self.wait(half, 4, way, 2)
            for sub in PAIR:
                rows = pl.ds(sub * self.quarter, self.quarter)
                last[half, rows] = last[half, rows] + self.arrived(half, 4, sub)
        for copy in self.sent:
            copy.wait_send()


def gather_scratch():
    return [pltpu.SemaphoreType.DMA((40,)), pltpu.SemaphoreType.DMA((40,))]


def scatter_scratch(rows, width):
    quarter = rows // 4
    return [pltpu.VMEM((2, 5, 2, 3, quarter, width), BF),
            pltpu.VMEM((2, 5, 2, quarter, width), BF),
            pltpu.VMEM((2, 3, 2 * quarter, width), BF),
            pltpu.VMEM((2, 2 * quarter, width), F32),
            pltpu.SemaphoreType.DMA((60,)), pltpu.SemaphoreType.DMA((60,))]


def vmem_specs(count):
    return [pl.BlockSpec(memory_space=pltpu.VMEM)] * count


def comm_params(ident):
    return pltpu.CompilerParams(collective_id=ident, has_side_effects=True, vmem_limit_bytes=COMM_VMEM[ident])


def normalised(vals):
    mean_val = jnp.mean(vals, axis=-1, keepdims=True)
    centered = vals - mean_val
    var_val = jnp.mean(centered * centered, axis=-1, keepdims=True)
    inv_std = lax.rsqrt(var_val + LN_EPS)
    return centered * inv_std, inv_std


def norm_backward(d_out, vals, gain):
    unit, inv_std = normalised(vals)
    d_unit = d_out * gain
    mean_d = jnp.mean(d_unit, axis=-1, keepdims=True)
    mean_du = jnp.mean(d_unit * unit, axis=-1, keepdims=True)
    d_vals = inv_std * (d_unit - mean_d - unit * mean_du)
    return d_vals, jnp.sum(d_out * unit, axis=0, keepdims=True), jnp.sum(d_out, axis=0, keepdims=True)


def col_sum(vals):
    return jnp.sum(vals, axis=0, keepdims=True)


def first_kernel(group_size, x_ref, par_ref, h_ref, g_send, g_recv):
    net = Net(group_size)
    unit, _ = normalised(x_ref[...].astype(F32))
    h_ref[net.row, net.col] = (unit * par_ref[0:1] + par_ref[1:2]).astype(BF)
    net.barrier()
    Gather(net, h_ref, g_send, g_recv).run()


def forward_kernel(group_size, part_ref, res_ref, par_ref, new_ref, h_ref, recv, out, held, last, s_send, s_recv, g_send, g_recv):
    net = Net(group_size)
    rows, width = res_ref.shape
    net.barrier()
    Scatter(net, part_ref, recv, out, held, s_send, s_recv).run(last)
    new = res_ref[...] + last[...].reshape(rows, width) + par_ref[0:1]
    new_ref[...] = new
    unit, _ = normalised(new)
    h_ref[net.row, net.col] = (unit * par_ref[1:2] + par_ref[2:3]).astype(BF)
    Gather(net, h_ref, g_send, g_recv).run()


def turn_kernel(group_size, part_ref, res_ref, par_ref, dy_ref, y_ref, sum_ref, d_ref, recv, out, held, last, s_send, s_recv, g_send, g_recv):
    net = Net(group_size)
    rows, width = res_ref.shape
    d_ref[net.row, net.col] = dy_ref[...]
    net.barrier()
    Scatter(net, part_ref, recv, out, held, s_send, s_recv).run(last)
    y_ref[...] = (res_ref[...] + last[...].reshape(rows, width) + par_ref[0:1]).astype(BF)
    sum_ref[0:1] = col_sum(dy_ref[...].astype(F32))
    Gather(net, d_ref, g_send, g_recv).run()


def backward_kernel(group_size, part_ref, res_ref, par_ref, dres_ref, new_ref, sum_ref, d_ref, recv, out, held, last, s_send, s_recv, g_send, g_recv):
    net = Net(group_size)
    rows, width = res_ref.shape
    net.barrier()
    Scatter(net, part_ref, recv, out, held, s_send, s_recv).run(last)
    d_vals, d_gain, d_shift = norm_backward(last[...].reshape(rows, width), res_ref[...], par_ref[0:1])
    new = dres_ref[...] + d_vals
    new_ref[...] = new
    d_ref[net.row, net.col] = new.astype(BF)
    sum_ref[0:1] = d_gain
    sum_ref[1:2] = d_shift
    sum_ref[2:3] = col_sum(new)
    Gather(net, d_ref, g_send, g_recv).run()


def last_kernel(group_size, part_ref, res_ref, par_ref, dres_ref, new_ref, sum_ref, recv, out, held, last, s_send, s_recv):
    net = Net(group_size)
    rows, width = res_ref.shape
    net.barrier()
    Scatter(net, part_ref, recv, out, held, s_send, s_recv).run(last)
    d_vals, d_gain, d_shift = norm_backward(last[...].reshape(rows, width), res_ref[...], par_ref[0:1])
    new_ref[...] = (dres_ref[...] + d_vals).astype(BF)
    sum_ref[0:1] = d_gain
    sum_ref[1:2] = d_shift


def sum_kernel(group_size, in_ref, out_ref, buf, sem_s, sem_r):
    net = Net(group_size)
    sem = pltpu.get_barrier_semaphore()
    targets = [[(net.row, net.shift(net.col, off)) for off in (1, 2, 3)], [(net.shift(net.row, off), net.col) for off in (1, 2, 3)]]
    devs = [[{'tp': (row * net.side + col) * 2 + net.core} for row, col in pair] for pair in targets]
    for dev in devs[0] + devs[1] + [net.partner()]:
        pl.semaphore_signal(sem, inc=1, device_id=dev, device_id_type=MESH)
    pl.semaphore_wait(sem, 7)
    value = in_ref[...]
    for axis in PAIR:
        own = net.col if axis == 0 else net.row
        buf[axis, own] = value
        copies = []
        for num, dev in enumerate(devs[axis]):
            copies.append(pltpu.make_async_remote_copy(
                src_ref=buf.at[axis, own], dst_ref=buf.at[axis, own], send_sem=sem_s.at[axis * 3 + num],
                recv_sem=sem_r.at[axis * 3 + num], device_id=dev, device_id_type=MESH))
            copies[-1].start()
        for copy in copies:
            copy.wait_recv()
        value = buf[axis, 0] + buf[axis, 1] + buf[axis, 2] + buf[axis, 3]
        for copy in copies:
            copy.wait_send()
    buf[2, 0] = value
    copy = pltpu.make_async_remote_copy(src_ref=buf.at[2, 0], dst_ref=buf.at[2, 1], send_sem=sem_s.at[6], recv_sem=sem_r.at[6],
                                        device_id=net.partner(), device_id_type=MESH)
    copy.start()
    copy.wait()
    out_ref[...] = value + buf[2, 1]


def gelu_tanh(pre_act):
    return jax.nn.gelu(pre_act, approximate=True)


def attention_kernel(group_size, qkv_ref, nat_ref, stat_ref, a_ref, send, score, prob, a_nat, a_part, send_sem, recv_sem):
    net = Net(group_size)
    net.pair_barrier()
    parts, n_blk, _, rows, head = nat_ref.shape
    core, n_plane = net.core, n_blk * rows
    for part in range(parts):
        send[part] = qkv_ref[:, (parts + part) * head:(parts + part + 1) * head].reshape(n_blk, rows, head)
    copies = [net.pair_copy(send, nat_ref.at[:, :, core], send_sem, recv_sem, 0)]
    copies[0].start()
    for part in range(parts):
        nat_ref[part, :, core] = qkv_ref[:, part * head:(part + 1) * head].reshape(n_blk, rows, head)
    copies[0].wait_recv()
    step = n_blk // Q_BLOCKS
    n_q = 2 * step * rows
    factor = head ** -0.5 * LOG2E
    for blk in range(Q_BLOCKS):
        here, upto, left = pl.ds(blk * step, step), (blk + 1) * step, blk * n_q
        size = left + n_q
        score[:, :size] = matmul(nat_ref[0, here].reshape(n_q, head), nat_ref[1, :upto].reshape(size, head), NT)

        def softmax_rows(num, carry):
            row = pl.ds(pl.multiple_of(num * ROW_CHUNK, ROW_CHUNK), ROW_CHUNK)
            vals = [score[row, :left]] if left else []
            vals.append(masked(score[row, left:size], num * ROW_CHUNK))
            top = functools.reduce(jnp.maximum, [jnp.max(val, axis=1, keepdims=True) for val in vals])
            exps = [jnp.exp2((val - top) * factor) for val in vals]
            inv = 1.0 / sum(jnp.sum(val, axis=1, keepdims=True) for val in exps)
            if left:
                prob[row, :left] = (exps[0] * inv).astype(BF)
            prob[row, left:size] = (exps[-1] * inv).astype(BF)
            stat = pl.ds(pl.multiple_of(left + num * ROW_CHUNK, ROW_CHUNK), ROW_CHUNK)
            stat_ref[0, stat] = top
            stat_ref[1, stat] = inv
            return carry

        lax.fori_loop(0, n_q // ROW_CHUNK, softmax_rows, 0, unroll=ROW_UNROLL)
        attn = matmul(prob[:, :size], nat_ref[2, :upto].reshape(size, head), NN).astype(BF)
        a_nat[here] = attn.reshape(step, 2, rows, head)
        copies.append(net.pair_copy(a_nat.at[here, 1 - core], a_part.at[here], send_sem, recv_sem, 1 + blk))
        copies[-1].start()
    a_ref[:, :head] = a_nat[:, core].reshape(n_plane, head)
    for copy in copies[1:]:
        copy.wait_recv()
    a_ref[:, head:] = a_part[...].reshape(n_plane, head)
    for copy in copies:
        copy.wait_send()


def masked(vals, first_row):
    row = first_row + lax.broadcasted_iota(jnp.int32, vals.shape, 0)
    return jnp.where(row >= lax.broadcasted_iota(jnp.int32, vals.shape, 1), vals, -1e30)


def attention_back_kernel(group_size, d_ref, nat_ref, stat_ref, dq_ref, send, d_nat, score, d_prob, prob, d_score, dk_acc, dv_acc,
                          g_nat, g_part, send_sem, recv_sem):
    net = Net(group_size)
    net.pair_barrier()
    parts, n_blk, _, rows, head = nat_ref.shape
    core, n_plane = net.core, n_blk * rows
    send[...] = d_ref[:, head:].reshape(n_blk, rows, head)
    copies = [net.pair_copy(send, d_nat.at[:, core], send_sem, recv_sem, 0)]
    copies[0].start()
    d_nat[:, core] = d_ref[:, :head].reshape(n_blk, rows, head)
    copies[0].wait_recv()
    step = n_blk // Q_BLOCKS
    n_q = 2 * step * rows
    scale = head ** -0.5
    for blk in reversed(range(Q_BLOCKS)):
        here, upto, left = pl.ds(blk * step, step), (blk + 1) * step, blk * n_q
        size = left + n_q
        q_vals = nat_ref[0, here].reshape(n_q, head)
        k_vals = nat_ref[1, :upto].reshape(size, head)
        d_vals = d_nat[here].reshape(n_q, head)
        score[:, :size] = matmul(q_vals, k_vals, NT)
        d_prob[:, :size] = matmul(d_vals, nat_ref[2, :upto].reshape(size, head), NT)

        def score_rows(num, carry):
            row = pl.ds(pl.multiple_of(num * BACK_CHUNK, BACK_CHUNK), BACK_CHUNK)
            stat = pl.ds(pl.multiple_of(left + num * BACK_CHUNK, BACK_CHUNK), BACK_CHUNK)
            top, inv = stat_ref[0, stat], stat_ref[1, stat]
            cols = [slice(0, left)] if left else []
            cols.append(slice(left, size))
            probs = []
            for col in cols:
                val = score[row, col]
                if col is cols[-1]:
                    val = masked(val, num * BACK_CHUNK)
                probs.append((jnp.exp2((val - top) * (scale * LOG2E)) * inv).astype(BF))
                prob[row, col] = probs[-1]
            wide = [val.astype(F32) for val in probs]
            grads = [d_prob[row, col] for col in cols]
            dot = sum(jnp.sum(val * grad, axis=1, keepdims=True) for val, grad in zip(wide, grads))
            for col, val, grad in zip(cols, wide, grads):
                d_score[row, col] = (val * (grad - dot) * scale).astype(BF)
            return carry

        lax.fori_loop(0, n_q // BACK_CHUNK, score_rows, 0, unroll=BACK_UNROLL)
        g_nat[0, here] = matmul(d_score[:, :size], k_vals, NN).astype(BF).reshape(step, 2, rows, head)
        for acc, lhs, rhs in ((dk_acc, d_score, q_vals), (dv_acc, prob, d_vals)):
            term = matmul(lhs[:, :size], rhs, TN)
            if blk + 1 == Q_BLOCKS:
                acc[...] = term
            else:
                acc[:size] = acc[:size] + term
        for part, acc in ((1, dk_acc), (2, dv_acc)):
            g_nat[part, here] = acc[left:size].astype(BF).reshape(step, 2, rows, head)
        copies.append(net.pair_copy(g_nat.at[:, here, 1 - core], g_part.at[:, here], send_sem, recv_sem, 1 + blk))
        copies[-1].start()
    for part in range(parts):
        dq_ref[:, part * head:(part + 1) * head] = g_nat[part, :, core].reshape(n_plane, head)
    for copy in copies[1:]:
        copy.wait_recv()
    for part in range(parts):
        dq_ref[:, (parts + part) * head:(parts + part + 1) * head] = g_part[part].reshape(n_plane, head)
    for copy in copies:
        copy.wait_send()


def solution(mesh):
    group_size = mesh.shape['tp']
    side = math.isqrt(group_size // 2)
    if 2 * side * side != group_size or side != len(OFFS):
        raise ValueError('unsupported group')
    swap = [(dev, dev + 1 - 2 * (dev % 2)) for dev in range(group_size)]

    def device_step(x_loc, dy_loc, ln_par, bias_d, w_qkv, w_out, w_up, b_up, w_down):
        n_layers, width = ln_par.shape[0], x_loc.shape[-1]
        rows = x_loc.shape[1]
        n_plane = rows * side * side
        head = w_qkv.shape[-1]
        n_col = w_up.shape[-1]
        plane = jax.ShapeDtypeStruct((side, side, rows, width), BF)
        local_f = jax.ShapeDtypeStruct((rows, width), F32)
        local_b = jax.ShapeDtypeStruct((rows, width), BF)

        def sums(count):
            return jax.ShapeDtypeStruct((count, width), F32)

        def comm(kernel, ident, args, outs, scratch):
            return pl.pallas_call(
                functools.partial(kernel, group_size), name=kernel.__name__, out_shape=outs,
                in_specs=vmem_specs(len(args)), out_specs=jax.tree.map(lambda _: vmem_specs(1)[0], outs),
                scratch_shapes=scratch, compiler_params=comm_params(ident))(*args)

        block_shape = (side * side, rows, head)
        nat_shape = jax.ShapeDtypeStruct((3, side * side, 2, rows, head), BF)
        n_all, n_q = 2 * n_plane, 2 * n_plane // Q_BLOCKS
        stat_shape = jax.ShapeDtypeStruct((2, n_all, 1), F32)
        pair_sems = [pltpu.SemaphoreType.DMA((1 + Q_BLOCKS,))] * 2

        both_scratch = scatter_scratch(rows, width) + gather_scratch()

        def swapped(vals):
            return lax.ppermute(vals, 'tp', swap)

        def blocks(part):
            return part.astype(BF).reshape(side, side, rows, width)

        wq_mine = w_qkv.reshape(n_layers, width, 3 * head)
        wq_both = jnp.concatenate([wq_mine, swapped(wq_mine)], axis=2)
        wo_mine = w_out.reshape(n_layers, head, width)
        wo_both = jnp.concatenate([wo_mine, swapped(wo_mine)], axis=1)
        wu_both = jnp.concatenate([w_up, swapped(w_up)], axis=2)
        wd_both = jnp.concatenate([w_down, swapped(w_down)], axis=1)
        bu_both = jnp.concatenate([b_up, swapped(b_up)], axis=1)

        x_rows = x_loc.reshape(rows, width)
        dy_rows = dy_loc.reshape(rows, width)
        h_plane = comm(first_kernel, 0, [x_rows, ln_par[0, 0:2]], plane, gather_scratch())
        res_one = x_rows.astype(F32)
        saved = []
        for layer in range(n_layers):
            h_flat = h_plane.reshape(n_plane, width)
            qkv = matmul(h_flat, wq_both[layer], NN).astype(BF)
            nat, stat, a_both = comm(attention_kernel, 6, [qkv], (nat_shape, stat_shape, jax.ShapeDtypeStruct((n_plane, 2 * head), BF)), [
                pltpu.VMEM((3,) + block_shape, BF), pltpu.VMEM((n_q, n_all), F32), pltpu.VMEM((n_q, n_all), BF),
                pltpu.VMEM(nat_shape.shape[1:], BF), pltpu.VMEM(block_shape, BF)] + pair_sems)
            part = blocks(matmul(a_both, wo_both[layer], NN))
            par = jnp.concatenate([bias_d[layer, 0:1], ln_par[layer, 2:4]], axis=0)
            res_two, h2_plane = comm(forward_kernel, 1, [part, res_one, par], (local_f, plane), both_scratch)
            h2_flat = h2_plane.reshape(n_plane, width)
            pre_act = matmul(h2_flat, wu_both[layer], NN) + bu_both[layer]
            act_f, gelu_pull = jax.vjp(gelu_tanh, pre_act)
            act = act_f.astype(BF)
            part = blocks(matmul(act, wd_both[layer], NN))
            saved.append((res_one, h_flat, nat, stat, a_both, res_two, h2_flat, gelu_pull, act))
            if layer + 1 < n_layers:
                par = jnp.concatenate([bias_d[layer, 1:2], ln_par[layer + 1, 0:2]], axis=0)
                res_one, h_plane = comm(forward_kernel, 1, [part, res_two, par], (local_f, plane), both_scratch)
            else:
                y_rows, top_sum, d_plane = comm(turn_kernel, 2, [part, res_two, bias_d[layer, 1:2], dy_rows],
                                                (local_b, sums(1), plane), both_scratch)

        d_res = dy_rows.astype(F32)
        bias_two = top_sum[0:1]
        grads = [None] * n_layers
        for layer in reversed(range(n_layers)):
            res_one, h_flat, nat, stat, a_both, res_two, h2_flat, gelu_pull, act = saved[layer]
            d_flat = d_plane.reshape(n_plane, width)
            d_act = matmul(d_flat, wd_both[layer], NT)
            d_pre = gelu_pull(d_act)[0]
            d_pre_bf = d_pre.astype(BF)
            d_bup = jnp.sum(d_pre, axis=0)
            part = blocks(matmul(d_pre_bf, wu_both[layer], NT))
            d_res, sum_two, da_plane = comm(backward_kernel, 3, [part, res_two, ln_par[layer, 2:3], d_res],
                                            (local_f, sums(3), plane), both_scratch)
            d_wdown = matmul(act, d_flat, TN)
            d_wup = matmul(h2_flat, d_pre_bf, TN)
            da_flat = da_plane.reshape(n_plane, width)
            d_both = matmul(da_flat, wo_both[layer], NT).astype(BF)
            dq_both = comm(attention_back_kernel, 7, [d_both, nat, stat], jax.ShapeDtypeStruct((n_plane, 6 * head), BF), [
                pltpu.VMEM(block_shape, BF), pltpu.VMEM(nat_shape.shape[1:], BF), pltpu.VMEM((n_q, n_all), F32),
                pltpu.VMEM((n_q, n_all), F32), pltpu.VMEM((n_q, n_all), BF), pltpu.VMEM((n_q, n_all), BF),
                pltpu.VMEM((n_all, head), F32), pltpu.VMEM((n_all, head), F32), pltpu.VMEM(nat_shape.shape, BF),
                pltpu.VMEM((3,) + block_shape, BF)] + pair_sems)
            part = blocks(matmul(dq_both, wq_both[layer], NT))
            args = [part, res_one, ln_par[layer, 0:1], d_res]
            d_wout = matmul(a_both, da_flat, TN)
            d_wqkv = matmul(h_flat, dq_both, TN)
            if layer > 0:
                d_res, sum_one, d_plane = comm(backward_kernel, 3, args, (local_f, sums(3), plane), both_scratch)
                next_two = sum_one[2:3]
            else:
                x_grad, sum_one = comm(last_kernel, 4, args, (local_b, sums(2)), scatter_scratch(rows, width))
                next_two = None
            small = jnp.concatenate([sum_one[0:2], sum_two[0:2], sum_two[2:3], bias_two], axis=0)
            bias_two = next_two
            grads[layer] = (
                small,
                (d_wqkv[:, :3 * head] + swapped(d_wqkv[:, 3 * head:].astype(BF)).astype(F32)).astype(BF),
                (d_wout[:head] + swapped(d_wout[head:].astype(BF)).astype(F32)).astype(BF),
                (d_wup[:, :n_col] + swapped(d_wup[:, n_col:].astype(BF)).astype(F32)).astype(BF),
                d_bup[:n_col] + swapped(d_bup[n_col:]),
                (d_wdown[:n_col] + swapped(d_wdown[n_col:].astype(BF)).astype(F32)).astype(BF))
        n_small = grads[0][0].shape[0]
        packed = jnp.concatenate([grad[0] for grad in grads], axis=0)
        pad = -packed.shape[0] % 8
        packed = jnp.concatenate([packed, jnp.zeros((pad, width), F32)], axis=0)
        total = comm(sum_kernel, 5, [packed], sums(packed.shape[0]),
                     [pltpu.VMEM((3, side) + packed.shape, F32), pltpu.SemaphoreType.DMA((7,)), pltpu.SemaphoreType.DMA((7,))])
        total = total[:n_small * n_layers].reshape(n_layers, n_small, width)
        return (y_rows.reshape(x_loc.shape), x_grad.reshape(x_loc.shape), total[:, :4], total[:, 4:],
                jnp.stack([grad[1].reshape(width, 3, 1, head) for grad in grads]),
                jnp.stack([grad[2].reshape(1, head, width) for grad in grads]),
                jnp.stack([grad[3] for grad in grads]),
                jnp.stack([grad[4] for grad in grads]),
                jnp.stack([grad[5] for grad in grads]))

    def on_tp(dim, first=None):
        return P(first, *[None] * (dim - 1), 'tp')

    rows_spec = P('dp', 'tp')
    in_specs = (rows_spec, rows_spec, P(), P(), on_tp(3), on_tp(1), on_tp(2), on_tp(1), on_tp(1))
    out_specs = (rows_spec, rows_spec, P('dp'), P('dp'), on_tp(3, 'dp'), on_tp(1, 'dp'), on_tp(2, 'dp'), on_tp(1, 'dp'), on_tp(1, 'dp'))
    return jax.shard_map(device_step, mesh=mesh, in_specs=in_specs, out_specs=out_specs, check_vma=False)
```

time: 1730 us -> 609 us (0.35)
  waiting for transfers between devices: 768 us -> 1.42 us
  blocking collectives: 550 us -> 0 us
  Pallas kernels: 0 us -> 491 us
  matrix products: 257 us -> 70.8 us
  other arithmetic: 94.8 us -> 7.68 us
  starting transfers between devices: 27.5 us -> 6.1 us
    pallas_call x0 -> x14, Pallas kernels: none -> 491 us  [comm(): pl.pallas_call(functools.partial(kernel, group_size), name=kernel.__name_...]
    all_to_all x4 -> x0, blocking collectives: 433 us -> none  [scatter_rows(): received = lax.all_to_all(sent, 'tp', 1, 1, tiled=True)]
    all_gather x8 -> x0, waiting for transfers between devices: 379 us -> none  [gather_rows(): return lax.all_gather(local_vals, 'tp', axis=1, tiled=True)]
    all_to_all x4 -> x0, waiting for transfers between devices: 298 us -> none  [scatter_rows(): received = lax.all_to_all(sent, 'tp', 1, 1, tiled=True)]
    dot_general x48 -> x24, matrix products: 257 us -> 70.8 us  [matmul(): lax.dot_general(lhs, rhs, (dims, ((), ())), preferred_element_type=F32)]
    psum x1 -> x0, blocking collectives: 117 us -> none  [device_step(): lax.psum((jnp.stack([grad_set[0] for grad_set in layer_grads]), jnp.stack...]
    psum x1 -> x0, waiting for transfers between devices: 89.6 us -> none  [device_step(): lax.psum((jnp.stack([grad_set[0] for grad_set in layer_grads]), jnp.stack...]
    reduce_sum x29 -> x0, other arithmetic: 51.4 us -> none  [the longest x9 19.7 us: layer_norm(): return centered * lax.rsqrt(var_val + 1e-05) * ln_gain + ln_shift]
  transfers between devices with their start and end apart: 13 -> 15, of which waited for: 12 -> 2; matrix products, arithmetic and copies ran while one was open for 4% -> 4% of each run, Pallas kernels for 0% -> 15%
where the time goes in v1:
time: 609 us; the launch traced here: 600 us
  Pallas kernels  491 us (81%)
  matrix products  70.8 us (12%)
  local copies, waits for them, and re-layouts  20.9 us (3%)
  other arithmetic  7.68 us (1%)
  starting transfers between devices  6.1 us (1%)
    pallas_call x14, Pallas kernels, comm(): pl.pallas_call(functools.partial(kernel, group_size), name=kernel.__name_...  491 us
    dot_general x24, matrix products, matmul(): lax.dot_general(lhs, rhs, (dims, ((), ())), preferred_element_type=F32)  70.8 us
  transfers between devices with their start and end apart: 15, of which 2 were waited for; matrix products, arithmetic and copies ran while one was open for 4% of the time, Pallas kernels for 15%

profile of v1, /device:TPU:97, one launch (start us, length us, event | category | flops | bytes accessed | tf_op | source)
XLA Modules:
  0.0 599.7 jit_solution(7236962292002734189)
XLA Ops:
  0.6 2.1 collective-permute-start.3
  5.6 1.9 constant_dynamic-update-slice_fusion.1
  8.9 29.3 %first_kernel.1 = bf16[4,4,64,2048]{3,2,1,0:T(8,128)(2,1)S(1)} custom-call(bf16[64,2048]{1,0:T(8,128)(2,1)S(1)} %bitcast.153, f32[2,2048]{1,0:T(2,128)S(1)} %get-tuple-element.68.par_ref), custom_call_target="tpu_custom_call" | custom-call | tf_op jit(solution)/shard_map/first_kernel/pallas_call | solution.py:514
  38.3 1.1 copy-done.20
  39.4 2.4 convolution_convert_fusion.9.qkv_ref
  41.8 13.9 %attention_kernel.2 = (bf16[3,16,2,64,64]{4,3,2,1,0:T(8,128)(2,1)S(1)}, f32[2,2048,1]{2,1,0:T(8,128)S(1)}, bf16[1024,128]{1,0:T(8,128)(2,1)S(1)}) custom-call(bf16[1024,384]{1,0:T(8,128)(2,1)S(1)} %convolution_convert_fusion.9.qkv_ref), custom_call_target="tpu_custom_call" | custom-call | tf_op jit(solution)/shard_map/attention_kernel/pallas_call | solution.py:514
  55.7 1.2 convolution_convert_fusion.7
  56.9 49.0 %forward_kernel.3 = (f32[64,2048]{1,0:T(8,128)S(1)}, bf16[4,4,64,2048]{3,2,1,0:T(8,128)(2,1)S(1)}) custom-call(bf16[4,4,64,2048]{3,2,1,0:T(8,128)(2,1)S(1)} %bitcast.140, f32[64,2048]{1,0:T(8,128)S(1)} %bitcast_convert_fusion.1.res_ref, f32[3,2048]{1,0:T(4,128)S(1)} %get-tuple-element.79.par_ref), custom_call_target="tpu_custom_call" | custom-call | tf_op jit(solution)/shard_map/forward_kernel/pallas_call | solution.py:514
  106.1 2.3 fusion.16
  109.8 2.6 convolution_convert_fusion.5
  112.4 47.1 %forward_kernel.4 = (f32[64,2048]{1,0:T(8,128)S(1)}, bf16[4,4,64,2048]{3,2,1,0:T(8,128)(2,1)S(1)}) custom-call(bf16[4,4,64,2048]{3,2,1,0:T(8,128)(2,1)S(1)} %bitcast.146, f32[64,2048]{1,0:T(8,128)S(1)} %get-tuple-element.37.res_ref, f32[3,2048]{1,0:T(4,128)S(1)} %pad_maximum_fusion.7.par_ref), custom_call_target="tpu_custom_call" | custom-call | tf_op jit(solution)/shard_map/forward_kernel/pallas_call | solution.py:514
  159.6 2.4 convolution_convert_fusion.8.qkv_ref
  162.0 17.6 %attention_kernel.3 = (bf16[3,16,2,64,64]{4,3,2,1,0:T(8,128)(2,1)S(1)}, f32[2,2048,1]{2,1,0:T(8,128)S(1)}, bf16[1024,128]{1,0:T(8,128)(2,1)S(1)}) custom-call(bf16[1024,384]{1,0:T(8,128)(2,1)S(1)} %convolution_convert_fusion.8.qkv_ref), custom_call_target="tpu_custom_call" | custom-call | tf_op jit(solution)/shard_map/attention_kernel/pallas_call | solution.py:514
  179.6 1.2 convolution_convert_fusion.6
  180.8 49.1 %forward_kernel.5 = (f32[64,2048]{1,0:T(8,128)S(1)}, bf16[4,4,64,2048]{3,2,1,0:T(8,128)(2,1)S(1)}) custom-call(bf16[4,4,64,2048]{3,2,1,0:T(8,128)(2,1)S(1)} %bitcast.139, f32[64,2048]{1,0:T(8,128)S(1)} %get-tuple-element.40.res_ref, f32[3,2048]{1,0:T(4,128)S(1)} %get-tuple-element.80.par_ref), custom_call_target="tpu_custom_call" | custom-call | tf_op jit(solution)/shard_map/forward_kernel/pallas_call | solution.py:514
  230.0 3.7 fusion.18
  233.6 5.2 convolution_convert_fusion.4
  238.9 46.1 %turn_kernel.1 = (bf16[64,2048]{1,0:T(8,128)(2,1)S(1)}, f32[1,2048]{1,0:T(1,128)S(1)}, bf16[4,4,64,2048]{3,2,1,0:T(8,128)(2,1)S(1)}) custom-call(bf16[4,4,64,2048]{3,2,1,0:T(8,128)(2,1)S(1)} %bitcast.145, f32[64,2048]{1,0:T(8,128)S(1)} %get-tuple-element.42.res_ref, f32[1,2048]{1,0:T(1,128)S(1)} %get-tuple-element.69.par_ref, bf16[64,2048]{1,0:T(8,128)(2,1)S(1)} %bitcast.154), custom_call_target="tpu_custom_call" | custom-call | tf_op jit(solution)/shard_map/turn_kernel/pallas_call | solution.py:514
  285.0 5.2 fusion.57
  290.2 4.7 fusion.55
  294.9 4.7 fusion.37
  299.5 2.4 convolution_convert_fusion.3
  301.9 42.8 %backward_kernel.3 = (f32[64,2048]{1,0:T(8,128)S(1)}, f32[3,2048]{1,0:T(4,128)S(1)}, bf16[4,4,64,2048]{3,2,1,0:T(8,128)(2,1)S(1)}) custom-call(bf16[4,4,64,2048]{3,2,1,0:T(8,128)(2,1)S(1)} %bitcast.143, f32[64,2048]{1,0:T(8,128)S(1)} %get-tuple-element.42.res_ref, f32[1,2048]{1,0:T(1,128)S(1)} %get-tuple-element.63.par_ref, ...), custom_call_target="tpu_custom_call" | custom-call | tf_op jit(solution)/shard_map/backward_kernel/pallas_call | solution.py:514
  345.5 1.3 convolution_convert_fusion.11.d_ref
  346.7 28.7 %attention_back_kernel.2 = bf16[1024,384]{1,0:T(8,128)(2,1)S(1)} custom-call(bf16[1024,128]{1,0:T(8,128)(2,1)S(1)} %convolution_convert_fusion.11.d_ref, bf16[3,16,2,64,64]{4,3,2,1,0:T(8,128)(2,1)S(1)} %get-tuple-element.46.nat_ref, f32[2,2048,1]{2,1,0:T(8,128)S(1)} %get-tuple-element.47.stat_ref), custom_call_target="tpu_custom_call" | custom-call | tf_op jit(solution)/shard_map/attention_back_kernel/pallas_call | solution.py:514
  375.5 3.5 fusion.60
  379.0 2.4 convolution_convert_fusion.1
  381.4 50.8 %backward_kernel.4 = (f32[64,2048]{1,0:T(8,128)S(1)}, f32[3,2048]{1,0:T(4,128)S(1)}, bf16[4,4,64,2048]{3,2,1,0:T(8,128)(2,1)S(1)}) custom-call(bf16[4,4,64,2048]{3,2,1,0:T(8,128)(2,1)S(1)} %bitcast.144, f32[64,2048]{1,0:T(8,128)S(1)} %get-tuple-element.40.res_ref, f32[1,2048]{1,0:T(1,128)S(1)} %get-tuple-element.62.par_ref, ...), custom_call_target="tpu_custom_call" | custom-call | tf_op jit(solution)/shard_map/backward_kernel/pallas_call | solution.py:514
  432.2 5.3 fusion.58
  437.6 4.9 fusion.54
  442.5 4.4 fusion.34
  446.9 2.4 convolution_convert_fusion.2
  449.3 46.0 %backward_kernel.5 = (f32[64,2048]{1,0:T(8,128)S(1)}, f32[3,2048]{1,0:T(4,128)S(1)}, bf16[4,4,64,2048]{3,2,1,0:T(8,128)(2,1)S(1)}) custom-call(bf16[4,4,64,2048]{3,2,1,0:T(8,128)(2,1)S(1)} %bitcast.141, f32[64,2048]{1,0:T(8,128)S(1)} %get-tuple-element.37.res_ref, f32[1,2048]{1,0:T(1,128)S(1)} %get-tuple-element.64.par_ref, ...), custom_call_target="tpu_custom_call" | custom-call | tf_op jit(solution)/shard_map/backward_kernel/pallas_call | solution.py:514
  496.0 1.3 convolution_convert_fusion.10.d_ref
  497.3 26.0 %attention_back_kernel.3 = bf16[1024,384]{1,0:T(8,128)(2,1)S(1)} custom-call(bf16[1024,128]{1,0:T(8,128)(2,1)S(1)} %convolution_convert_fusion.10.d_ref, bf16[3,16,2,64,64]{4,3,2,1,0:T(8,128)(2,1)S(1)} %get-tuple-element.52.nat_ref, f32[2,2048,1]{2,1,0:T(8,128)S(1)} %get-tuple-element.53.stat_ref), custom_call_target="tpu_custom_call" | custom-call | tf_op jit(solution)/shard_map/attention_back_kernel/pallas_call | solution.py:514
  523.4 3.6 fusion.59
  527.0 2.3 convolution_convert_fusion
  529.3 26.3 %last_kernel.1 = (bf16[64,2048]{1,0:T(8,128)(2,1)S(1)}, f32[2,2048]{1,0:T(2,128)S(1)}) custom-call(bf16[4,4,64,2048]{3,2,1,0:T(8,128)(2,1)S(1)} %bitcast.142, f32[64,2048]{1,0:T(8,128)S(1)} %bitcast_convert_fusion.1.res_ref, f32[1,2048]{1,0:T(1,128)S(1)} %get-tuple-element.61.par_ref, f32[64,2048]{1,0:T(8,128)S(1)} %get-tuple-element.54.dres_ref), custom_call_target="tpu_custom_call" | custom-call | tf_op jit(solution)/shard_map/last_kernel/pallas_call | solution.py:514
  555.8 18.2 %sum_kernel.1 = f32[16,2048]{1,0:T(8,128)S(1)} custom-call(f32[16,2048]{1,0:T(8,128)S(1)} %concatenate.35.in_ref), custom_call_target="tpu_custom_call" | custom-call | tf_op jit(solution)/shard_map/sum_kernel/pallas_call | solution.py:514
  575.4 1.8 slice.338
  577.3 1.8 slice.336
  580.2 1.7 slice.340
  582.3 1.5 slice.341
  589.5 1.3 pad_maximum_fusion.3
  590.7 1.3 copy-done.7
  592.6 1.5 pad_maximum_fusion.1
  594.1 1.4 copy-done.6
  596.4 1.5 pad_maximum_fusion
  (122 shorter events, 18.6 us)
Async XLA Ops:
  0.6 37.6 %collective-permute-start.3 = (f32[2,256]{1,0:T(2,128)}, f32[2,256]{1,0:T(2,128)S(1)}, u32[]{:S(2)}, u32[]{:S(2)}) collective-permute-start(f32[2,256]{1,0:T(2,128)} %param.16), channel_id=1, source_target_pairs={{0,1},{1,0},{2,3},{3,2},{4,5},{5,4},{6,7},{7,6},{8,9},{9,8},{10,11... | collective-permute-start | bytes 6152 | tf_op jit(solution)/shard_map/ppermute | solution.py:528
  2.8 52.9 %collective-permute-start.1 = (bf16[2,64,2048]{2,1,0:T(8,128)(2,1)}, bf16[2,64,2048]{2,1,0:T(8,128)(2,1)S(1)}, u32[]{:S(2)}, u32[]{:S(2)}) collective-permute-start(bf16[2,64,2048]{2,1,0:T(8,128)(2,1)} %bitcast.170), channel_id=1, source_target_pairs={{0,1},{1,0},{2,3},{3,2},{4,5},{5,4},{6,7},{7,6},{8,9},{9,8},{10,11... | collective-permute-start | bytes 1572872 | tf_op jit(solution)/shard_map/ppermute | solution.py:528
  2.9 35.4 %collective-permute-start = (bf16[2,2048,192]{1,2,0:T(8,128)(2,1)}, bf16[2,2048,192]{1,2,0:T(8,128)(2,1)S(1)}, u32[]{:S(2)}, u32[]{:S(2)}) collective-permute-start(bf16[2,2048,192]{1,2,0:T(8,128)(2,1)} %bitcast.183), channel_id=1, source_target_pairs={{0,1},{1,0},{2,3},{3,2},{4,5},{5,4},{6,7},{7,6},{8,9},{9,8},{10,11... | collective-permute-start | bytes 4718600 | tf_op jit(solution)/shard_map/ppermute | solution.py:528
  3.3 102.7 %collective-permute-start.2 = (bf16[2,2048,256]{2,1,0:T(8,128)(2,1)}, bf16[2,2048,256]{2,1,0:T(8,128)(2,1)S(1)}, u32[]{:S(2)}, u32[]{:S(2)}) collective-permute-start(bf16[2,2048,256]{2,1,0:T(8,128)(2,1)} %param.15), channel_id=1, source_target_pairs={{0,1},{1,0},{2,3},{3,2},{4,5},{5,4},{6,7},{7,6},{8,9},{9,8},{10,11... | collective-permute-start | bytes 6291464 | tf_op jit(solution)/shard_map/ppermute | solution.py:528
  3.4 105.1 %collective-permute-start.4 = (bf16[2,256,2048]{2,1,0:T(8,128)(2,1)}, bf16[2,256,2048]{2,1,0:T(8,128)(2,1)S(1)}, u32[]{:S(2)}, u32[]{:S(2)}) collective-permute-start(bf16[2,256,2048]{2,1,0:T(8,128)(2,1)} %param.17), channel_id=1, source_target_pairs={{0,1},{1,0},{2,3},{3,2},{4,5},{5,4},{6,7},{7,6},{8,9},{9,8},{10,11... | collective-permute-start | bytes 6291464 | tf_op jit(solution)/shard_map/ppermute | solution.py:528
  5.5 1.9 copy-start.16
  5.5 2.0 copy-start
  5.6 2.3 copy-start.11
  7.9 0.9 copy-start.1
  7.9 1.0 copy-start.17
  8.9 30.6 %copy-start.18 = (bf16[2,2048,3,1,64]{1,4,3,2,0:T(8,128)(2,1)S(1)}, bf16[2,2048,3,1,64]{1,4,3,2,0:T(8,128)(2,1)}, u32[]{:S(2)}) copy-start(bf16[2,2048,3,1,64]{1,4,3,2,0:T(8,128)(2,1)} %param.13) | copy-start | bytes 4718596
  38.3 1.1 copy-start.20
  39.4 16.2 %copy-start.10 = (bf16[2,1,64,2048]{3,2,1,0:T(8,128)(2,1)S(1)}, bf16[2,1,64,2048]{3,2,1,0:T(8,128)(2,1)}, u32[]{:S(2)}) copy-start(bf16[2,1,64,2048]{3,2,1,0:T(8,128)(2,1)} %param.14) | copy-start | bytes 1572868
  108.5 1.3 copy-start.24
  108.7 3.7 copy-start.14
  112.4 47.2 %copy-start.19 = (bf16[2,2048,3,1,64]{1,4,3,2,0:T(8,128)(2,1)S(1)}, bf16[2,2048,3,1,64]{1,4,3,2,0:T(8,128)(2,1)}, u32[]{:S(2)}) copy-start(bf16[2,2048,3,1,64]{1,4,3,2,0:T(8,128)(2,1)} %param.13) | copy-start | bytes 4718596
  112.4 47.2 %copy-start.21 = (bf16[2,2048,192]{1,2,0:T(8,128)(2,1)S(1)}, bf16[2,2048,192]{1,2,0:T(8,128)(2,1)}, u32[]{:S(2)}) copy-start(bf16[2,2048,192]{1,2,0:T(8,128)(2,1)} %copy-done.20) | copy-start | bytes 4718596
  159.6 2.4 copy-start.2
  229.9 3.7 copy-start.4
  238.9 46.1 %copy-start.26 = (f32[1024,512]{1,0:T(8,128)S(1)}, f32[1024,512]{1,0:T(8,128)}, u32[]{:S(2)}) copy-start(f32[1024,512]{1,0:T(8,128)} %fusion.18) | copy-start | bytes 6291460
  290.2 4.7 copy-start.5
  346.7 28.7 %copy-start.3 = (bf16[4,4,64,2048]{3,2,1,0:T(8,128)(2,1)S(1)}, bf16[4,4,64,2048]{3,2,1,0:T(8,128)(2,1)}, u32[]{:S(2)}) copy-start(bf16[4,4,64,2048]{3,2,1,0:T(8,128)(2,1)} %copy-done.2) | copy-start | bytes 12582916
  375.5 3.5 copy-start.22
  381.4 50.8 %copy-start.15 = (bf16[2,512,2048]{2,1,0:T(8,128)(2,1)S(1)}, bf16[2,512,2048]{2,1,0:T(8,128)(2,1)}, u32[]{:S(2)}) copy-start(bf16[2,512,2048]{2,1,0:T(8,128)(2,1)} %copy-done.14) | copy-start | bytes 12582916
  432.2 5.4 copy-start.25
  523.4 3.6 copy-start.23
  575.3 8.9 %collective-permute-start.12 = (f32[256]{0:T(256)S(1)}, f32[256]{0:T(256)S(1)}, u32[]{:S(2)}, u32[]{:S(2)}) collective-permute-start(f32[256]{0:T(256)S(1)} %slice.205), channel_id=1, source_target_pairs={{0,1},{1,0},{2,3},{3,2},{4,5},{5,4},{6,7},{7,6},{8,9},{9,8},{10,11... | collective-permute-start | bytes 3080 | tf_op jit(solution)/shard_map/ppermute | solution.py:528
  575.4 8.6 %copy-start.9 = (f32[512,2048]{1,0:T(8,128)S(1)}, f32[512,2048]{1,0:T(8,128)}, u32[]{:S(2)}) copy-start(f32[512,2048]{1,0:T(8,128)} %fusion.54) | copy-start | bytes 12582916
  579.0 4.8 copy-start.8
  579.1 11.7 %collective-permute-start.14 = (bf16[256,2048]{1,0:T(8,128)(2,1)S(1)}, bf16[256,2048]{1,0:T(8,128)(2,1)S(1)}, u32[]{:S(2)}, u32[]{:S(2)}) collective-permute-start(bf16[256,2048]{1,0:T(8,128)(2,1)S(1)} %slice.336), channel_id=1, source_target_pairs={{0,1},{1,0},{2,3},{3,2},{4,5},{5,4},{6,7},{7,6},{8,9},{9,8},{10,11... | collective-permute-start | bytes 3145736 | tf_op jit(solution)/shard_map/ppermute | solution.py:528
  579.5 14.6 %collective-permute-start.10 = (bf16[2048,256]{1,0:T(8,128)(2,1)S(1)}, bf16[2048,256]{1,0:T(8,128)(2,1)S(1)}, u32[]{:S(2)}, u32[]{:S(2)}) collective-permute-start(bf16[2048,256]{1,0:T(8,128)(2,1)S(1)} %slice.338), channel_id=1, source_target_pairs={{0,1},{1,0},{2,3},{3,2},{4,5},{5,4},{6,7},{7,6},{8,9},{9,8},{10,11... | collective-permute-start | bytes 3145736 | tf_op jit(solution)/shard_map/ppermute | solution.py:528
  579.7 6.5 %collective-permute-start.8 = (bf16[64,2048]{1,0:T(8,128)(2,1)S(1)}, bf16[64,2048]{1,0:T(8,128)(2,1)S(1)}, u32[]{:S(2)}, u32[]{:S(2)}) collective-permute-start(bf16[64,2048]{1,0:T(8,128)(2,1)S(1)} %slice.342), channel_id=1, source_target_pairs={{0,1},{1,0},{2,3},{3,2},{4,5},{5,4},{6,7},{7,6},{8,9},{9,8},{10,11... | collective-permute-start | bytes 786440 | tf_op jit(solution)/shard_map/ppermute | solution.py:528
  581.8 6.2 %collective-permute-start.6 = (bf16[2048,192]{0,1:T(8,128)(2,1)S(1)}, bf16[2048,192]{0,1:T(8,128)(2,1)S(1)}, u32[]{:S(2)}, u32[]{:S(2)}) collective-permute-start(bf16[2048,192]{0,1:T(8,128)(2,1)S(1)} %slice.340), channel_id=1, source_target_pairs={{0,1},{1,0},{2,3},{3,2},{4,5},{5,4},{6,7},{7,6},{8,9},{9,8},{10,11... | collective-permute-start | bytes 2359304 | tf_op jit(solution)/shard_map/ppermute | solution.py:528
  584.1 4.3 copy-start.12
  584.2 1.3 collective-permute-start.11
  585.4 1.5 collective-permute-start.7
  586.2 2.4 collective-permute-start.5
  587.0 5.4 collective-permute-start.13
  587.2 2.1 copy-start.13
  588.0 7.9 %collective-permute-start.9 = (bf16[2048,256]{1,0:T(8,128)(2,1)S(1)}, bf16[2048,256]{1,0:T(8,128)(2,1)S(1)}, u32[]{:S(2)}, u32[]{:S(2)}) collective-permute-start(bf16[2048,256]{1,0:T(8,128)(2,1)S(1)} %slice.339), channel_id=1, source_target_pairs={{0,1},{1,0},{2,3},{3,2},{4,5},{5,4},{6,7},{7,6},{8,9},{9,8},{10,11... | collective-permute-start | bytes 3145736 | tf_op jit(solution)/shard_map/ppermute | solution.py:528
  589.3 2.8 copy-start.7
  592.6 2.9 copy-start.6

commit v2 on v1

--- a/solution.py
+++ b/solution.py
@@ -21,13 +21,17 @@
 NT = ((1,), (1,))
 TN = ((0,), (0,))
 MIB = 1 << 20
-COMM_VMEM = [size * MIB for size in (12, 26, 26, 26, 22, 8, 20, 26)]
+COMM_VMEM = [size * MIB for size in (4, 10, 6, 16, 14, 14, 12, 20, 20)]
 Q_BLOCKS = 8
 ROW_CHUNK = 64
 BACK_CHUNK = 64
 ROW_UNROLL = 4
 BACK_UNROLL = 2
 LOG2E = math.log2(math.e)
+BOTH_ORDER = 'axaaaxaaaaaamccxccxcccc'
+SCATTER_ORDER = 'axaxaaxaaxaaam'
+WORK_CHUNK = 512
+GATHER_PLAN = [1] * Q_BLOCKS
 
 
 def matmul(lhs, rhs, dims):
@@ -56,6 +60,9 @@
             row, col = self.row, self.shift(self.col, sgn)
         else:
             row, col = self.shift(self.row, sgn), self.col
+        return self.member(row, col)
+
+    def member(self, row, col):
         return {'tp': (row * self.side + col) * 2 + self.core}
 
     def partner(self):
@@ -65,23 +72,18 @@
         return pltpu.make_async_remote_copy(src_ref=src, dst_ref=dst, send_sem=send_sem.at[num], recv_sem=recv_sem.at[num],
                                             device_id=self.partner(), device_id_type=MESH)
 
-    def pair_barrier(self):
+    def barrier(self, with_partner=False):
         sem = pltpu.get_barrier_semaphore()
-        pl.semaphore_signal(sem, inc=1, device_id=self.partner(), device_id_type=MESH)
-        pl.semaphore_wait(sem, 1)
-
-    def barrier(self):
-        sem = pltpu.get_barrier_semaphore()
-        for half in PAIR:
-            for sgn in WAYS:
-                pl.semaphore_signal(sem, inc=1, device_id=self.neighbour(half, 0, sgn), device_id_type=MESH)
-        pl.semaphore_wait(sem, 4)
+        targets = [self.neighbour(half, 0, sgn) for half in PAIR for sgn in WAYS] + [self.partner()] * with_partner
+        for target in targets:
+            pl.semaphore_signal(sem, inc=1, device_id=target, device_id_type=MESH)
+        pl.semaphore_wait(sem, len(targets))
 
 
 class Gather:
-    def __init__(self, net, buf, send_sem, recv_sem):
+    def __init__(self, net, buf, send_sem, recv_sem, rows, start=0):
         self.net, self.buf, self.send_sem, self.recv_sem = net, buf, send_sem, recv_sem
-        self.rows = buf.shape[2]
+        self.rows, self.base = rows, start
         self.sent = []
 
     def ident(self, half, stage, first, kind):
@@ -90,7 +92,7 @@
     def slot(self, half, first, second, kind):
         row, col = self.net.block(half, first, second)
         n_half = self.rows // 2
-        start, size = half * n_half, n_half
+        start, size = self.base + half * n_half, n_half
         if kind >= 2:
             size = n_half // 2
             start += (kind - 2) * size
@@ -124,19 +126,24 @@
         self.wait(half, stage, first, kind)
         self.send(half, stage, first, kind + 2)
 
-    def run(self):
+    def steps(self):
         self.each(self.send, 0, 0, PAIR)
         self.each(self.send, 1, 0, PAIR)
+        yield
         for kind in PAIR:
             for half in PAIR:
                 self.onward(half, 0, 0, kind)
                 for way in PAIR:
                     self.send(half, 1, -WAYS[kind], way)
+        yield
         self.each(self.onward, 1, 0, PAIR)
+        yield
         self.each(self.wait, 0, 0, LATE)
         self.each(self.send, 1, 2, PAIR)
+        yield
         for first in OFFS[1:]:
             self.each(self.onward, 1, first, PAIR)
+            yield
         for first in OFFS:
             self.each(self.wait, 1, first, LATE)
         for copy in self.sent:
@@ -144,10 +151,10 @@
 
 
 class Scatter:
-    def __init__(self, net, part, recv, out, held, send_sem, recv_sem):
-        self.net, self.part, self.recv, self.out, self.held = net, part, recv, out, held
+    def __init__(self, net, part, recv, out, held, last, send_sem, recv_sem, start=0):
+        self.net, self.part, self.recv, self.out, self.held, self.last = net, part, recv, out, held, last
         self.send_sem, self.recv_sem = send_sem, recv_sem
-        self.quarter = part.shape[2] // 4
+        self.quarter, self.base = recv.shape[-2], start
         self.sent = []
 
     def copy(self, half, stage, way, kind, ref):
@@ -169,7 +176,7 @@
         if stage == 4:
             return self.held.at[half, {2: 0, 1: 1, -1: 2}[off], pl.ds(sub * self.quarter, self.quarter)]
         row, col = self.net.block(half, RS_ORDER[stage], off)
-        return self.part.at[row, col, pl.ds((2 * half + sub) * self.quarter, self.quarter)]
+        return self.part.at[row, col, pl.ds(self.base + (2 * half + sub) * self.quarter, self.quarter)]
 
     def far(self, half, stage):
         for way in PAIR:
@@ -201,41 +208,105 @@
             else:
                 self.last[half, rows] = total
 
-    def run(self, last):
-        self.last = last
-        for stage in range(4):
+    def near(self, stage):
+        for half in PAIR:
+            for way in PAIR:
+                self.near_summed(half, stage, way)
+                self.near_plain(half, stage, way)
+
+    def steps(self):
+        last = len(OFFS)
+        for stage in range(last):
             for half in PAIR:
                 self.far(half, stage)
-        for stage in range(3):
-            for half in PAIR:
-                for way in PAIR:
-                    self.near_summed(half, stage, way)
-                    self.near_plain(half, stage, way)
+        yield
+        for stage in range(last - 1):
+            self.near(stage)
+            yield
         for half in PAIR:
             self.finish(half, 0)
-            self.far(half, 4)
-        for half in PAIR:
-            for way in PAIR:
-                self.near_summed(half, 3, way)
-                self.near_plain(half, 3, way)
+            self.far(half, last)
+        yield
+        self.near(last - 1)
+        yield
         for stage in (1, 2):
             for half in PAIR:
                 self.finish(half, stage)
-                self.near_plain(half, 4, stage - 1)
+                self.near_plain(half, last, stage - 1)
+        yield
         for half in PAIR:
             for way in PAIR:
-                self.near_summed(half, 4, way)
+                self.near_summed(half, last, way)
+        yield
         for half in PAIR:
-            self.finish(half, 3)
+            self.finish(half, last - 1)
+        yield
         for half in PAIR:
             for way in PAIR:
-                self.wait(half, 4, way, 1)
-                self.wait(half, 4, way, 2)
+                self.wait(half, last, way, 1)
+                self.wait(half, last, way, 2)
             for sub in PAIR:
                 rows = pl.ds(sub * self.quarter, self.quarter)
-                last[half, rows] = last[half, rows] + self.arrived(half, 4, sub)
+                self.last[half, rows] = self.last[half, rows] + self.arrived(half, last, sub)
         for copy in self.sent:
             copy.wait_send()
+
+    def total(self):
+        n_half, width = self.last.shape[1:]
+        return self.last[...].reshape(2 * n_half, width)
+
+
+def exchanged(net, part_ref, out_ref, scratch, middle, other, order):
+    scatter = Scatter(net, part_ref, *scratch[:6])
+    tasks = {'a': scatter.steps(), 'x': other}
+    if out_ref is not None:
+        tasks['c'] = Gather(net, out_ref, *scratch[6:], part_ref.shape[2]).steps()
+    for code in order:
+        if code == 'm':
+            for _ in tasks['a']:
+                pass
+            middle(scatter.total())
+        else:
+            next(tasks[code], None)
+    for task in tasks.values():
+        for _ in task:
+            pass
+
+
+def weight_work(net, jobs, send_sem, recv_sem):
+    def product(job, which, store):
+        left, right, split_left, out = job[:4]
+        count = out.shape[0] if split_left else out.shape[1]
+        own = slice(which * count, (which + 1) * count)
+        wide = right.shape[1] if split_left else left.shape[1]
+
+        def chunk(num, carry):
+            cols = pl.ds(pl.multiple_of(num * WORK_CHUNK, WORK_CHUNK), WORK_CHUNK)
+            if split_left:
+                store((slice(None), cols), matmul(left[:, own], right[:, cols], TN))
+            else:
+                store((cols, slice(None)), matmul(left[:, cols], right[:, own], TN))
+            return carry
+
+        lax.fori_loop(0, wide // WORK_CHUNK, chunk, 0)
+
+    copies = []
+    for num, job in enumerate(jobs):
+        def keep(place, vals, send=job[4]):
+            send[place] = vals.astype(BF)
+        product(job, 1, keep)
+        copies.append(net.pair_copy(job[4], job[5], send_sem, recv_sem, num))
+        copies[-1].start()
+        yield
+    for copy, job in zip(copies, jobs):
+        copy.wait_recv()
+
+        def add(place, vals, out=job[3], recv=job[5]):
+            out[place] = (vals + recv[place].astype(F32)).astype(BF)
+        product(job, 0, add)
+        yield
+    for copy in copies:
+        copy.wait_send()
 
 
 def gather_scratch():
@@ -285,109 +356,106 @@
     unit, _ = normalised(x_ref[...].astype(F32))
     h_ref[net.row, net.col] = (unit * par_ref[0:1] + par_ref[1:2]).astype(BF)
     net.barrier()
-    Gather(net, h_ref, g_send, g_recv).run()
-
-
-def forward_kernel(group_size, part_ref, res_ref, par_ref, new_ref, h_ref, recv, out, held, last, s_send, s_recv, g_send, g_recv):
+    for _ in Gather(net, h_ref, g_send, g_recv, x_ref.shape[0]).steps():
+        pass
+
+
+def forward_kernel(group_size, part_ref, res_ref, par_ref, new_ref, h_ref, *scratch):
     net = Net(group_size)
-    rows, width = res_ref.shape
     net.barrier()
-    Scatter(net, part_ref, recv, out, held, s_send, s_recv).run(last)
-    new = res_ref[...] + last[...].reshape(rows, width) + par_ref[0:1]
-    new_ref[...] = new
-    unit, _ = normalised(new)
-    h_ref[net.row, net.col] = (unit * par_ref[1:2] + par_ref[2:3]).astype(BF)
-    Gather(net, h_ref, g_send, g_recv).run()
-
-
-def turn_kernel(group_size, part_ref, res_ref, par_ref, dy_ref, y_ref, sum_ref, d_ref, recv, out, held, last, s_send, s_recv, g_send, g_recv):
+
+    def middle(total):
+        new = res_ref[...] + total + par_ref[0:1]
+        new_ref[...] = new
+        unit, _ = normalised(new)
+        h_ref[net.row, net.col] = (unit * par_ref[1:2] + par_ref[2:3]).astype(BF)
+
+    exchanged(net, part_ref, h_ref, scratch, middle, iter(PAIR), BOTH_ORDER)
+
+
+def backward_kernel(splits, gathers, group_size, part_ref, res_ref, par_ref, dres_ref, *refs):
     net = Net(group_size)
-    rows, width = res_ref.shape
-    d_ref[net.row, net.col] = dy_ref[...]
-    net.barrier()
-    Scatter(net, part_ref, recv, out, held, s_send, s_recv).run(last)
-    y_ref[...] = (res_ref[...] + last[...].reshape(rows, width) + par_ref[0:1]).astype(BF)
-    sum_ref[0:1] = col_sum(dy_ref[...].astype(F32))
-    Gather(net, d_ref, g_send, g_recv).run()
-
-
-def backward_kernel(group_size, part_ref, res_ref, par_ref, dres_ref, new_ref, sum_ref, d_ref, recv, out, held, last, s_send, s_recv, g_send, g_recv):
-    net = Net(group_size)
-    rows, width = res_ref.shape
-    net.barrier()
-    Scatter(net, part_ref, recv, out, held, s_send, s_recv).run(last)
-    d_vals, d_gain, d_shift = norm_backward(last[...].reshape(rows, width), res_ref[...], par_ref[0:1])
-    new = dres_ref[...] + d_vals
-    new_ref[...] = new
-    d_ref[net.row, net.col] = new.astype(BF)
-    sum_ref[0:1] = d_gain
-    sum_ref[1:2] = d_shift
-    sum_ref[2:3] = col_sum(new)
-    Gather(net, d_ref, g_send, g_recv).run()
-
-
-def last_kernel(group_size, part_ref, res_ref, par_ref, dres_ref, new_ref, sum_ref, recv, out, held, last, s_send, s_recv):
-    net = Net(group_size)
-    rows, width = res_ref.shape
-    net.barrier()
-    Scatter(net, part_ref, recv, out, held, s_send, s_recv).run(last)
-    d_vals, d_gain, d_shift = norm_backward(last[...].reshape(rows, width), res_ref[...], par_ref[0:1])
-    new_ref[...] = (dres_ref[...] + d_vals).astype(BF)
-    sum_ref[0:1] = d_gain
-    sum_ref[1:2] = d_shift
-
-
-def sum_kernel(group_size, in_ref, out_ref, buf, sem_s, sem_r):
+    net.barrier(True)
+    work, refs = refs[:4], refs[4:]
+    outs, refs = refs[:2], refs[2:]
+    new_ref, sum_ref = refs[:2]
+    d_ref = refs[2] if gathers else None
+    bufs = refs[3 if gathers else 2:]
+    jobs = [(work[2 * num], work[2 * num + 1], split, outs[num], bufs[2 * num], bufs[2 * num + 1]) for num, split in enumerate(splits)]
+    send_sem, recv_sem = bufs[4:6]
+
+    def middle(total):
+        d_vals, d_gain, d_shift = norm_backward(total, res_ref[...], par_ref[0:1])
+        new = dres_ref[...] + d_vals
+        new_ref[...] = new.astype(new_ref.dtype)
+        if gathers:
+            d_ref[net.row, net.col] = new.astype(BF)
+        sum_ref[0:1] = d_gain
+        sum_ref[1:2] = d_shift
+        sum_ref[2:3] = col_sum(new)
+
+    exchanged(net, part_ref, d_ref, bufs[6:], middle, weight_work(net, jobs, send_sem, recv_sem), BOTH_ORDER if gathers else SCATTER_ORDER)
+
+
+def sum_kernel(group_size, in_ref, out_ref, buf, pair_buf, sem_s, sem_r):
     net = Net(group_size)
     sem = pltpu.get_barrier_semaphore()
-    targets = [[(net.row, net.shift(net.col, off)) for off in (1, 2, 3)], [(net.shift(net.row, off), net.col) for off in (1, 2, 3)]]
-    devs = [[{'tp': (row * net.side + col) * 2 + net.core} for row, col in pair] for pair in targets]
-    for dev in devs[0] + devs[1] + [net.partner()]:
+    far = range(1, net.side)
+    devs = [[net.member(net.row, net.shift(net.col, off)) for off in far], [net.member(net.shift(net.row, off), net.col) for off in far]]
+    everyone = devs[0] + devs[1] + [net.partner()]
+    for dev in everyone:
         pl.semaphore_signal(sem, inc=1, device_id=dev, device_id_type=MESH)
-    pl.semaphore_wait(sem, 7)
-    value = in_ref[...]
+    pl.semaphore_wait(sem, len(everyone))
+    n_half = in_ref.shape[0] // 2
+    own, other = [pl.ds(pl.multiple_of(core * n_half, n_half), n_half) for core in (net.core, 1 - net.core)]
+    copy = net.pair_copy(in_ref.at[other], pair_buf, sem_s, sem_r, 0)
+    copy.start()
+    copy.wait()
+    value = in_ref[own] + pair_buf[...]
     for axis in PAIR:
-        own = net.col if axis == 0 else net.row
-        buf[axis, own] = value
+        place = net.row if axis else net.col
+        buf[axis, place] = value
         copies = []
         for num, dev in enumerate(devs[axis]):
+            ident = 2 + axis * len(far) + num
             copies.append(pltpu.make_async_remote_copy(
-                src_ref=buf.at[axis, own], dst_ref=buf.at[axis, own], send_sem=sem_s.at[axis * 3 + num],
-                recv_sem=sem_r.at[axis * 3 + num], device_id=dev, device_id_type=MESH))
+                src_ref=buf.at[axis, place], dst_ref=buf.at[axis, place], send_sem=sem_s.at[ident], recv_sem=sem_r.at[ident],
+                device_id=dev, device_id_type=MESH))
             copies[-1].start()
         for copy in copies:
             copy.wait_recv()
-        value = buf[axis, 0] + buf[axis, 1] + buf[axis, 2] + buf[axis, 3]
+        value = sum(buf[axis, num] for num in range(net.side))
         for copy in copies:
             copy.wait_send()
-    buf[2, 0] = value
-    copy = pltpu.make_async_remote_copy(src_ref=buf.at[2, 0], dst_ref=buf.at[2, 1], send_sem=sem_s.at[6], recv_sem=sem_r.at[6],
-                                        device_id=net.partner(), device_id_type=MESH)
+    out_ref[own] = value
+    copy = net.pair_copy(out_ref.at[own], out_ref.at[own], sem_s, sem_r, 1)
     copy.start()
     copy.wait()
-    out_ref[...] = value + buf[2, 1]
 
 
 def gelu_tanh(pre_act):
     return jax.nn.gelu(pre_act, approximate=True)
 
 
-def attention_kernel(group_size, qkv_ref, nat_ref, stat_ref, a_ref, send, score, prob, a_nat, a_part, send_sem, recv_sem):
+def attention_kernel(group_size, qkv_ref, dy_ref, nat_ref, stat_ref, a_ref, plane_ref, send, score, prob, a_nat, a_part, send_sem, recv_sem, g_send, g_recv):
     net = Net(group_size)
-    net.pair_barrier()
+    plane_ref[net.row, net.col] = dy_ref[...]
+    net.barrier(True)
+    moves = Gather(net, plane_ref, g_send, g_recv, dy_ref.shape[0]).steps()
     parts, n_blk, _, rows, head = nat_ref.shape
     core, n_plane = net.core, n_blk * rows
     for part in range(parts):
         send[part] = qkv_ref[:, (parts + part) * head:(parts + part + 1) * head].reshape(n_blk, rows, head)
     copies = [net.pair_copy(send, nat_ref.at[:, :, core], send_sem, recv_sem, 0)]
     copies[0].start()
+    next(moves)
     for part in range(parts):
         nat_ref[part, :, core] = qkv_ref[:, part * head:(part + 1) * head].reshape(n_blk, rows, head)
     copies[0].wait_recv()
     step = n_blk // Q_BLOCKS
     n_q = 2 * step * rows
     factor = head ** -0.5 * LOG2E
-    for blk in range(Q_BLOCKS):
+    for blk in reversed(range(Q_BLOCKS)):
         here, upto, left = pl.ds(blk * step, step), (blk + 1) * step, blk * n_q
         size = left + n_q
         score[:, :size] = matmul(nat_ref[0, here].reshape(n_q, head), nat_ref[1, :upto].reshape(size, head), NT)
@@ -412,10 +480,14 @@
         a_nat[here] = attn.reshape(step, 2, rows, head)
         copies.append(net.pair_copy(a_nat.at[here, 1 - core], a_part.at[here], send_sem, recv_sem, 1 + blk))
         copies[-1].start()
+        for _ in range(GATHER_PLAN[Q_BLOCKS - 1 - blk]):
+            next(moves, None)
     a_ref[:, :head] = a_nat[:, core].reshape(n_plane, head)
     for copy in copies[1:]:
         copy.wait_recv()
     a_ref[:, head:] = a_part[...].reshape(n_plane, head)
+    for _ in moves:
+        pass
     for copy in copies:
         copy.wait_send()
 
@@ -425,15 +497,18 @@
     return jnp.where(row >= lax.broadcasted_iota(jnp.int32, vals.shape, 1), vals, -1e30)
 
 
-def attention_back_kernel(group_size, d_ref, nat_ref, stat_ref, dq_ref, send, d_nat, score, d_prob, prob, d_score, dk_acc, dv_acc,
-                          g_nat, g_part, send_sem, recv_sem):
+def attention_back_kernel(first_row, group_size, d_ref, nat_ref, stat_ref, part_ref, res_ref, bias_ref, dq_ref, y_ref, send, d_nat, score, d_prob, prob, d_score, dk_acc, dv_acc,
+                          g_nat, g_part, send_sem, recv_sem, *scratch):
     net = Net(group_size)
-    net.pair_barrier()
+    net.barrier(True)
+    scatter = Scatter(net, part_ref, *scratch, start=first_row)
+    moves = scatter.steps()
     parts, n_blk, _, rows, head = nat_ref.shape
     core, n_plane = net.core, n_blk * rows
     send[...] = d_ref[:, head:].reshape(n_blk, rows, head)
     copies = [net.pair_copy(send, d_nat.at[:, core], send_sem, recv_sem, 0)]
     copies[0].start()
+    next(moves)
     d_nat[:, core] = d_ref[:, :head].reshape(n_blk, rows, head)
     copies[0].wait_recv()
     step = n_blk // Q_BLOCKS
@@ -480,12 +555,16 @@
             g_nat[part, here] = acc[left:size].astype(BF).reshape(step, 2, rows, head)
         copies.append(net.pair_copy(g_nat.at[:, here, 1 - core], g_part.at[:, here], send_sem, recv_sem, 1 + blk))
         copies[-1].start()
+        next(moves, None)
     for part in range(parts):
         dq_ref[:, part * head:(part + 1) * head] = g_nat[part, :, core].reshape(n_plane, head)
     for copy in copies[1:]:
         copy.wait_recv()
     for part in range(parts):
         dq_ref[:, (parts + part) * head:(parts + part + 1) * head] = g_part[part].reshape(n_plane, head)
+    for _ in moves:
+        pass
+    y_ref[...] = (res_ref[...] + scatter.total() + bias_ref[...]).astype(BF)
     for copy in copies:
         copy.wait_send()
 
@@ -510,9 +589,9 @@
         def sums(count):
             return jax.ShapeDtypeStruct((count, width), F32)
 
-        def comm(kernel, ident, args, outs, scratch):
+        def comm(kernel, ident, args, outs, scratch, *static):
             return pl.pallas_call(
-                functools.partial(kernel, group_size), name=kernel.__name__, out_shape=outs,
+                functools.partial(kernel, *static, group_size), name=kernel.__name__, out_shape=outs,
                 in_specs=vmem_specs(len(args)), out_specs=jax.tree.map(lambda _: vmem_specs(1)[0], outs),
                 scratch_shapes=scratch, compiler_params=comm_params(ident))(*args)
 
@@ -522,7 +601,13 @@
         stat_shape = jax.ShapeDtypeStruct((2, n_all, 1), F32)
         pair_sems = [pltpu.SemaphoreType.DMA((1 + Q_BLOCKS,))] * 2
 
-        both_scratch = scatter_scratch(rows, width) + gather_scratch()
+        part_rows = rows // n_layers
+        part_scatter = scatter_scratch(part_rows, width)
+        one_scatter = scatter_scratch(rows, width)
+        both_scratch = one_scatter + gather_scratch()
+
+        def part_slice(layer):
+            return slice(layer * part_rows, (layer + 1) * part_rows)
 
         def swapped(vals):
             return lax.ppermute(vals, 'tp', swap)
@@ -542,13 +627,15 @@
         dy_rows = dy_loc.reshape(rows, width)
         h_plane = comm(first_kernel, 0, [x_rows, ln_par[0, 0:2]], plane, gather_scratch())
         res_one = x_rows.astype(F32)
-        saved = []
+        saved, d_parts, y_parts = [], [], [None] * n_layers
         for layer in range(n_layers):
             h_flat = h_plane.reshape(n_plane, width)
             qkv = matmul(h_flat, wq_both[layer], NN).astype(BF)
-            nat, stat, a_both = comm(attention_kernel, 6, [qkv], (nat_shape, stat_shape, jax.ShapeDtypeStruct((n_plane, 2 * head), BF)), [
+            nat, stat, a_both, dy_part = comm(attention_kernel, 6, [qkv, dy_rows[part_slice(layer)]], (
+                nat_shape, stat_shape, jax.ShapeDtypeStruct((n_plane, 2 * head), BF), jax.ShapeDtypeStruct((side, side, part_rows, width), BF)), [
                 pltpu.VMEM((3,) + block_shape, BF), pltpu.VMEM((n_q, n_all), F32), pltpu.VMEM((n_q, n_all), BF),
-                pltpu.VMEM(nat_shape.shape[1:], BF), pltpu.VMEM(block_shape, BF)] + pair_sems)
+                pltpu.VMEM(nat_shape.shape[1:], BF), pltpu.VMEM(block_shape, BF)] + pair_sems + gather_scratch())
+            d_parts.append(dy_part)
             part = blocks(matmul(a_both, wo_both[layer], NN))
             par = jnp.concatenate([bias_d[layer, 0:1], ln_par[layer, 2:4]], axis=0)
             res_two, h2_plane = comm(forward_kernel, 1, [part, res_one, par], (local_f, plane), both_scratch)
@@ -561,12 +648,16 @@
             if layer + 1 < n_layers:
                 par = jnp.concatenate([bias_d[layer, 1:2], ln_par[layer + 1, 0:2]], axis=0)
                 res_one, h_plane = comm(forward_kernel, 1, [part, res_two, par], (local_f, plane), both_scratch)
-            else:
-                y_rows, top_sum, d_plane = comm(turn_kernel, 2, [part, res_two, bias_d[layer, 1:2], dy_rows],
-                                                (local_b, sums(1), plane), both_scratch)
+
+        top_part, top_res = part, res_two
+        d_plane = jnp.concatenate(d_parts, axis=2)
+        def backward(args, splits, shapes, ident, gathers):
+            outs = [jax.ShapeDtypeStruct(shape, BF) for shape in shapes] + [local_f if gathers else local_b, sums(3)] + [plane] * gathers
+            bufs = [pltpu.VMEM(shape, BF) for shape in shapes for _ in PAIR] + [pltpu.SemaphoreType.DMA((2,))] * 2
+            return comm(backward_kernel, ident, args, tuple(outs), bufs + one_scatter + gather_scratch() * gathers, splits, gathers)
 
         d_res = dy_rows.astype(F32)
-        bias_two = top_sum[0:1]
+        bias_two = jnp.sum(d_res, axis=0, keepdims=True)
         grads = [None] * n_layers
         for layer in reversed(range(n_layers)):
             res_one, h_flat, nat, stat, a_both, res_two, h2_flat, gelu_pull, act = saved[layer]
@@ -576,44 +667,38 @@
             d_pre_bf = d_pre.astype(BF)
             d_bup = jnp.sum(d_pre, axis=0)
             part = blocks(matmul(d_pre_bf, wu_both[layer], NT))
-            d_res, sum_two, da_plane = comm(backward_kernel, 3, [part, res_two, ln_par[layer, 2:3], d_res],
-                                            (local_f, sums(3), plane), both_scratch)
-            d_wdown = matmul(act, d_flat, TN)
-            d_wup = matmul(h2_flat, d_pre_bf, TN)
+            d_wdown, d_wup, d_res, sum_two, da_plane = backward(
+                [part, res_two, ln_par[layer, 2:3], d_res, act, d_flat, h2_flat, d_pre_bf], (True, False),
+                [(n_col, width), (width, n_col)], 3, True)
             da_flat = da_plane.reshape(n_plane, width)
             d_both = matmul(da_flat, wo_both[layer], NT).astype(BF)
-            dq_both = comm(attention_back_kernel, 7, [d_both, nat, stat], jax.ShapeDtypeStruct((n_plane, 6 * head), BF), [
+            dq_both, y_part = comm(attention_back_kernel, 7 + layer, [d_both, nat, stat, top_part, top_res[part_slice(layer)], bias_d[n_layers - 1, 1:2]], (
+                jax.ShapeDtypeStruct((n_plane, 6 * head), BF), jax.ShapeDtypeStruct((part_rows, width), BF)), [
                 pltpu.VMEM(block_shape, BF), pltpu.VMEM(nat_shape.shape[1:], BF), pltpu.VMEM((n_q, n_all), F32),
                 pltpu.VMEM((n_q, n_all), F32), pltpu.VMEM((n_q, n_all), BF), pltpu.VMEM((n_q, n_all), BF),
                 pltpu.VMEM((n_all, head), F32), pltpu.VMEM((n_all, head), F32), pltpu.VMEM(nat_shape.shape, BF),
-                pltpu.VMEM((3,) + block_shape, BF)] + pair_sems)
+                pltpu.VMEM((3,) + block_shape, BF)] + pair_sems + part_scatter, layer * part_rows)
+            y_parts[layer] = y_part
             part = blocks(matmul(dq_both, wq_both[layer], NT))
-            args = [part, res_one, ln_par[layer, 0:1], d_res]
-            d_wout = matmul(a_both, da_flat, TN)
-            d_wqkv = matmul(h_flat, dq_both, TN)
+            args = [part, res_one, ln_par[layer, 0:1], d_res, a_both, da_flat, h_flat, dq_both]
+            shapes = [(head, width), (width, 3 * head)]
             if layer > 0:
-                d_res, sum_one, d_plane = comm(backward_kernel, 3, args, (local_f, sums(3), plane), both_scratch)
-                next_two = sum_one[2:3]
+                d_wout, d_wqkv, d_res, sum_one, d_plane = backward(args, (True, False), shapes, 4, True)
             else:
-                x_grad, sum_one = comm(last_kernel, 4, args, (local_b, sums(2)), scatter_scratch(rows, width))
-                next_two = None
+                d_wout, d_wqkv, x_grad, sum_one = backward(args, (True, False), shapes, 5, False)
+            next_two = sum_one[2:3]
             small = jnp.concatenate([sum_one[0:2], sum_two[0:2], sum_two[2:3], bias_two], axis=0)
             bias_two = next_two
-            grads[layer] = (
-                small,
-                (d_wqkv[:, :3 * head] + swapped(d_wqkv[:, 3 * head:].astype(BF)).astype(F32)).astype(BF),
-                (d_wout[:head] + swapped(d_wout[head:].astype(BF)).astype(F32)).astype(BF),
-                (d_wup[:, :n_col] + swapped(d_wup[:, n_col:].astype(BF)).astype(F32)).astype(BF),
-                d_bup[:n_col] + swapped(d_bup[n_col:]),
-                (d_wdown[:n_col] + swapped(d_wdown[n_col:].astype(BF)).astype(F32)).astype(BF))
+            grads[layer] = (small, d_wqkv, d_wout, d_wup, d_bup[:n_col] + swapped(d_bup[n_col:]), d_wdown)
         n_small = grads[0][0].shape[0]
         packed = jnp.concatenate([grad[0] for grad in grads], axis=0)
-        pad = -packed.shape[0] % 8
+        pad = -packed.shape[0] % 16
         packed = jnp.concatenate([packed, jnp.zeros((pad, width), F32)], axis=0)
-        total = comm(sum_kernel, 5, [packed], sums(packed.shape[0]),
-                     [pltpu.VMEM((3, side) + packed.shape, F32), pltpu.SemaphoreType.DMA((7,)), pltpu.SemaphoreType.DMA((7,))])
+        half_shape = (packed.shape[0] // 2, width)
+        total = comm(sum_kernel, 2, [packed], sums(packed.shape[0]),
+                     [pltpu.VMEM((2, side) + half_shape, F32), pltpu.VMEM(half_shape, F32)] + [pltpu.SemaphoreType.DMA((2 * side,))] * 2)
         total = total[:n_small * n_layers].reshape(n_layers, n_small, width)
-        return (y_rows.reshape(x_loc.shape), x_grad.reshape(x_loc.shape), total[:, :4], total[:, 4:],
+        return (jnp.concatenate(y_parts, axis=0).reshape(x_loc.shape), x_grad.reshape(x_loc.shape), total[:, :4], total[:, 4:],
                 jnp.stack([grad[1].reshape(width, 3, 1, head) for grad in grads]),
                 jnp.stack([grad[2].reshape(1, head, width) for grad in grads]),
                 jnp.stack([grad[3] for grad in grads]),

time: 609 us -> 581 us (0.954)
  matrix products: 70.8 us -> 48.8 us
  Pallas kernels: 491 us -> 473 us
  local copies, waits for them, and re-layouts: 20.9 us -> 31.2 us
    dot_general x24 -> x16, matrix products: 70.8 us -> 48.8 us  [matmul(): lax.dot_general(lhs, rhs, (dims, ((), ())), preferred_element_type=F32)]
    pallas_call x14 -> x13, Pallas kernels: 491 us -> 473 us  [comm(): pl.pallas_call(functools.partial(kernel, *static, group_size), name=kerne...]
    unnamed x59 -> x162, local copies, waits for them, and re-layouts: 10.2 us -> 19.8 us
  transfers between devices with their start and end apart: 15 -> 7, of which waited for: 2 -> 1; matrix products, arithmetic and copies ran while one was open for 4% -> 6% of each run, Pallas kernels for 15% -> 39%
where the time goes in v2:
time: 581 us; the launch traced here: 572 us
  Pallas kernels  473 us (81%)
  matrix products  48.8 us (8%)
  local copies, waits for them, and re-layouts  31.2 us (5%)
  other arithmetic  9.4 us (2%)
  starting transfers between devices  6.63 us (1%)
    pallas_call x13, Pallas kernels, comm(): pl.pallas_call(functools.partial(kernel, *static, group_size), name=kerne...  473 us
    dot_general x16, matrix products, matmul(): lax.dot_general(lhs, rhs, (dims, ((), ())), preferred_element_type=F32)  48.8 us
    unnamed x162, local copies, waits for them, and re-layouts  19.8 us
  transfers between devices with their start and end apart: 7, of which 1 were waited for; matrix products, arithmetic and copies ran while one was open for 6% of the time, Pallas kernels for 39%

profile of v2, /device:TPU:97, one launch (start us, length us, event | category | flops | bytes accessed | tf_op | source)
XLA Modules:
  0.0 571.7 jit_solution(3392958982694124688)
XLA Ops:
  0.6 2.1 collective-permute-start
  4.7 1.5 slice_bitcast_fusion.22
  7.1 1.0 convert_bitcast_fusion.dres_ref
  9.0 1.9 constant_dynamic-update-slice_fusion.1
  12.6 29.3 %first_kernel.1 = bf16[4,4,64,2048]{3,2,1,0:T(8,128)(2,1)S(1)} custom-call(bf16[64,2048]{1,0:T(8,128)(2,1)S(1)} %bitcast.154, f32[2,2048]{1,0:T(2,128)S(1)} %get-tuple-element.107.par_ref), custom_call_target="tpu_custom_call" | custom-call | tf_op jit(solution)/shard_map/first_kernel/pallas_call | solution.py:593
  42.1 2.3 convolution_convert_fusion.9.qkv_ref
  44.4 24.9 %attention_kernel.2 = (bf16[3,16,2,64,64]{4,3,2,1,0:T(8,128)(2,1)S(1)}, f32[2,2048,1]{2,1,0:T(8,128)S(1)}, bf16[1024,128]{1,0:T(8,128)(2,1)S(1)}, bf16[4,4,32,2048]{3,2,1,0:T(8,128)(2,1)S(1)}) custom-call(bf16[1024,384]{1,0:T(8,128)(2,1)S(1)} %convolution_convert_fusion.9.qkv_ref, bf16[32,2048]{1,0:T(8,128)(2,1)S(1)} %get-tuple-element.99.dy_ref), custom_call_target="tpu_custom_call" | custom-call | tf_op jit(solution)/shard_map/attention_kernel/pallas_call | solution.py:593
  69.3 1.3 copy-done.1
  70.6 1.1 copy-done.14
  71.8 1.4 convolution_convert_fusion.7
  73.3 49.2 %forward_kernel.3 = (f32[64,2048]{1,0:T(8,128)S(1)}, bf16[4,4,64,2048]{3,2,1,0:T(8,128)(2,1)S(1)}) custom-call(bf16[4,4,64,2048]{3,2,1,0:T(8,128)(2,1)S(1)} %bitcast.130, f32[64,2048]{1,0:T(8,128)S(1)} %bitcast_convert_fusion.res_ref, f32[3,2048]{1,0:T(4,128)S(1)} %get-tuple-element.120.par_ref), custom_call_target="tpu_custom_call" | custom-call | tf_op jit(solution)/shard_map/forward_kernel/pallas_call | solution.py:593
  122.7 4.0 multiply_convert_fusion.1
  127.7 2.3 convolution_convert_fusion.5
  130.1 47.0 %forward_kernel.4 = (f32[64,2048]{1,0:T(8,128)S(1)}, bf16[4,4,64,2048]{3,2,1,0:T(8,128)(2,1)S(1)}) custom-call(bf16[4,4,64,2048]{3,2,1,0:T(8,128)(2,1)S(1)} %bitcast.153, f32[64,2048]{1,0:T(8,128)S(1)} %get-tuple-element.49.res_ref, f32[3,2048]{1,0:T(4,128)S(1)} %pad_maximum_fusion.7.par_ref), custom_call_target="tpu_custom_call" | custom-call | tf_op jit(solution)/shard_map/forward_kernel/pallas_call | solution.py:593
  177.1 2.6 convolution_convert_fusion.8.qkv_ref
  179.6 28.7 %attention_kernel.3 = (bf16[3,16,2,64,64]{4,3,2,1,0:T(8,128)(2,1)S(1)}, f32[2,2048,1]{2,1,0:T(8,128)S(1)}, bf16[1024,128]{1,0:T(8,128)(2,1)S(1)}, bf16[4,4,32,2048]{3,2,1,0:T(8,128)(2,1)S(1)}) custom-call(bf16[1024,384]{1,0:T(8,128)(2,1)S(1)} %convolution_convert_fusion.8.qkv_ref, bf16[32,2048]{1,0:T(8,128)(2,1)S(1)} %get-tuple-element.98.dy_ref), custom_call_target="tpu_custom_call" | custom-call | tf_op jit(solution)/shard_map/attention_kernel/pallas_call | solution.py:593
  208.4 1.3 copy-done.3
  209.7 1.1 copy-done.16
  210.9 1.2 convolution_convert_fusion.6
  212.1 50.4 %forward_kernel.5 = (f32[64,2048]{1,0:T(8,128)S(1)}, bf16[4,4,64,2048]{3,2,1,0:T(8,128)(2,1)S(1)}) custom-call(bf16[4,4,64,2048]{3,2,1,0:T(8,128)(2,1)S(1)} %bitcast.129, f32[64,2048]{1,0:T(8,128)S(1)} %get-tuple-element.53.res_ref, f32[3,2048]{1,0:T(4,128)S(1)} %get-tuple-element.121.par_ref), custom_call_target="tpu_custom_call" | custom-call | tf_op jit(solution)/shard_map/forward_kernel/pallas_call | solution.py:593
  263.3 4.4 multiply_convert_fusion
  268.3 6.4 %fusion.35 = (f32[512]{0:T(512)}, bf16[1024,512]{1,0:T(8,128)(2,1)S(1)}) fusion(f32[1024,512]{1,0:T(8,128)} %get-tuple-element.118, f32[512]{0:T(512)S(1)} %bitcast.176, bf16[1024,2048]{1,0:T(8,128)(2,1)S(1)} %bitcast.135, bf16[2,512,2048]{2,1,0:T(8,128)(2,1)} %copy-done.61), kind=kOutput, calls=%fused_computation.90 | convolution fusion | flops 2159017472 | bytes 9441280 | tf_op jit(solution)/shard_map/dot_general | solution.py:38
  274.7 6.5 %convolution_convert_fusion.4 = bf16[1024,2048]{1,0:T(8,128)(2,1)} fusion(bf16[1024,512]{1,0:T(8,128)(2,1)S(1)} %get-tuple-element.95.refs_3_, bf16[2,2048,512]{2,1,0:T(8,128)(2,1)} %copy-done.63), kind=kOutput, calls=%fused_computation.5 | convolution fusion | flops 2149580800 | bytes 7340032 | tf_op jit(solution)/shard_map/dot_general | solution.py:38
  281.2 2.4 convolution_convert_fusion.3
  284.3 2.2 copy-done
  286.5 1.0 copy-done.7
  287.6 1.2 copy-done.21
  288.8 49.5 %backward_kernel.4 = (bf16[256,2048]{1,0:T(8,128)(2,1)S(1)}, bf16[2048,256]{1,0:T(8,128)(2,1)S(1)}, f32[64,2048]{1,0:T(8,128)S(1)}, f32[3,2048]{1,0:T(4,128)S(1)}, bf16[4,4,64,2048]{3,2,1,0:T(8,128)(2,1)S(1)}) custom-call(bf16[4,4,64,2048]{3,2,1,0:T(8,128)(2,1)S(1)} %bitcast.150, f32[64,2048]{1,0:T(8,128)S(1)} %copy-done.7, ...), custom_call_target="tpu_custom_call" | custom-call | tf_op jit(solution)/shard_map/backward_kernel/pallas_call | solution.py:593
  338.4 1.3 convolution_convert_fusion.11.d_ref
  339.7 1.0 copy-done.4
  341.1 26.9 %attention_back_kernel.2 = (bf16[1024,384]{1,0:T(8,128)(2,1)S(1)}, bf16[32,2048]{1,0:T(8,128)(2,1)S(1)}) custom-call(bf16[1024,128]{1,0:T(8,128)(2,1)S(1)} %convolution_convert_fusion.11.d_ref, bf16[3,16,2,64,64]{4,3,2,1,0:T(8,128)(2,1)S(1)} %copy-done.17, f32[2,2048,1]{2,1,0:T(8,128)S(1)} %copy-done.4, bf16[4,4,64,2048]{3,2,1,0:T(8,128)(2,1)S(1)} %bitcast.133, ...), custom_call_target="tpu_custom_call" | custom-call | tf_op jit(solution)/shard_map/attention_back_kernel/pallas_call | solution.py:593
  368.0 2.3 convolution_convert_fusion.1
  370.4 49.0 %backward_kernel.5 = (bf16[64,2048]{1,0:T(8,128)(2,1)S(1)}, bf16[2048,192]{1,0:T(8,128)(2,1)S(1)}, f32[64,2048]{1,0:T(8,128)S(1)}, f32[3,2048]{1,0:T(4,128)S(1)}, bf16[4,4,64,2048]{3,2,1,0:T(8,128)(2,1)S(1)}) custom-call(bf16[4,4,64,2048]{3,2,1,0:T(8,128)(2,1)S(1)} %bitcast.152, f32[64,2048]{1,0:T(8,128)S(1)} %get-tuple-element.53.res_ref, ...), custom_call_target="tpu_custom_call" | custom-call | tf_op jit(solution)/shard_map/backward_kernel/pallas_call | solution.py:593
  419.5 5.7 fusion.34
  425.3 2.4 convolution_convert_fusion.2
  428.3 3.3 collective-permute-start.5
  431.6 50.6 %backward_kernel.6 = (bf16[256,2048]{1,0:T(8,128)(2,1)S(1)}, bf16[2048,256]{1,0:T(8,128)(2,1)S(1)}, f32[64,2048]{1,0:T(8,128)S(1)}, f32[3,2048]{1,0:T(4,128)S(1)}, bf16[4,4,64,2048]{3,2,1,0:T(8,128)(2,1)S(1)}) custom-call(bf16[4,4,64,2048]{3,2,1,0:T(8,128)(2,1)S(1)} %bitcast.149, f32[64,2048]{1,0:T(8,128)S(1)} %get-tuple-element.49.res_ref, ...), custom_call_target="tpu_custom_call" | custom-call | tf_op jit(solution)/shard_map/backward_kernel/pallas_call | solution.py:593
  482.3 1.2 convolution_convert_fusion.10.d_ref
  483.6 1.0 copy-done.2
  485.1 26.0 %attention_back_kernel.3 = (bf16[1024,384]{1,0:T(8,128)(2,1)S(1)}, bf16[32,2048]{1,0:T(8,128)(2,1)S(1)}) custom-call(bf16[1024,128]{1,0:T(8,128)(2,1)S(1)} %convolution_convert_fusion.10.d_ref, bf16[3,16,2,64,64]{4,3,2,1,0:T(8,128)(2,1)S(1)} %copy-done.15, f32[2,2048,1]{2,1,0:T(8,128)S(1)} %copy-done.2, bf16[4,4,64,2048]{3,2,1,0:T(8,128)(2,1)S(1)} %bitcast.134, ...), custom_call_target="tpu_custom_call" | custom-call | tf_op jit(solution)/shard_map/attention_back_kernel/pallas_call | solution.py:593
  511.2 2.3 convolution_convert_fusion
  513.5 26.2 %backward_kernel.7 = (bf16[64,2048]{1,0:T(8,128)(2,1)S(1)}, bf16[2048,192]{1,0:T(8,128)(2,1)S(1)}, bf16[64,2048]{1,0:T(8,128)(2,1)S(1)}, f32[3,2048]{1,0:T(4,128)S(1)}) custom-call(bf16[4,4,64,2048]{3,2,1,0:T(8,128)(2,1)S(1)} %bitcast.151, f32[64,2048]{1,0:T(8,128)S(1)} %bitcast_convert_fusion.res_ref, f32[1,2048]{1,0:T(1,128)S(1)} %copy-done.42, ...), custom_call_target="tpu_custom_call" | custom-call | tf_op jit(solution)/shard_map/backward_kernel/pallas_call | solution.py:593
  541.1 1.3 copy.20
  542.4 1.2 copy.21
  544.4 1.5 pad_maximum_fusion.2
  546.7 1.5 pad_maximum_fusion.1
  549.1 1.3 maximum_bitcast_fusion
  552.0 15.5 %sum_kernel.1 = f32[16,2048]{1,0:T(8,128)S(1)} custom-call(f32[16,2048]{1,0:T(8,128)S(1)} %concatenate.43.in_ref), custom_call_target="tpu_custom_call" | custom-call | tf_op jit(solution)/shard_map/sum_kernel/pallas_call | solution.py:593
  (192 shorter events, 19.5 us)
Async XLA Ops:
  0.6 41.4 %collective-permute-start = (bf16[2,2048,192]{1,2,0:T(8,128)(2,1)}, bf16[2,2048,192]{1,2,0:T(8,128)(2,1)S(1)}, u32[]{:S(2)}, u32[]{:S(2)}) collective-permute-start(bf16[2,2048,192]{1,2,0:T(8,128)(2,1)} %bitcast.177), channel_id=1, source_target_pairs={{0,1},{1,0},{2,3},{3,2},{4,5},{5,4},{6,7},{7,6},{8,9},{9,8},{10,11... | collective-permute-start | bytes 4718600 | tf_op jit(solution)/shard_map/ppermute | solution.py:613
  2.8 69.0 %collective-permute-start.1 = (bf16[2,64,2048]{2,1,0:T(8,128)(2,1)}, bf16[2,64,2048]{2,1,0:T(8,128)(2,1)S(1)}, u32[]{:S(2)}, u32[]{:S(2)}) collective-permute-start(bf16[2,64,2048]{2,1,0:T(8,128)(2,1)} %bitcast.165), channel_id=1, source_target_pairs={{0,1},{1,0},{2,3},{3,2},{4,5},{5,4},{6,7},{7,6},{8,9},{9,8},{10,11... | collective-permute-start | bytes 1572872 | tf_op jit(solution)/shard_map/ppermute | solution.py:613
  2.9 119.6 %collective-permute-start.2 = (bf16[2,2048,256]{2,1,0:T(8,128)(2,1)}, bf16[2,2048,256]{2,1,0:T(8,128)(2,1)S(1)}, u32[]{:S(2)}, u32[]{:S(2)}) collective-permute-start(bf16[2,2048,256]{2,1,0:T(8,128)(2,1)} %param.15), channel_id=1, source_target_pairs={{0,1},{1,0},{2,3},{3,2},{4,5},{5,4},{6,7},{7,6},{8,9},{9,8},{10,11... | collective-permute-start | bytes 6291464 | tf_op jit(solution)/shard_map/ppermute | solution.py:613
  3.3 38.7 %collective-permute-start.3 = (f32[2,256]{1,0:T(2,128)}, f32[2,256]{1,0:T(2,128)S(1)}, u32[]{:S(2)}, u32[]{:S(2)}) collective-permute-start(f32[2,256]{1,0:T(2,128)} %param.16), channel_id=1, source_target_pairs={{0,1},{1,0},{2,3},{3,2},{4,5},{5,4},{6,7},{7,6},{8,9},{9,8},{10,11... | collective-permute-start | bytes 6152 | tf_op jit(solution)/shard_map/ppermute | solution.py:613
  3.4 123.3 %collective-permute-start.4 = (bf16[2,256,2048]{2,1,0:T(8,128)(2,1)}, bf16[2,256,2048]{2,1,0:T(8,128)(2,1)S(1)}, u32[]{:S(2)}, u32[]{:S(2)}) collective-permute-start(bf16[2,256,2048]{2,1,0:T(8,128)(2,1)} %param.17), channel_id=1, source_target_pairs={{0,1},{1,0},{2,3},{3,2},{4,5},{5,4},{6,7},{7,6},{8,9},{9,8},{10,11... | collective-permute-start | bytes 6291464 | tf_op jit(solution)/shard_map/ppermute | solution.py:613
  9.0 2.6 copy-start.60
  12.6 29.4 %copy-start.72 = (bf16[2,2048,3,1,64]{1,4,3,2,0:T(8,128)(2,1)S(1)}, bf16[2,2048,3,1,64]{1,4,3,2,0:T(8,128)(2,1)}, u32[]{:S(2)}) copy-start(bf16[2,2048,3,1,64]{1,4,3,2,0:T(8,128)(2,1)} %param.13) | copy-start | bytes 4718596
  42.0 80.6 %copy-start.70 = (f32[1,512]{1,0:T(1,128)}, f32[1,512]{1,0:T(1,128)S(1)}, u32[]{:S(2)}) copy-start(f32[1,512]{1,0:T(1,128)S(1)} %get-tuple-element.113) | copy-start | bytes 6148
  42.0 135.0 %copy-start.75 = (bf16[2,2048,192]{1,2,0:T(8,128)(2,1)}, bf16[2,2048,192]{1,2,0:T(8,128)(2,1)S(1)}, u32[]{:S(2)}) copy-start(bf16[2,2048,192]{1,2,0:T(8,128)(2,1)S(1)} %collective-permute-done) | copy-start | bytes 4718596
  42.1 29.8 %copy-start.54 = (bf16[2,1,64,2048]{3,2,1,0:T(8,128)(2,1)S(1)}, bf16[2,1,64,2048]{3,2,1,0:T(8,128)(2,1)}, u32[]{:S(2)}) copy-start(bf16[2,1,64,2048]{3,2,1,0:T(8,128)(2,1)} %param.14) | copy-start | bytes 1572868
  71.8 139.1 %copy-start.57 = (bf16[2,64,2048]{2,1,0:T(8,128)(2,1)}, bf16[2,64,2048]{2,1,0:T(8,128)(2,1)S(1)}, u32[]{:S(2)}) copy-start(bf16[2,64,2048]{2,1,0:T(8,128)(2,1)S(1)} %collective-permute-done.1) | copy-start | bytes 1572868
  122.7 140.6 %copy-start.63 = (bf16[2,2048,512]{2,1,0:T(8,128)(2,1)}, bf16[2,2048,512]{2,1,0:T(8,128)(2,1)S(1)}, u32[]{:S(2)}) copy-start(bf16[2,2048,512]{2,1,0:T(8,128)(2,1)S(1)} %constant_dynamic-update-slice_fusion) | copy-start | bytes 12582916
  127.0 3.1 copy-start.61
  263.3 4.4 copy-start.9
  274.7 6.5 %copy-start.22 = (bf16[1024,512]{1,0:T(8,128)(2,1)}, bf16[1024,512]{1,0:T(8,128)(2,1)S(1)}, u32[]{:S(2)}) copy-start(bf16[1024,512]{1,0:T(8,128)(2,1)S(1)} %get-tuple-element.95.refs_3_) | copy-start | bytes 3145732
  274.7 6.5 %copy-start.20 = (bf16[1024,512]{1,0:T(8,128)(2,1)S(1)}, bf16[1024,512]{1,0:T(8,128)(2,1)}, u32[]{:S(2)}) copy-start(bf16[1024,512]{1,0:T(8,128)(2,1)} %get-tuple-element.117.refs_0_) | copy-start | bytes 3145732
  274.7 6.5 %copy-start.62 = (bf16[2,512,2048]{2,1,0:T(8,128)(2,1)S(1)}, bf16[2,512,2048]{2,1,0:T(8,128)(2,1)}, u32[]{:S(2)}) copy-start(bf16[2,512,2048]{2,1,0:T(8,128)(2,1)} %copy-done.61) | copy-start | bytes 12582916
  281.2 2.4 copy-start.6
  281.2 3.1 copy-start.23
  288.8 49.5 %copy-start.55 = (bf16[2,1,64,2048]{3,2,1,0:T(8,128)(2,1)S(1)}, bf16[2,1,64,2048]{3,2,1,0:T(8,128)(2,1)}, u32[]{:S(2)}) copy-start(bf16[2,1,64,2048]{3,2,1,0:T(8,128)(2,1)} %param.14) | copy-start | bytes 1572868
  288.8 49.5 %copy-start.58 = (bf16[2,64,2048]{2,1,0:T(8,128)(2,1)S(1)}, bf16[2,64,2048]{2,1,0:T(8,128)(2,1)}, u32[]{:S(2)}) copy-start(bf16[2,64,2048]{2,1,0:T(8,128)(2,1)} %copy-done.57) | copy-start | bytes 1572868
  338.3 2.8 copy-start.17
  341.1 26.9 %copy-start.73 = (bf16[2,2048,3,1,64]{1,4,3,2,0:T(8,128)(2,1)S(1)}, bf16[2,2048,3,1,64]{1,4,3,2,0:T(8,128)(2,1)}, u32[]{:S(2)}) copy-start(bf16[2,2048,3,1,64]{1,4,3,2,0:T(8,128)(2,1)} %param.13) | copy-start | bytes 4718596
  341.1 26.9 %copy-start.76 = (bf16[2,2048,192]{1,2,0:T(8,128)(2,1)S(1)}, bf16[2,2048,192]{1,2,0:T(8,128)(2,1)}, u32[]{:S(2)}) copy-start(bf16[2,2048,192]{1,2,0:T(8,128)(2,1)} %copy-done.75) | copy-start | bytes 4718596
  370.4 49.1 %copy-start.71 = (f32[1,512]{1,0:T(1,128)S(1)}, f32[1,512]{1,0:T(1,128)}, u32[]{:S(2)}) copy-start(f32[1,512]{1,0:T(1,128)} %copy-done.70) | copy-start | bytes 6148
  370.4 49.1 %copy-start.78 = (f32[1024,512]{1,0:T(8,128)S(1)}, f32[1024,512]{1,0:T(8,128)}, u32[]{:S(2)}) copy-start(f32[1024,512]{1,0:T(8,128)} %get-tuple-element.115) | copy-start | bytes 6291460
  419.5 5.8 %copy-start.25 = (bf16[2048,192]{1,0:T(8,128)(2,1)}, bf16[2048,192]{1,0:T(8,128)(2,1)S(1)}, u32[]{:S(2)}) copy-start(bf16[2048,192]{1,0:T(8,128)(2,1)S(1)} %get-tuple-element.76) | copy-start | bytes 2359300
  419.5 5.8 %copy-start.36 = (bf16[64,2048]{1,0:T(8,128)(2,1)}, bf16[64,2048]{1,0:T(8,128)(2,1)S(1)}, u32[]{:S(2)}) copy-start(bf16[64,2048]{1,0:T(8,128)(2,1)S(1)} %get-tuple-element.78) | copy-start | bytes 786436
  419.5 5.8 %copy-start.48 = (f32[3,2048]{1,0:T(4,128)}, f32[3,2048]{1,0:T(4,128)S(1)}, u32[]{:S(2)}) copy-start(f32[3,2048]{1,0:T(4,128)S(1)} %get-tuple-element.73) | copy-start | bytes 73732
  419.5 5.7 %copy-start.64 = (bf16[2,2048,512]{2,1,0:T(8,128)(2,1)S(1)}, bf16[2,2048,512]{2,1,0:T(8,128)(2,1)}, u32[]{:S(2)}) copy-start(bf16[2,2048,512]{2,1,0:T(8,128)(2,1)} %copy-done.63) | copy-start | bytes 12582916
  425.3 2.4 copy-start.67
  425.3 6.3 %copy-start.19 = (bf16[1024,512]{1,0:T(8,128)(2,1)S(1)}, bf16[1024,512]{1,0:T(8,128)(2,1)}, u32[]{:S(2)}) copy-start(bf16[1024,512]{1,0:T(8,128)(2,1)} %copy-done.18) | copy-start | bytes 3145732
  428.3 140.8 %collective-permute-start.5 = (f32[256]{0:T(256)}, f32[256]{0:T(256)}, u32[]{:S(2)}, u32[]{:S(2)}) collective-permute-start(f32[256]{0:T(256)} %slice.164), channel_id=1, source_target_pairs={{0,1},{1,0},{2,3},{3,2},{4,5},{5,4},{6,7},{7,6},{8,9},{9,8},{10,11... | collective-permute-start | bytes 3080 | tf_op jit(solution)/shard_map/ppermute | solution.py:613
  431.6 50.7 %copy-start.56 = (bf16[2,1,64,2048]{3,2,1,0:T(8,128)(2,1)S(1)}, bf16[2,1,64,2048]{3,2,1,0:T(8,128)(2,1)}, u32[]{:S(2)}) copy-start(bf16[2,1,64,2048]{3,2,1,0:T(8,128)(2,1)} %param.14) | copy-start | bytes 1572868
  431.6 50.7 %copy-start.59 = (bf16[2,64,2048]{2,1,0:T(8,128)(2,1)S(1)}, bf16[2,64,2048]{2,1,0:T(8,128)(2,1)}, u32[]{:S(2)}) copy-start(bf16[2,64,2048]{2,1,0:T(8,128)(2,1)} %copy-done.57) | copy-start | bytes 1572868
  482.3 2.8 copy-start.15
  482.3 2.8 copy-start.27
  485.1 26.1 %copy-start.74 = (bf16[2,2048,3,1,64]{1,4,3,2,0:T(8,128)(2,1)S(1)}, bf16[2,2048,3,1,64]{1,4,3,2,0:T(8,128)(2,1)}, u32[]{:S(2)}) copy-start(bf16[2,2048,3,1,64]{1,4,3,2,0:T(8,128)(2,1)} %param.13) | copy-start | bytes 4718596
  485.1 26.1 %copy-start.77 = (bf16[2,2048,192]{1,2,0:T(8,128)(2,1)S(1)}, bf16[2,2048,192]{1,2,0:T(8,128)(2,1)}, u32[]{:S(2)}) copy-start(bf16[2,2048,192]{1,2,0:T(8,128)(2,1)} %copy-done.75) | copy-start | bytes 4718596
  511.1 2.4 copy-start.40
  541.1 3.3 copy-start.31
  549.0 2.8 copy-start.50
  549.0 2.9 copy-start.45
  549.0 2.9 copy-start.47
  549.0 2.9 copy-start.65
  549.1 19.8 %copy-start.66 = (f32[512]{0:T(512)S(1)}, f32[512]{0:T(512)}, u32[]{:S(2)}) copy-start(f32[512]{0:T(512)} %get-tuple-element.94) | copy-start | bytes 6148
  549.1 20.0 %copy-start.68 = (f32[512]{0:T(512)S(1)}, f32[512]{0:T(512)}, u32[]{:S(2)}) copy-start(f32[512]{0:T(512)} %copy-done.67) | copy-start | bytes 6148
  568.9 1.2 collective-permute-start.6
  (38 other events, 59.9 us)

commit v3 on v2

--- a/solution.py
+++ b/solution.py
@@ -31,7 +31,8 @@
 BOTH_ORDER = 'axaaaxaaaaaamccxccxcccc'
 SCATTER_ORDER = 'axaxaaxaaxaaam'
 WORK_CHUNK = 512
-GATHER_PLAN = [1] * Q_BLOCKS
+COST = pl.CostEstimate(flops=20 * 10 ** 9, bytes_accessed=MIB, transcendentals=0)
+GATHER_PLAN = [int(code) for code in '01011111']
 
 
 def matmul(lhs, rhs, dims):
@@ -373,16 +374,68 @@
     exchanged(net, part_ref, h_ref, scratch, middle, iter(PAIR), BOTH_ORDER)
 
 
+class SmallSum:
+    def __init__(self, net):
+        far = range(1, net.side)
+        self.net = net
+        self.devs = [[net.member(net.row, net.shift(net.col, off)) for off in far], [net.member(net.shift(net.row, off), net.col) for off in far]]
+
+    def barrier(self):
+        sem = pltpu.get_barrier_semaphore()
+        everyone = self.devs[0] + self.devs[1] + [self.net.partner()]
+        for dev in everyone:
+            pl.semaphore_signal(sem, inc=1, device_id=dev, device_id_type=MESH)
+        pl.semaphore_wait(sem, len(everyone))
+
+    def run(self, in_ref, out_ref, pair_send, pair_recv, buf, sem_s, sem_r):
+        net = self.net
+        n_half = in_ref.shape[0] // 2
+        own, other = [pl.ds(pl.multiple_of(core * n_half, n_half), n_half) for core in (net.core, 1 - net.core)]
+        pair_send[...] = in_ref[other].astype(BF)
+        copy = net.pair_copy(pair_send, pair_recv, sem_s, sem_r, 0)
+        copy.start()
+        copy.wait()
+        value = in_ref[own] + pair_recv[...].astype(F32)
+        for axis in PAIR:
+            place = net.row if axis else net.col
+            buf[axis, place] = value.astype(BF)
+            copies = []
+            for num, dev in enumerate(self.devs[axis]):
+                ident = 2 + axis * len(self.devs[0]) + num
+                copies.append(pltpu.make_async_remote_copy(
+                    src_ref=buf.at[axis, place], dst_ref=buf.at[axis, place], send_sem=sem_s.at[ident], recv_sem=sem_r.at[ident],
+                    device_id=dev, device_id_type=MESH))
+                copies[-1].start()
+            for copy in copies:
+                copy.wait_recv()
+            value = sum(buf[axis, num].astype(F32) for num in range(net.side))
+            for copy in copies:
+                copy.wait_send()
+        out_ref[own] = value
+        copy = net.pair_copy(out_ref.at[own], out_ref.at[own], sem_s, sem_r, 1)
+        copy.start()
+        copy.wait()
+
+
 def backward_kernel(splits, gathers, group_size, part_ref, res_ref, par_ref, dres_ref, *refs):
     net = Net(group_size)
-    net.barrier(True)
+    small = SmallSum(net)
+    if gathers:
+        net.barrier(True)
+    else:
+        small.barrier()
     work, refs = refs[:4], refs[4:]
+    if not gathers:
+        small_ref, refs = refs[0], refs[1:]
     outs, refs = refs[:2], refs[2:]
     new_ref, sum_ref = refs[:2]
     d_ref = refs[2] if gathers else None
     bufs = refs[3 if gathers else 2:]
     jobs = [(work[2 * num], work[2 * num + 1], split, outs[num], bufs[2 * num], bufs[2 * num + 1]) for num, split in enumerate(splits)]
     send_sem, recv_sem = bufs[4:6]
+    bufs = bufs[6:]
+    if not gathers:
+        stage, small_bufs, bufs = bufs[0], bufs[1:6], bufs[6:]
 
     def middle(total):
         d_vals, d_gain, d_shift = norm_backward(total, res_ref[...], par_ref[0:1])
@@ -390,47 +443,16 @@
         new_ref[...] = new.astype(new_ref.dtype)
         if gathers:
             d_ref[net.row, net.col] = new.astype(BF)
-        sum_ref[0:1] = d_gain
-        sum_ref[1:2] = d_shift
-        sum_ref[2:3] = col_sum(new)
-
-    exchanged(net, part_ref, d_ref, bufs[6:], middle, weight_work(net, jobs, send_sem, recv_sem), BOTH_ORDER if gathers else SCATTER_ORDER)
-
-
-def sum_kernel(group_size, in_ref, out_ref, buf, pair_buf, sem_s, sem_r):
-    net = Net(group_size)
-    sem = pltpu.get_barrier_semaphore()
-    far = range(1, net.side)
-    devs = [[net.member(net.row, net.shift(net.col, off)) for off in far], [net.member(net.shift(net.row, off), net.col) for off in far]]
-    everyone = devs[0] + devs[1] + [net.partner()]
-    for dev in everyone:
-        pl.semaphore_signal(sem, inc=1, device_id=dev, device_id_type=MESH)
-    pl.semaphore_wait(sem, len(everyone))
-    n_half = in_ref.shape[0] // 2
-    own, other = [pl.ds(pl.multiple_of(core * n_half, n_half), n_half) for core in (net.core, 1 - net.core)]
-    copy = net.pair_copy(in_ref.at[other], pair_buf, sem_s, sem_r, 0)
-    copy.start()
-    copy.wait()
-    value = in_ref[own] + pair_buf[...]
-    for axis in PAIR:
-        place = net.row if axis else net.col
-        buf[axis, place] = value
-        copies = []
-        for num, dev in enumerate(devs[axis]):
-            ident = 2 + axis * len(far) + num
-            copies.append(pltpu.make_async_remote_copy(
-                src_ref=buf.at[axis, place], dst_ref=buf.at[axis, place], send_sem=sem_s.at[ident], recv_sem=sem_r.at[ident],
-                device_id=dev, device_id_type=MESH))
-            copies[-1].start()
-        for copy in copies:
-            copy.wait_recv()
-        value = sum(buf[axis, num] for num in range(net.side))
-        for copy in copies:
-            copy.wait_send()
-    out_ref[own] = value
-    copy = net.pair_copy(out_ref.at[own], out_ref.at[own], sem_s, sem_r, 1)
-    copy.start()
-    copy.wait()
+            sum_ref[2:3] = col_sum(new)
+        else:
+            stage[...] = small_ref[...]
+        rows = sum_ref if gathers else stage
+        rows[0:1] = d_gain
+        rows[1:2] = d_shift
+        if not gathers:
+            small.run(stage, sum_ref, *small_bufs)
+
+    exchanged(net, part_ref, d_ref, bufs, middle, weight_work(net, jobs, send_sem, recv_sem), BOTH_ORDER if gathers else SCATTER_ORDER)
 
 
 def gelu_tanh(pre_act):
@@ -593,7 +615,7 @@
             return pl.pallas_call(
                 functools.partial(kernel, *static, group_size), name=kernel.__name__, out_shape=outs,
                 in_specs=vmem_specs(len(args)), out_specs=jax.tree.map(lambda _: vmem_specs(1)[0], outs),
-                scratch_shapes=scratch, compiler_params=comm_params(ident))(*args)
+                scratch_shapes=scratch, compiler_params=comm_params(ident), cost_estimate=COST)(*args)
 
         block_shape = (side * side, rows, head)
         nat_shape = jax.ShapeDtypeStruct((3, side * side, 2, rows, head), BF)
@@ -652,13 +674,19 @@
         top_part, top_res = part, res_two
         d_plane = jnp.concatenate(d_parts, axis=2)
         def backward(args, splits, shapes, ident, gathers):
-            outs = [jax.ShapeDtypeStruct(shape, BF) for shape in shapes] + [local_f if gathers else local_b, sums(3)] + [plane] * gathers
+            outs = [jax.ShapeDtypeStruct(shape, BF) for shape in shapes]
+            outs += [local_f, sums(3), plane] if gathers else [local_b, sums(args[-1].shape[0])]
             bufs = [pltpu.VMEM(shape, BF) for shape in shapes for _ in PAIR] + [pltpu.SemaphoreType.DMA((2,))] * 2
+            if not gathers:
+                count = args[-1].shape[0]
+                half = (count // 2, width)
+                bufs += [pltpu.VMEM((count, width), F32), pltpu.VMEM(half, BF), pltpu.VMEM(half, BF), pltpu.VMEM((2, side) + half, BF)]
+                bufs += [pltpu.SemaphoreType.DMA((2 * side,))] * 2
             return comm(backward_kernel, ident, args, tuple(outs), bufs + one_scatter + gather_scratch() * gathers, splits, gathers)
 
         d_res = dy_rows.astype(F32)
         bias_two = jnp.sum(d_res, axis=0, keepdims=True)
-        grads = [None] * n_layers
+        grads, smalls = [None] * n_layers, []
         for layer in reversed(range(n_layers)):
             res_one, h_flat, nat, stat, a_both, res_two, h2_flat, gelu_pull, act = saved[layer]
             d_flat = d_plane.reshape(n_plane, width)
@@ -682,28 +710,24 @@
             part = blocks(matmul(dq_both, wq_both[layer], NT))
             args = [part, res_one, ln_par[layer, 0:1], d_res, a_both, da_flat, h_flat, dq_both]
             shapes = [(head, width), (width, 3 * head)]
+            others = [sum_two[0:2], sum_two[2:3], bias_two]
             if layer > 0:
                 d_wout, d_wqkv, d_res, sum_one, d_plane = backward(args, (True, False), shapes, 4, True)
+                bias_two = sum_one[2:3]
+                smalls = [sum_one[0:2]] + others + smalls
             else:
-                d_wout, d_wqkv, x_grad, sum_one = backward(args, (True, False), shapes, 5, False)
-            next_two = sum_one[2:3]
-            small = jnp.concatenate([sum_one[0:2], sum_two[0:2], sum_two[2:3], bias_two], axis=0)
-            bias_two = next_two
-            grads[layer] = (small, d_wqkv, d_wout, d_wup, d_bup[:n_col] + swapped(d_bup[n_col:]), d_wdown)
-        n_small = grads[0][0].shape[0]
-        packed = jnp.concatenate([grad[0] for grad in grads], axis=0)
-        pad = -packed.shape[0] % 16
-        packed = jnp.concatenate([packed, jnp.zeros((pad, width), F32)], axis=0)
-        half_shape = (packed.shape[0] // 2, width)
-        total = comm(sum_kernel, 2, [packed], sums(packed.shape[0]),
-                     [pltpu.VMEM((2, side) + half_shape, F32), pltpu.VMEM(half_shape, F32)] + [pltpu.SemaphoreType.DMA((2 * side,))] * 2)
-        total = total[:n_small * n_layers].reshape(n_layers, n_small, width)
+                smalls = [jnp.zeros((2, width), F32)] + others + smalls
+                n_small = sum(piece.shape[0] for piece in smalls)
+                packed = jnp.concatenate(smalls + [jnp.zeros((-n_small % 16, width), F32)], axis=0)
+                d_wout, d_wqkv, x_grad, total = backward(args + [packed], (True, False), shapes, 5, False)
+            grads[layer] = (d_wqkv, d_wout, d_wup, d_bup[:n_col] + swapped(d_bup[n_col:]), d_wdown)
+        total = total[:n_small].reshape(n_layers, n_small // n_layers, width)
         return (jnp.concatenate(y_parts, axis=0).reshape(x_loc.shape), x_grad.reshape(x_loc.shape), total[:, :4], total[:, 4:],
-                jnp.stack([grad[1].reshape(width, 3, 1, head) for grad in grads]),
-                jnp.stack([grad[2].reshape(1, head, width) for grad in grads]),
+                jnp.stack([grad[0].reshape(width, 3, 1, head) for grad in grads]),
+                jnp.stack([grad[1].reshape(1, head, width) for grad in grads]),
+                jnp.stack([grad[2] for grad in grads]),
                 jnp.stack([grad[3] for grad in grads]),
-                jnp.stack([grad[4] for grad in grads]),
-                jnp.stack([grad[5] for grad in grads]))
+                jnp.stack([grad[4] for grad in grads]))
 
     def on_tp(dim, first=None):
         return P(first, *[None] * (dim - 1), 'tp')

time: 581 us -> 553 us (0.952)
  Pallas kernels: 473 us -> 461 us
  matrix products: 48.8 us -> 40.5 us
  local copies, waits for them, and re-layouts: 31.2 us -> 23 us
    pallas_call x13 -> x12, Pallas kernels: 473 us -> 461 us  [comm(): pl.pallas_call(functools.partial(kernel, *static, group_size), name=kerne...]
    dot_general x16, matrix products: 48.8 us -> 40.5 us  [matmul(): lax.dot_general(lhs, rhs, (dims, ((), ())), preferred_element_type=F32)]
    unnamed x162 -> x150, local copies, waits for them, and re-layouts: 19.8 us -> 16.7 us
  transfers between devices with their start and end apart: 7 -> 7, of which waited for: 1 -> 1; matrix products, arithmetic and copies ran while one was open for 6% -> 5% of each run, Pallas kernels for 39% -> 39%
where the time goes in v3:
time: 553 us; the launch traced here: 544 us
  Pallas kernels  461 us (83%)
  matrix products  40.5 us (7%)
  local copies, waits for them, and re-layouts  23 us (4%)
  other arithmetic  9.11 us (2%)
  starting transfers between devices  7.33 us (1%)
    pallas_call x12, Pallas kernels, comm(): pl.pallas_call(functools.partial(kernel, *static, group_size), name=kerne...  461 us
    dot_general x16, matrix products, matmul(): lax.dot_general(lhs, rhs, (dims, ((), ())), preferred_element_type=F32)  40.5 us
    unnamed x150, local copies, waits for them, and re-layouts  16.7 us
  transfers between devices with their start and end apart: 7, of which 1 were waited for; matrix products, arithmetic and copies ran while one was open for 5% of the time, Pallas kernels for 39%

profile of v3, /device:TPU:97, one launch (start us, length us, event | category | flops | bytes accessed | tf_op | source)
XLA Modules:
  0.0 544.3 jit_solution(16459985558178703805)
XLA Ops:
  0.6 2.1 collective-permute-start
  3.8 1.8 constant_dynamic-update-slice_fusion.1
  7.3 29.3 %first_kernel.1 = bf16[4,4,64,2048]{3,2,1,0:T(8,128)(2,1)S(1)} custom-call(bf16[64,2048]{1,0:T(8,128)(2,1)S(1)} %bitcast.137, f32[2,2048]{1,0:T(2,128)S(1)} %get-tuple-element.107.par_ref), custom_call_target="tpu_custom_call" | custom-call | flops 20000000000 | bytes 1048576 | tf_op jit(solution)/shard_map/first_kernel/pallas_call | solution.py:615
  36.9 2.4 convolution_convert_fusion.9.qkv_ref
  39.3 22.3 %attention_kernel.2 = (bf16[3,16,2,64,64]{4,3,2,1,0:T(8,128)(2,1)S(1)}, f32[2,2048,1]{2,1,0:T(8,128)S(1)}, bf16[1024,128]{1,0:T(8,128)(2,1)S(1)}, bf16[4,4,32,2048]{3,2,1,0:T(8,128)(2,1)S(1)}) custom-call(bf16[1024,384]{1,0:T(8,128)(2,1)S(1)} %convolution_convert_fusion.9.qkv_ref, bf16[32,2048]{1,0:T(8,128)(2,1)S(1)} %get-tuple-element.99.dy_ref), custom_call_target="tpu_custom_call" | custom-call | flops 20000000000 | bytes 1048576 | tf_op jit(solution)/shard_map/attention_kernel/pallas_call | solution.py:615
  61.6 1.3 copy-done.35
  63.0 1.4 convolution_convert_fusion.7
  64.5 47.6 %forward_kernel.3 = (f32[64,2048]{1,0:T(8,128)S(1)}, bf16[4,4,64,2048]{3,2,1,0:T(8,128)(2,1)S(1)}) custom-call(bf16[4,4,64,2048]{3,2,1,0:T(8,128)(2,1)S(1)} %bitcast.130, f32[64,2048]{1,0:T(8,128)S(1)} %bitcast_convert_fusion.res_ref, f32[3,2048]{1,0:T(4,128)S(1)} %get-tuple-element.120.par_ref), custom_call_target="tpu_custom_call" | custom-call | flops 20000000000 | bytes 1048576 | tf_op jit(solution)/shard_map/forward_kernel/pallas_call | solution.py:615
  112.3 1.8 copy-done.21
  114.1 4.0 multiply_convert_fusion.1
  118.3 0.8 copy-done.33
  119.1 2.3 convolution_convert_fusion.5
  121.5 43.8 %forward_kernel.4 = (f32[64,2048]{1,0:T(8,128)S(1)}, bf16[4,4,64,2048]{3,2,1,0:T(8,128)(2,1)S(1)}) custom-call(bf16[4,4,64,2048]{3,2,1,0:T(8,128)(2,1)S(1)} %bitcast.162, f32[64,2048]{1,0:T(8,128)S(1)} %get-tuple-element.49.res_ref, f32[3,2048]{1,0:T(4,128)S(1)} %pad_maximum_fusion.7.par_ref), custom_call_target="tpu_custom_call" | custom-call | flops 20000000000 | bytes 1048576 | tf_op jit(solution)/shard_map/forward_kernel/pallas_call | solution.py:615
  165.3 2.6 convolution_convert_fusion.8.qkv_ref
  167.9 28.9 %attention_kernel.3 = (bf16[3,16,2,64,64]{4,3,2,1,0:T(8,128)(2,1)S(1)}, f32[2,2048,1]{2,1,0:T(8,128)S(1)}, bf16[1024,128]{1,0:T(8,128)(2,1)S(1)}, bf16[4,4,32,2048]{3,2,1,0:T(8,128)(2,1)S(1)}) custom-call(bf16[1024,384]{1,0:T(8,128)(2,1)S(1)} %convolution_convert_fusion.8.qkv_ref, bf16[32,2048]{1,0:T(8,128)(2,1)S(1)} %get-tuple-element.98.dy_ref), custom_call_target="tpu_custom_call" | custom-call | flops 20000000000 | bytes 1048576 | tf_op jit(solution)/shard_map/attention_kernel/pallas_call | solution.py:615
  196.8 1.3 copy-done.37
  198.1 1.2 convolution_convert_fusion.6
  199.4 48.8 %forward_kernel.5 = (f32[64,2048]{1,0:T(8,128)S(1)}, bf16[4,4,64,2048]{3,2,1,0:T(8,128)(2,1)S(1)}) custom-call(bf16[4,4,64,2048]{3,2,1,0:T(8,128)(2,1)S(1)} %bitcast.129, f32[64,2048]{1,0:T(8,128)S(1)} %get-tuple-element.53.res_ref, f32[3,2048]{1,0:T(4,128)S(1)} %get-tuple-element.121.par_ref), custom_call_target="tpu_custom_call" | custom-call | flops 20000000000 | bytes 1048576 | tf_op jit(solution)/shard_map/forward_kernel/pallas_call | solution.py:615
  248.2 2.8 multiply_convert_fusion
  251.6 4.2 fusion.35
  255.8 2.4 convolution_convert_fusion.4
  258.3 2.4 convolution_convert_fusion.3
  260.7 51.2 %backward_kernel.4 = (bf16[256,2048]{1,0:T(8,128)(2,1)S(1)}, bf16[2048,256]{1,0:T(8,128)(2,1)S(1)}, f32[64,2048]{1,0:T(8,128)S(1)}, f32[3,2048]{1,0:T(4,128)S(1)}, bf16[4,4,64,2048]{3,2,1,0:T(8,128)(2,1)S(1)}) custom-call(bf16[4,4,64,2048]{3,2,1,0:T(8,128)(2,1)S(1)} %bitcast.159, f32[64,2048]{1,0:T(8,128)S(1)} %get-tuple-element.55.res_ref, ...), custom_call_target="tpu_custom_call" | custom-call | flops 20000000000 | bytes 1048576 | tf_op jit(solution)/shard_map/backward_kernel/pallas_call | solution.py:615
  312.0 1.3 convolution_convert_fusion.11.d_ref
  314.4 25.9 %attention_back_kernel.2 = (bf16[1024,384]{1,0:T(8,128)(2,1)S(1)}, bf16[32,2048]{1,0:T(8,128)(2,1)S(1)}) custom-call(bf16[1024,128]{1,0:T(8,128)(2,1)S(1)} %convolution_convert_fusion.11.d_ref, bf16[3,16,2,64,64]{4,3,2,1,0:T(8,128)(2,1)S(1)} %copy-done.42, f32[2,2048,1]{2,1,0:T(8,128)S(1)} %copy-done.38, bf16[4,4,64,2048]{3,2,1,0:T(8,128)(2,1)S(1)} %bitcast.146, ...), custom_call_target="tpu_custom_call" | custom-call | flops 20000000000 | bytes 1048576 | tf_op jit(solution)/shard_map/attention_back_kernel/pallas_call | solution.py:615
  340.3 2.4 convolution_convert_fusion.1
  342.8 50.3 %backward_kernel.5 = (bf16[64,2048]{1,0:T(8,128)(2,1)S(1)}, bf16[2048,192]{1,0:T(8,128)(2,1)S(1)}, f32[64,2048]{1,0:T(8,128)S(1)}, f32[3,2048]{1,0:T(4,128)S(1)}, bf16[4,4,64,2048]{3,2,1,0:T(8,128)(2,1)S(1)}) custom-call(bf16[4,4,64,2048]{3,2,1,0:T(8,128)(2,1)S(1)} %bitcast.161, f32[64,2048]{1,0:T(8,128)S(1)} %copy-done.48, ...), custom_call_target="tpu_custom_call" | custom-call | flops 20000000000 | bytes 1048576 | tf_op jit(solution)/shard_map/backward_kernel/pallas_call | solution.py:615
  393.1 3.6 fusion.34
  396.8 2.4 convolution_convert_fusion.2
  399.8 4.0 collective-permute-start.5
  403.8 49.8 %backward_kernel.6 = (bf16[256,2048]{1,0:T(8,128)(2,1)S(1)}, bf16[2048,256]{1,0:T(8,128)(2,1)S(1)}, f32[64,2048]{1,0:T(8,128)S(1)}, f32[3,2048]{1,0:T(4,128)S(1)}, bf16[4,4,64,2048]{3,2,1,0:T(8,128)(2,1)S(1)}) custom-call(bf16[4,4,64,2048]{3,2,1,0:T(8,128)(2,1)S(1)} %bitcast.158, f32[64,2048]{1,0:T(8,128)S(1)} %copy-done.44, ...), custom_call_target="tpu_custom_call" | custom-call | flops 20000000000 | bytes 1048576 | tf_op jit(solution)/shard_map/backward_kernel/pallas_call | solution.py:615
  453.7 1.3 convolution_convert_fusion.10.d_ref
  455.0 1.8 copy-done.27
  457.1 1.2 copy-done.24
  459.0 25.1 %attention_back_kernel.3 = (bf16[1024,384]{1,0:T(8,128)(2,1)S(1)}, bf16[32,2048]{1,0:T(8,128)(2,1)S(1)}) custom-call(bf16[1024,128]{1,0:T(8,128)(2,1)S(1)} %convolution_convert_fusion.10.d_ref, bf16[3,16,2,64,64]{4,3,2,1,0:T(8,128)(2,1)S(1)} %copy-done.40, f32[2,2048,1]{2,1,0:T(8,128)S(1)} %copy-done.36, bf16[4,4,64,2048]{3,2,1,0:T(8,128)(2,1)S(1)} %bitcast.147, ...), custom_call_target="tpu_custom_call" | custom-call | flops 20000000000 | bytes 1048576 | tf_op jit(solution)/shard_map/attention_back_kernel/pallas_call | solution.py:615
  484.7 1.5 concatenate.43.refs_4_
  486.2 3.9 convolution_convert_fusion
  490.4 1.1 copy-done.32
  491.6 38.1 %backward_kernel.7 = (bf16[64,2048]{1,0:T(8,128)(2,1)S(1)}, bf16[2048,192]{1,0:T(8,128)(2,1)S(1)}, bf16[64,2048]{1,0:T(8,128)(2,1)S(1)}, f32[16,2048]{1,0:T(8,128)S(1)}) custom-call(bf16[4,4,64,2048]{3,2,1,0:T(8,128)(2,1)S(1)} %bitcast.160, f32[64,2048]{1,0:T(8,128)S(1)} %copy-done.8, f32[1,2048]{1,0:T(1,128)S(1)} %get-tuple-element.100.par_ref, ...), custom_call_target="tpu_custom_call" | custom-call | flops 20000000000 | bytes 1048576 | tf_op jit(solution)/shard_map/backward_kernel/pallas_call | solution.py:615
  530.4 1.3 copy.20
  531.7 1.2 copy.21
  532.9 2.8 pad_maximum_fusion.2
  535.8 1.5 pad_maximum_fusion.1
  537.3 0.8 pad_maximum_fusion.5
  538.2 1.3 maximum_bitcast_fusion
  539.4 0.7 maximum_bitcast_fusion.1
  541.6 1.0 collective-permute-done.6
  543.2 0.7 copy.27
  (179 shorter events, 10.3 us)
Async XLA Ops:
  0.6 36.2 %collective-permute-start = (bf16[2,2048,192]{1,2,0:T(8,128)(2,1)}, bf16[2,2048,192]{1,2,0:T(8,128)(2,1)S(1)}, u32[]{:S(2)}, u32[]{:S(2)}) collective-permute-start(bf16[2,2048,192]{1,2,0:T(8,128)(2,1)} %bitcast.177), channel_id=1, source_target_pairs={{0,1},{1,0},{2,3},{3,2},{4,5},{5,4},{6,7},{7,6},{8,9},{9,8},{10,11... | collective-permute-start | bytes 4718600 | tf_op jit(solution)/shard_map/ppermute | solution.py:635
  2.8 2.8 copy-start.58
  2.8 60.2 %collective-permute-start.1 = (bf16[2,64,2048]{2,1,0:T(8,128)(2,1)}, bf16[2,64,2048]{2,1,0:T(8,128)(2,1)S(1)}, u32[]{:S(2)}, u32[]{:S(2)}) collective-permute-start(bf16[2,64,2048]{2,1,0:T(8,128)(2,1)} %bitcast.165), channel_id=1, source_target_pairs={{0,1},{1,0},{2,3},{3,2},{4,5},{5,4},{6,7},{7,6},{8,9},{9,8},{10,11... | collective-permute-start | bytes 1572872 | tf_op jit(solution)/shard_map/ppermute | solution.py:635
  2.9 109.2 %collective-permute-start.2 = (bf16[2,2048,256]{2,1,0:T(8,128)(2,1)}, bf16[2,2048,256]{2,1,0:T(8,128)(2,1)S(1)}, u32[]{:S(2)}, u32[]{:S(2)}) collective-permute-start(bf16[2,2048,256]{2,1,0:T(8,128)(2,1)} %param.15), channel_id=1, source_target_pairs={{0,1},{1,0},{2,3},{3,2},{4,5},{5,4},{6,7},{7,6},{8,9},{9,8},{10,11... | collective-permute-start | bytes 6291464 | tf_op jit(solution)/shard_map/ppermute | solution.py:635
  3.3 33.6 %collective-permute-start.3 = (f32[2,256]{1,0:T(2,128)}, f32[2,256]{1,0:T(2,128)S(1)}, u32[]{:S(2)}, u32[]{:S(2)}) collective-permute-start(f32[2,256]{1,0:T(2,128)} %param.16), channel_id=1, source_target_pairs={{0,1},{1,0},{2,3},{3,2},{4,5},{5,4},{6,7},{7,6},{8,9},{9,8},{10,11... | collective-permute-start | bytes 6152 | tf_op jit(solution)/shard_map/ppermute | solution.py:635
  3.4 114.7 %collective-permute-start.4 = (bf16[2,256,2048]{2,1,0:T(8,128)(2,1)}, bf16[2,256,2048]{2,1,0:T(8,128)(2,1)S(1)}, u32[]{:S(2)}, u32[]{:S(2)}) collective-permute-start(bf16[2,256,2048]{2,1,0:T(8,128)(2,1)} %param.17), channel_id=1, source_target_pairs={{0,1},{1,0},{2,3},{3,2},{4,5},{5,4},{6,7},{7,6},{8,9},{9,8},{10,11... | collective-permute-start | bytes 6291464 | tf_op jit(solution)/shard_map/ppermute | solution.py:635
  7.3 29.6 %copy-start.67 = (f32[2,256]{1,0:T(2,128)S(1)}, f32[2,256]{1,0:T(2,128)}, u32[]{:S(2)}) copy-start(f32[2,256]{1,0:T(2,128)} %param.16) | copy-start | bytes 6148
  7.3 29.6 %copy-start.70 = (bf16[2,2048,3,1,64]{1,4,3,2,0:T(8,128)(2,1)S(1)}, bf16[2,2048,3,1,64]{1,4,3,2,0:T(8,128)(2,1)}, u32[]{:S(2)}) copy-start(bf16[2,2048,3,1,64]{1,4,3,2,0:T(8,128)(2,1)} %param.13) | copy-start | bytes 4718596
  36.8 27.7 %copy-start.7 = (f32[64,2048]{1,0:T(8,128)}, f32[64,2048]{1,0:T(8,128)S(1)}, u32[]{:S(2)}) copy-start(f32[64,2048]{1,0:T(8,128)S(1)} %bitcast_convert_fusion.res_ref) | copy-start | bytes 1572868
  36.9 75.4 %copy-start.68 = (f32[1,512]{1,0:T(1,128)}, f32[1,512]{1,0:T(1,128)S(1)}, u32[]{:S(2)}) copy-start(f32[1,512]{1,0:T(1,128)S(1)} %get-tuple-element.113) | copy-start | bytes 6148
  36.9 303.4 %copy-start.71 = (bf16[2,2048,192]{1,2,0:T(8,128)(2,1)}, bf16[2,2048,192]{1,2,0:T(8,128)(2,1)S(1)}, u32[]{:S(2)}) copy-start(bf16[2,2048,192]{1,2,0:T(8,128)(2,1)S(1)} %collective-permute-done) | copy-start | bytes 4718596
  39.3 23.7 %copy-start.52 = (bf16[2,1,64,2048]{3,2,1,0:T(8,128)(2,1)S(1)}, bf16[2,1,64,2048]{3,2,1,0:T(8,128)(2,1)}, u32[]{:S(2)}) copy-start(bf16[2,1,64,2048]{3,2,1,0:T(8,128)(2,1)} %param.14) | copy-start | bytes 1572868
  63.0 135.2 %copy-start.55 = (bf16[2,64,2048]{2,1,0:T(8,128)(2,1)}, bf16[2,64,2048]{2,1,0:T(8,128)(2,1)S(1)}, u32[]{:S(2)}) copy-start(bf16[2,64,2048]{2,1,0:T(8,128)(2,1)S(1)} %collective-permute-done.1) | copy-start | bytes 1572868
  112.1 9.4 %copy-start.43 = (f32[64,2048]{1,0:T(8,128)}, f32[64,2048]{1,0:T(8,128)S(1)}, u32[]{:S(2)}) copy-start(f32[64,2048]{1,0:T(8,128)S(1)} %get-tuple-element.49.res_ref) | copy-start | bytes 1572868
  112.3 143.5 %copy-start.61 = (bf16[2,2048,512]{2,1,0:T(8,128)(2,1)}, bf16[2,2048,512]{2,1,0:T(8,128)(2,1)S(1)}, u32[]{:S(2)}) copy-start(bf16[2,2048,512]{2,1,0:T(8,128)(2,1)S(1)} %constant_dynamic-update-slice_fusion) | copy-start | bytes 12582916
  118.3 140.0 %copy-start.59 = (bf16[2,512,2048]{2,1,0:T(8,128)(2,1)}, bf16[2,512,2048]{2,1,0:T(8,128)(2,1)S(1)}, u32[]{:S(2)}) copy-start(bf16[2,512,2048]{2,1,0:T(8,128)(2,1)S(1)} %constant_dynamic-update-slice_fusion.4) | copy-start | bytes 12582916
  165.3 34.1 %copy-start.47 = (f32[64,2048]{1,0:T(8,128)}, f32[64,2048]{1,0:T(8,128)S(1)}, u32[]{:S(2)}) copy-start(f32[64,2048]{1,0:T(8,128)S(1)} %get-tuple-element.53.res_ref) | copy-start | bytes 1572868
  248.2 2.8 copy-start.29
  260.6 52.6 %copy-start.23 = (bf16[1024,2048]{1,0:T(8,128)(2,1)}, bf16[1024,2048]{1,0:T(8,128)(2,1)S(1)}, u32[]{:S(2)}) copy-start(bf16[1024,2048]{1,0:T(8,128)(2,1)S(1)} %convolution_convert_fusion.3) | copy-start | bytes 12582916
  260.7 51.2 %copy-start.53 = (bf16[2,1,64,2048]{3,2,1,0:T(8,128)(2,1)S(1)}, bf16[2,1,64,2048]{3,2,1,0:T(8,128)(2,1)}, u32[]{:S(2)}) copy-start(bf16[2,1,64,2048]{3,2,1,0:T(8,128)(2,1)} %param.14) | copy-start | bytes 1572868
  260.7 51.2 %copy-start.56 = (bf16[2,64,2048]{2,1,0:T(8,128)(2,1)S(1)}, bf16[2,64,2048]{2,1,0:T(8,128)(2,1)}, u32[]{:S(2)}) copy-start(bf16[2,64,2048]{2,1,0:T(8,128)(2,1)} %copy-done.55) | copy-start | bytes 1572868
  342.7 50.4 %copy-start.60 = (bf16[2,512,2048]{2,1,0:T(8,128)(2,1)S(1)}, bf16[2,512,2048]{2,1,0:T(8,128)(2,1)}, u32[]{:S(2)}) copy-start(bf16[2,512,2048]{2,1,0:T(8,128)(2,1)} %copy-done.59) | copy-start | bytes 12582916
  342.7 50.4 %copy-start.69 = (f32[1,512]{1,0:T(1,128)S(1)}, f32[1,512]{1,0:T(1,128)}, u32[]{:S(2)}) copy-start(f32[1,512]{1,0:T(1,128)} %copy-done.68) | copy-start | bytes 6148
  342.7 50.4 %copy-start.72 = (f32[1024,512]{1,0:T(8,128)S(1)}, f32[1024,512]{1,0:T(8,128)}, u32[]{:S(2)}) copy-start(f32[1024,512]{1,0:T(8,128)} %get-tuple-element.115) | copy-start | bytes 6291460
  393.1 3.7 copy-start.10
  393.1 3.6 copy-start.62
  396.8 7.0 %copy-start.22 = (bf16[4,4,64,2048]{3,2,1,0:T(8,128)(2,1)S(1)}, bf16[4,4,64,2048]{3,2,1,0:T(8,128)(2,1)}, u32[]{:S(2)}) copy-start(bf16[4,4,64,2048]{3,2,1,0:T(8,128)(2,1)} %copy-done.21) | copy-start | bytes 12582916
  396.8 7.0 %copy-start.34 = (bf16[1024,512]{1,0:T(8,128)(2,1)S(1)}, bf16[1024,512]{1,0:T(8,128)(2,1)}, u32[]{:S(2)}) copy-start(bf16[1024,512]{1,0:T(8,128)(2,1)} %copy-done.33) | copy-start | bytes 3145732
  396.8 7.0 %copy-start.44 = (f32[64,2048]{1,0:T(8,128)S(1)}, f32[64,2048]{1,0:T(8,128)}, u32[]{:S(2)}) copy-start(f32[64,2048]{1,0:T(8,128)} %copy-done.43) | copy-start | bytes 1572868
  399.8 141.8 %collective-permute-start.5 = (f32[256]{0:T(256)}, f32[256]{0:T(256)S(1)}, u32[]{:S(2)}, u32[]{:S(2)}) collective-permute-start(f32[256]{0:T(256)} %slice.160), channel_id=1, source_target_pairs={{0,1},{1,0},{2,3},{3,2},{4,5},{5,4},{6,7},{7,6},{8,9},{9,8},{10,11... | collective-permute-start | bytes 3080 | tf_op jit(solution)/shard_map/ppermute | solution.py:635
  403.8 49.9 %copy-start.54 = (bf16[2,1,64,2048]{3,2,1,0:T(8,128)(2,1)S(1)}, bf16[2,1,64,2048]{3,2,1,0:T(8,128)(2,1)}, u32[]{:S(2)}) copy-start(bf16[2,1,64,2048]{3,2,1,0:T(8,128)(2,1)} %param.14) | copy-start | bytes 1572868
  403.8 49.9 %copy-start.57 = (bf16[2,64,2048]{2,1,0:T(8,128)(2,1)S(1)}, bf16[2,64,2048]{2,1,0:T(8,128)(2,1)}, u32[]{:S(2)}) copy-start(bf16[2,64,2048]{2,1,0:T(8,128)(2,1)} %copy-done.55) | copy-start | bytes 1572868
  403.8 53.2 %copy-start.40 = (bf16[3,16,2,64,64]{4,3,2,1,0:T(8,128)(2,1)S(1)}, bf16[3,16,2,64,64]{4,3,2,1,0:T(8,128)(2,1)}, u32[]{:S(2)}) copy-start(bf16[3,16,2,64,64]{4,3,2,1,0:T(8,128)(2,1)} %copy-done.39) | copy-start | bytes 2359300
  453.7 3.2 copy-start.27
  453.7 3.4 copy-start.45
  453.7 4.6 copy-start.24
  453.7 5.2 copy-start.36
  459.0 25.8 %copy-start.64 = (f32[2048]{0:T(1024)S(1)}, f32[2048]{0:T(1024)}, u32[]{:S(2)}) copy-start(f32[2048]{0:T(1024)} %convert_reduce_fusion) | copy-start | bytes 24580
  484.7 5.4 copy-start.31
  486.2 3.9 copy-start.6
  486.2 3.9 copy-start.8
  486.2 3.9 copy-start.14
  486.2 3.9 copy-start.20
  486.2 4.2 copy-start.28
  486.2 4.2 copy-start.46
  532.9 2.8 copy-start.3
  538.2 3.3 copy-start.66
  541.5 1.2 collective-permute-start.6
  (32 other events, 54.1 us)

commit v4 on v3

--- a/solution.py
+++ b/solution.py
@@ -28,8 +28,8 @@
 ROW_UNROLL = 4
 BACK_UNROLL = 2
 LOG2E = math.log2(math.e)
-BOTH_ORDER = 'axaaaxaaaaaamccxccxcccc'
-SCATTER_ORDER = 'axaxaaxaaxaaam'
+BOTH_ORDER = 'axaaaxaaaaaamccdxccxcccc'
+SCATTER_ORDER = 'axaxaaxaaxaaamd'
 WORK_CHUNK = 512
 COST = pl.CostEstimate(flops=20 * 10 ** 9, bytes_accessed=MIB, transcendentals=0)
 GATHER_PLAN = [int(code) for code in '01011111']
@@ -249,6 +249,8 @@
             for sub in PAIR:
                 rows = pl.ds(sub * self.quarter, self.quarter)
                 self.last[half, rows] = self.last[half, rows] + self.arrived(half, last, sub)
+
+    def drain(self):
         for copy in self.sent:
             copy.wait_send()
 
@@ -267,6 +269,8 @@
             for _ in tasks['a']:
                 pass
             middle(scatter.total())
+        elif code == 'd':
+            scatter.drain()
         else:
             next(tasks[code], None)
     for task in tasks.values():
@@ -586,6 +590,7 @@
         dq_ref[:, (parts + part) * head:(parts + part + 1) * head] = g_part[part].reshape(n_plane, head)
     for _ in moves:
         pass
+    scatter.drain()
     y_ref[...] = (res_ref[...] + scatter.total() + bias_ref[...]).astype(BF)
     for copy in copies:
         copy.wait_send()

time: 553 us -> 553 us (level)
  no operation moved by 1% of the time
where the time goes in v4:
time: 553 us; the launch traced here: 544 us
  Pallas kernels  461 us (83%)
  matrix products  40.5 us (7%)
  local copies, waits for them, and re-layouts  23 us (4%)
  other arithmetic  9.11 us (2%)
  starting transfers between devices  7.31 us (1%)
    pallas_call x12, Pallas kernels, comm(): pl.pallas_call(functools.partial(kernel, *static, group_size), name=kerne...  461 us
    dot_general x16, matrix products, matmul(): lax.dot_general(lhs, rhs, (dims, ((), ())), preferred_element_type=F32)  40.5 us
    unnamed x150, local copies, waits for them, and re-layouts  16.7 us
  transfers between devices with their start and end apart: 7, of which 1 were waited for; matrix products, arithmetic and copies ran while one was open for 5% of the time, Pallas kernels for 39%

profile of v4, /device:TPU:97, one launch (start us, length us, event | category | flops | bytes accessed | tf_op | source)
XLA Modules:
  0.0 543.7 jit_solution(3898751631496282098)
XLA Ops:
  0.6 2.1 collective-permute-start
  3.8 1.8 constant_dynamic-update-slice_fusion.1
  7.3 29.3 %first_kernel.1 = bf16[4,4,64,2048]{3,2,1,0:T(8,128)(2,1)S(1)} custom-call(bf16[64,2048]{1,0:T(8,128)(2,1)S(1)} %bitcast.137, f32[2,2048]{1,0:T(2,128)S(1)} %get-tuple-element.107.par_ref), custom_call_target="tpu_custom_call" | custom-call | flops 20000000000 | bytes 1048576 | tf_op jit(solution)/shard_map/first_kernel/pallas_call | solution.py:620
  36.9 2.4 convolution_convert_fusion.9.qkv_ref
  39.3 22.3 %attention_kernel.2 = (bf16[3,16,2,64,64]{4,3,2,1,0:T(8,128)(2,1)S(1)}, f32[2,2048,1]{2,1,0:T(8,128)S(1)}, bf16[1024,128]{1,0:T(8,128)(2,1)S(1)}, bf16[4,4,32,2048]{3,2,1,0:T(8,128)(2,1)S(1)}) custom-call(bf16[1024,384]{1,0:T(8,128)(2,1)S(1)} %convolution_convert_fusion.9.qkv_ref, bf16[32,2048]{1,0:T(8,128)(2,1)S(1)} %get-tuple-element.99.dy_ref), custom_call_target="tpu_custom_call" | custom-call | flops 20000000000 | bytes 1048576 | tf_op jit(solution)/shard_map/attention_kernel/pallas_call | solution.py:620
  61.6 1.3 copy-done.35
  63.0 1.4 convolution_convert_fusion.7
  64.5 47.2 %forward_kernel.3 = (f32[64,2048]{1,0:T(8,128)S(1)}, bf16[4,4,64,2048]{3,2,1,0:T(8,128)(2,1)S(1)}) custom-call(bf16[4,4,64,2048]{3,2,1,0:T(8,128)(2,1)S(1)} %bitcast.130, f32[64,2048]{1,0:T(8,128)S(1)} %bitcast_convert_fusion.res_ref, f32[3,2048]{1,0:T(4,128)S(1)} %get-tuple-element.120.par_ref), custom_call_target="tpu_custom_call" | custom-call | flops 20000000000 | bytes 1048576 | tf_op jit(solution)/shard_map/forward_kernel/pallas_call | solution.py:620
  111.9 1.8 copy-done.21
  113.7 4.0 multiply_convert_fusion.1
  117.9 0.8 copy-done.33
  118.7 2.3 convolution_convert_fusion.5
  121.1 43.1 %forward_kernel.4 = (f32[64,2048]{1,0:T(8,128)S(1)}, bf16[4,4,64,2048]{3,2,1,0:T(8,128)(2,1)S(1)}) custom-call(bf16[4,4,64,2048]{3,2,1,0:T(8,128)(2,1)S(1)} %bitcast.162, f32[64,2048]{1,0:T(8,128)S(1)} %get-tuple-element.49.res_ref, f32[3,2048]{1,0:T(4,128)S(1)} %pad_maximum_fusion.7.par_ref), custom_call_target="tpu_custom_call" | custom-call | flops 20000000000 | bytes 1048576 | tf_op jit(solution)/shard_map/forward_kernel/pallas_call | solution.py:620
  164.2 2.6 convolution_convert_fusion.8.qkv_ref
  166.8 29.4 %attention_kernel.3 = (bf16[3,16,2,64,64]{4,3,2,1,0:T(8,128)(2,1)S(1)}, f32[2,2048,1]{2,1,0:T(8,128)S(1)}, bf16[1024,128]{1,0:T(8,128)(2,1)S(1)}, bf16[4,4,32,2048]{3,2,1,0:T(8,128)(2,1)S(1)}) custom-call(bf16[1024,384]{1,0:T(8,128)(2,1)S(1)} %convolution_convert_fusion.8.qkv_ref, bf16[32,2048]{1,0:T(8,128)(2,1)S(1)} %get-tuple-element.98.dy_ref), custom_call_target="tpu_custom_call" | custom-call | flops 20000000000 | bytes 1048576 | tf_op jit(solution)/shard_map/attention_kernel/pallas_call | solution.py:620
  196.2 1.3 copy-done.37
  197.6 1.2 convolution_convert_fusion.6
  198.8 47.9 %forward_kernel.5 = (f32[64,2048]{1,0:T(8,128)S(1)}, bf16[4,4,64,2048]{3,2,1,0:T(8,128)(2,1)S(1)}) custom-call(bf16[4,4,64,2048]{3,2,1,0:T(8,128)(2,1)S(1)} %bitcast.129, f32[64,2048]{1,0:T(8,128)S(1)} %get-tuple-element.53.res_ref, f32[3,2048]{1,0:T(4,128)S(1)} %get-tuple-element.121.par_ref), custom_call_target="tpu_custom_call" | custom-call | flops 20000000000 | bytes 1048576 | tf_op jit(solution)/shard_map/forward_kernel/pallas_call | solution.py:620
  246.8 2.8 multiply_convert_fusion
  250.2 4.2 fusion.35
  254.4 2.4 convolution_convert_fusion.4
  256.8 2.4 convolution_convert_fusion.3
  259.3 52.9 %backward_kernel.4 = (bf16[256,2048]{1,0:T(8,128)(2,1)S(1)}, bf16[2048,256]{1,0:T(8,128)(2,1)S(1)}, f32[64,2048]{1,0:T(8,128)S(1)}, f32[3,2048]{1,0:T(4,128)S(1)}, bf16[4,4,64,2048]{3,2,1,0:T(8,128)(2,1)S(1)}) custom-call(bf16[4,4,64,2048]{3,2,1,0:T(8,128)(2,1)S(1)} %bitcast.159, f32[64,2048]{1,0:T(8,128)S(1)} %get-tuple-element.55.res_ref, ...), custom_call_target="tpu_custom_call" | custom-call | flops 20000000000 | bytes 1048576 | tf_op jit(solution)/shard_map/backward_kernel/pallas_call | solution.py:620
  312.3 1.3 convolution_convert_fusion.11.d_ref
  314.7 25.3 %attention_back_kernel.2 = (bf16[1024,384]{1,0:T(8,128)(2,1)S(1)}, bf16[32,2048]{1,0:T(8,128)(2,1)S(1)}) custom-call(bf16[1024,128]{1,0:T(8,128)(2,1)S(1)} %convolution_convert_fusion.11.d_ref, bf16[3,16,2,64,64]{4,3,2,1,0:T(8,128)(2,1)S(1)} %copy-done.42, f32[2,2048,1]{2,1,0:T(8,128)S(1)} %copy-done.38, bf16[4,4,64,2048]{3,2,1,0:T(8,128)(2,1)S(1)} %bitcast.146, ...), custom_call_target="tpu_custom_call" | custom-call | flops 20000000000 | bytes 1048576 | tf_op jit(solution)/shard_map/attention_back_kernel/pallas_call | solution.py:620
  340.0 2.4 convolution_convert_fusion.1
  342.4 50.2 %backward_kernel.5 = (bf16[64,2048]{1,0:T(8,128)(2,1)S(1)}, bf16[2048,192]{1,0:T(8,128)(2,1)S(1)}, f32[64,2048]{1,0:T(8,128)S(1)}, f32[3,2048]{1,0:T(4,128)S(1)}, bf16[4,4,64,2048]{3,2,1,0:T(8,128)(2,1)S(1)}) custom-call(bf16[4,4,64,2048]{3,2,1,0:T(8,128)(2,1)S(1)} %bitcast.161, f32[64,2048]{1,0:T(8,128)S(1)} %copy-done.48, ...), custom_call_target="tpu_custom_call" | custom-call | flops 20000000000 | bytes 1048576 | tf_op jit(solution)/shard_map/backward_kernel/pallas_call | solution.py:620
  392.7 3.6 fusion.34
  396.4 2.4 convolution_convert_fusion.2
  399.3 4.0 collective-permute-start.5
  403.4 49.7 %backward_kernel.6 = (bf16[256,2048]{1,0:T(8,128)(2,1)S(1)}, bf16[2048,256]{1,0:T(8,128)(2,1)S(1)}, f32[64,2048]{1,0:T(8,128)S(1)}, f32[3,2048]{1,0:T(4,128)S(1)}, bf16[4,4,64,2048]{3,2,1,0:T(8,128)(2,1)S(1)}) custom-call(bf16[4,4,64,2048]{3,2,1,0:T(8,128)(2,1)S(1)} %bitcast.158, f32[64,2048]{1,0:T(8,128)S(1)} %copy-done.44, ...), custom_call_target="tpu_custom_call" | custom-call | flops 20000000000 | bytes 1048576 | tf_op jit(solution)/shard_map/backward_kernel/pallas_call | solution.py:620
  453.2 1.3 convolution_convert_fusion.10.d_ref
  454.5 1.8 copy-done.27
  456.5 1.2 copy-done.24
  458.4 25.1 %attention_back_kernel.3 = (bf16[1024,384]{1,0:T(8,128)(2,1)S(1)}, bf16[32,2048]{1,0:T(8,128)(2,1)S(1)}) custom-call(bf16[1024,128]{1,0:T(8,128)(2,1)S(1)} %convolution_convert_fusion.10.d_ref, bf16[3,16,2,64,64]{4,3,2,1,0:T(8,128)(2,1)S(1)} %copy-done.40, f32[2,2048,1]{2,1,0:T(8,128)S(1)} %copy-done.36, bf16[4,4,64,2048]{3,2,1,0:T(8,128)(2,1)S(1)} %bitcast.147, ...), custom_call_target="tpu_custom_call" | custom-call | flops 20000000000 | bytes 1048576 | tf_op jit(solution)/shard_map/attention_back_kernel/pallas_call | solution.py:620
  484.2 1.5 concatenate.43.refs_4_
  485.7 3.9 convolution_convert_fusion
  489.9 1.1 copy-done.32
  491.0 38.1 %backward_kernel.7 = (bf16[64,2048]{1,0:T(8,128)(2,1)S(1)}, bf16[2048,192]{1,0:T(8,128)(2,1)S(1)}, bf16[64,2048]{1,0:T(8,128)(2,1)S(1)}, f32[16,2048]{1,0:T(8,128)S(1)}) custom-call(bf16[4,4,64,2048]{3,2,1,0:T(8,128)(2,1)S(1)} %bitcast.160, f32[64,2048]{1,0:T(8,128)S(1)} %copy-done.8, f32[1,2048]{1,0:T(1,128)S(1)} %get-tuple-element.100.par_ref, ...), custom_call_target="tpu_custom_call" | custom-call | flops 20000000000 | bytes 1048576 | tf_op jit(solution)/shard_map/backward_kernel/pallas_call | solution.py:620
  529.8 1.3 copy.20
  531.1 1.2 copy.21
  532.4 2.8 pad_maximum_fusion.2
  535.2 1.5 pad_maximum_fusion.1
  536.7 0.8 pad_maximum_fusion.5
  537.6 1.3 maximum_bitcast_fusion
  538.9 0.7 maximum_bitcast_fusion.1
  541.1 1.0 collective-permute-done.6
  542.7 0.7 copy.27
  (179 shorter events, 10.3 us)
Async XLA Ops:
  0.6 36.2 %collective-permute-start = (bf16[2,2048,192]{1,2,0:T(8,128)(2,1)}, bf16[2,2048,192]{1,2,0:T(8,128)(2,1)S(1)}, u32[]{:S(2)}, u32[]{:S(2)}) collective-permute-start(bf16[2,2048,192]{1,2,0:T(8,128)(2,1)} %bitcast.177), channel_id=1, source_target_pairs={{0,1},{1,0},{2,3},{3,2},{4,5},{5,4},{6,7},{7,6},{8,9},{9,8},{10,11... | collective-permute-start | bytes 4718600 | tf_op jit(solution)/shard_map/ppermute | solution.py:640
  2.8 2.8 copy-start.58
  2.8 60.2 %collective-permute-start.1 = (bf16[2,64,2048]{2,1,0:T(8,128)(2,1)}, bf16[2,64,2048]{2,1,0:T(8,128)(2,1)S(1)}, u32[]{:S(2)}, u32[]{:S(2)}) collective-permute-start(bf16[2,64,2048]{2,1,0:T(8,128)(2,1)} %bitcast.165), channel_id=1, source_target_pairs={{0,1},{1,0},{2,3},{3,2},{4,5},{5,4},{6,7},{7,6},{8,9},{9,8},{10,11... | collective-permute-start | bytes 1572872 | tf_op jit(solution)/shard_map/ppermute | solution.py:640
  2.9 108.8 %collective-permute-start.2 = (bf16[2,2048,256]{2,1,0:T(8,128)(2,1)}, bf16[2,2048,256]{2,1,0:T(8,128)(2,1)S(1)}, u32[]{:S(2)}, u32[]{:S(2)}) collective-permute-start(bf16[2,2048,256]{2,1,0:T(8,128)(2,1)} %param.15), channel_id=1, source_target_pairs={{0,1},{1,0},{2,3},{3,2},{4,5},{5,4},{6,7},{7,6},{8,9},{9,8},{10,11... | collective-permute-start | bytes 6291464 | tf_op jit(solution)/shard_map/ppermute | solution.py:640
  3.3 33.6 %collective-permute-start.3 = (f32[2,256]{1,0:T(2,128)}, f32[2,256]{1,0:T(2,128)S(1)}, u32[]{:S(2)}, u32[]{:S(2)}) collective-permute-start(f32[2,256]{1,0:T(2,128)} %param.16), channel_id=1, source_target_pairs={{0,1},{1,0},{2,3},{3,2},{4,5},{5,4},{6,7},{7,6},{8,9},{9,8},{10,11... | collective-permute-start | bytes 6152 | tf_op jit(solution)/shard_map/ppermute | solution.py:640
  3.4 114.3 %collective-permute-start.4 = (bf16[2,256,2048]{2,1,0:T(8,128)(2,1)}, bf16[2,256,2048]{2,1,0:T(8,128)(2,1)S(1)}, u32[]{:S(2)}, u32[]{:S(2)}) collective-permute-start(bf16[2,256,2048]{2,1,0:T(8,128)(2,1)} %param.17), channel_id=1, source_target_pairs={{0,1},{1,0},{2,3},{3,2},{4,5},{5,4},{6,7},{7,6},{8,9},{9,8},{10,11... | collective-permute-start | bytes 6291464 | tf_op jit(solution)/shard_map/ppermute | solution.py:640
  7.3 29.6 %copy-start.67 = (f32[2,256]{1,0:T(2,128)S(1)}, f32[2,256]{1,0:T(2,128)}, u32[]{:S(2)}) copy-start(f32[2,256]{1,0:T(2,128)} %param.16) | copy-start | bytes 6148
  7.3 29.6 %copy-start.70 = (bf16[2,2048,3,1,64]{1,4,3,2,0:T(8,128)(2,1)S(1)}, bf16[2,2048,3,1,64]{1,4,3,2,0:T(8,128)(2,1)}, u32[]{:S(2)}) copy-start(bf16[2,2048,3,1,64]{1,4,3,2,0:T(8,128)(2,1)} %param.13) | copy-start | bytes 4718596
  36.8 27.7 %copy-start.7 = (f32[64,2048]{1,0:T(8,128)}, f32[64,2048]{1,0:T(8,128)S(1)}, u32[]{:S(2)}) copy-start(f32[64,2048]{1,0:T(8,128)S(1)} %bitcast_convert_fusion.res_ref) | copy-start | bytes 1572868
  36.9 75.0 %copy-start.68 = (f32[1,512]{1,0:T(1,128)}, f32[1,512]{1,0:T(1,128)S(1)}, u32[]{:S(2)}) copy-start(f32[1,512]{1,0:T(1,128)S(1)} %get-tuple-element.113) | copy-start | bytes 6148
  36.9 303.1 %copy-start.71 = (bf16[2,2048,192]{1,2,0:T(8,128)(2,1)}, bf16[2,2048,192]{1,2,0:T(8,128)(2,1)S(1)}, u32[]{:S(2)}) copy-start(bf16[2,2048,192]{1,2,0:T(8,128)(2,1)S(1)} %collective-permute-done) | copy-start | bytes 4718596
  39.3 23.7 %copy-start.52 = (bf16[2,1,64,2048]{3,2,1,0:T(8,128)(2,1)S(1)}, bf16[2,1,64,2048]{3,2,1,0:T(8,128)(2,1)}, u32[]{:S(2)}) copy-start(bf16[2,1,64,2048]{3,2,1,0:T(8,128)(2,1)} %param.14) | copy-start | bytes 1572868
  63.0 134.6 %copy-start.55 = (bf16[2,64,2048]{2,1,0:T(8,128)(2,1)}, bf16[2,64,2048]{2,1,0:T(8,128)(2,1)S(1)}, u32[]{:S(2)}) copy-start(bf16[2,64,2048]{2,1,0:T(8,128)(2,1)S(1)} %collective-permute-done.1) | copy-start | bytes 1572868
  111.7 9.4 %copy-start.43 = (f32[64,2048]{1,0:T(8,128)}, f32[64,2048]{1,0:T(8,128)S(1)}, u32[]{:S(2)}) copy-start(f32[64,2048]{1,0:T(8,128)S(1)} %get-tuple-element.49.res_ref) | copy-start | bytes 1572868
  111.9 142.5 %copy-start.61 = (bf16[2,2048,512]{2,1,0:T(8,128)(2,1)}, bf16[2,2048,512]{2,1,0:T(8,128)(2,1)S(1)}, u32[]{:S(2)}) copy-start(bf16[2,2048,512]{2,1,0:T(8,128)(2,1)S(1)} %constant_dynamic-update-slice_fusion) | copy-start | bytes 12582916
  117.9 138.9 %copy-start.59 = (bf16[2,512,2048]{2,1,0:T(8,128)(2,1)}, bf16[2,512,2048]{2,1,0:T(8,128)(2,1)S(1)}, u32[]{:S(2)}) copy-start(bf16[2,512,2048]{2,1,0:T(8,128)(2,1)S(1)} %constant_dynamic-update-slice_fusion.4) | copy-start | bytes 12582916
  164.2 34.6 %copy-start.47 = (f32[64,2048]{1,0:T(8,128)}, f32[64,2048]{1,0:T(8,128)S(1)}, u32[]{:S(2)}) copy-start(f32[64,2048]{1,0:T(8,128)S(1)} %get-tuple-element.53.res_ref) | copy-start | bytes 1572868
  246.7 2.8 copy-start.29
  259.2 54.4 %copy-start.23 = (bf16[1024,2048]{1,0:T(8,128)(2,1)}, bf16[1024,2048]{1,0:T(8,128)(2,1)S(1)}, u32[]{:S(2)}) copy-start(bf16[1024,2048]{1,0:T(8,128)(2,1)S(1)} %convolution_convert_fusion.3) | copy-start | bytes 12582916
  259.3 53.0 %copy-start.53 = (bf16[2,1,64,2048]{3,2,1,0:T(8,128)(2,1)S(1)}, bf16[2,1,64,2048]{3,2,1,0:T(8,128)(2,1)}, u32[]{:S(2)}) copy-start(bf16[2,1,64,2048]{3,2,1,0:T(8,128)(2,1)} %param.14) | copy-start | bytes 1572868
  259.3 53.0 %copy-start.56 = (bf16[2,64,2048]{2,1,0:T(8,128)(2,1)S(1)}, bf16[2,64,2048]{2,1,0:T(8,128)(2,1)}, u32[]{:S(2)}) copy-start(bf16[2,64,2048]{2,1,0:T(8,128)(2,1)} %copy-done.55) | copy-start | bytes 1572868
  342.4 50.3 %copy-start.60 = (bf16[2,512,2048]{2,1,0:T(8,128)(2,1)S(1)}, bf16[2,512,2048]{2,1,0:T(8,128)(2,1)}, u32[]{:S(2)}) copy-start(bf16[2,512,2048]{2,1,0:T(8,128)(2,1)} %copy-done.59) | copy-start | bytes 12582916
  342.4 50.3 %copy-start.69 = (f32[1,512]{1,0:T(1,128)S(1)}, f32[1,512]{1,0:T(1,128)}, u32[]{:S(2)}) copy-start(f32[1,512]{1,0:T(1,128)} %copy-done.68) | copy-start | bytes 6148
  342.4 50.3 %copy-start.72 = (f32[1024,512]{1,0:T(8,128)S(1)}, f32[1024,512]{1,0:T(8,128)}, u32[]{:S(2)}) copy-start(f32[1024,512]{1,0:T(8,128)} %get-tuple-element.115) | copy-start | bytes 6291460
  392.6 3.7 copy-start.10
  392.7 3.6 copy-start.62
  396.3 7.0 %copy-start.22 = (bf16[4,4,64,2048]{3,2,1,0:T(8,128)(2,1)S(1)}, bf16[4,4,64,2048]{3,2,1,0:T(8,128)(2,1)}, u32[]{:S(2)}) copy-start(bf16[4,4,64,2048]{3,2,1,0:T(8,128)(2,1)} %copy-done.21) | copy-start | bytes 12582916
  396.4 7.0 %copy-start.34 = (bf16[1024,512]{1,0:T(8,128)(2,1)S(1)}, bf16[1024,512]{1,0:T(8,128)(2,1)}, u32[]{:S(2)}) copy-start(bf16[1024,512]{1,0:T(8,128)(2,1)} %copy-done.33) | copy-start | bytes 3145732
  396.4 7.0 %copy-start.44 = (f32[64,2048]{1,0:T(8,128)S(1)}, f32[64,2048]{1,0:T(8,128)}, u32[]{:S(2)}) copy-start(f32[64,2048]{1,0:T(8,128)} %copy-done.43) | copy-start | bytes 1572868
  399.3 141.7 %collective-permute-start.5 = (f32[256]{0:T(256)}, f32[256]{0:T(256)S(1)}, u32[]{:S(2)}, u32[]{:S(2)}) collective-permute-start(f32[256]{0:T(256)} %slice.160), channel_id=1, source_target_pairs={{0,1},{1,0},{2,3},{3,2},{4,5},{5,4},{6,7},{7,6},{8,9},{9,8},{10,11... | collective-permute-start | bytes 3080 | tf_op jit(solution)/shard_map/ppermute | solution.py:640
  403.4 49.8 %copy-start.54 = (bf16[2,1,64,2048]{3,2,1,0:T(8,128)(2,1)S(1)}, bf16[2,1,64,2048]{3,2,1,0:T(8,128)(2,1)}, u32[]{:S(2)}) copy-start(bf16[2,1,64,2048]{3,2,1,0:T(8,128)(2,1)} %param.14) | copy-start | bytes 1572868
  403.4 49.8 %copy-start.57 = (bf16[2,64,2048]{2,1,0:T(8,128)(2,1)S(1)}, bf16[2,64,2048]{2,1,0:T(8,128)(2,1)}, u32[]{:S(2)}) copy-start(bf16[2,64,2048]{2,1,0:T(8,128)(2,1)} %copy-done.55) | copy-start | bytes 1572868
  403.4 53.1 %copy-start.40 = (bf16[3,16,2,64,64]{4,3,2,1,0:T(8,128)(2,1)S(1)}, bf16[3,16,2,64,64]{4,3,2,1,0:T(8,128)(2,1)}, u32[]{:S(2)}) copy-start(bf16[3,16,2,64,64]{4,3,2,1,0:T(8,128)(2,1)} %copy-done.39) | copy-start | bytes 2359300
  453.1 3.2 copy-start.27
  453.1 3.4 copy-start.45
  453.1 4.6 copy-start.24
  453.1 5.2 copy-start.36
  458.4 25.8 %copy-start.64 = (f32[2048]{0:T(1024)S(1)}, f32[2048]{0:T(1024)}, u32[]{:S(2)}) copy-start(f32[2048]{0:T(1024)} %convert_reduce_fusion) | copy-start | bytes 24580
  484.1 5.4 copy-start.31
  485.6 3.9 copy-start.6
  485.6 3.9 copy-start.8
  485.6 3.9 copy-start.14
  485.6 3.9 copy-start.20
  485.7 4.2 copy-start.28
  485.7 4.2 copy-start.46
  532.4 2.8 copy-start.3
  537.6 3.3 copy-start.66
  540.9 1.2 collective-permute-start.6
  (32 other events, 54.2 us)
